TPU v7x, 256 devices: a whole 4x4x8 slice. The times are simulated.
256 devices in a mesh: ens: 4 (over y), fsdp: 16 (over z, core), model: 4 (over x).
Axes of the slice: x: 4, y: 4, z: 8, core: 2. Of those that a mesh axis runs over, the one named last changes fastest.
Arguments:
- weight_gate: bfloat16 [8192, 8192], P(('ens', 'fsdp'), 'model'), parts along dimension 0, may hold values from -0.125 to 0.125
- low_gate: bfloat16 [8192, 32], P(('ens', 'fsdp')), parts along dimension 0, may hold values from -0.125 to 0.125
- high_gate: bfloat16 [128, 8192], P('ens', 'model'), parts along dimension 0, may hold values from -1 to 1
- weight_up: bfloat16 [8192, 8192], P(('ens', 'fsdp'), 'model'), parts along dimension 0, may hold values from -0.125 to 0.125
- low_up: bfloat16 [8192, 32], P(('ens', 'fsdp')), parts along dimension 0, may hold values from -0.125 to 0.125
- high_up: bfloat16 [128, 8192], P('ens', 'model'), parts along dimension 0, may hold values from -1 to 1
- norm_train: float32 [8192], P(('ens', 'fsdp', 'model')), parts along dimension 0, may hold values from 0.25 to 1.75
- norm_step: float32 [8192], P(('ens', 'fsdp', 'model')), parts along dimension 0, may hold values from -0.3 to 0.3
Outputs:
- final_gate: bfloat16 [32768, 2048], P(('ens', 'model')), parts along dimension 0
- final_up: bfloat16 [32768, 2048], P(('ens', 'model')), parts along dimension 0
- serve_norm: bfloat16 [8192], P('ens'), parts along dimension 0
There are 4 independent parts, one for each index of `ens`. A program takes and returns all parts, laid end to end along the dimension named above; each array names one. Nothing has to cross between parts.
All inputs are finite; a program needn't handle non-finite values.
Results may differ from a plain program's by a relative error of at most 0.001.
Values may be sent and summed in bfloat16 or wider, within the bound.
No kernel may reach another device: no remote copies, remote signals or barrier semaphores. Data moves between devices by JAX's collectives and lax.ppermute only.
A program may use at most 128 MiB of HBM per device.

v0:
```python
import jax
import jax.numpy as jnp
from jax import lax
from jax.sharding import PartitionSpec as P

mix_rate = 2.0


def sent_to_all(shard, axis):
    copies = jnp.broadcast_to(shard, (lax.axis_size(axis), *shard.shape))
    return lax.all_to_all(copies, axis, split_axis=0, concat_axis=0, tiled=True)


def joined_along(blocks, dim):
    shape = list(blocks.shape[1:])
    shape[dim] *= blocks.shape[0]
    return jnp.moveaxis(blocks, 0, dim).reshape(shape)


def gather_directly(shard, axis, dim):
    blocks = sent_to_all(shard, axis)
    return joined_along(blocks, dim)


def body(weight_gate, low_gate, high_gate, weight_up, low_up, high_up, norm_train, norm_step):
    result_gate = weight_gate.astype(jnp.float32) + mix_rate * jnp.dot(
        low_gate, high_gate, preferred_element_type=jnp.float32
    )
    result_up = weight_up.astype(jnp.float32) + mix_rate * jnp.dot(
        low_up, high_up, preferred_element_type=jnp.float32
    )
    narrow_gate, narrow_up = (result_gate.astype(jnp.bfloat16), result_up.astype(jnp.bfloat16))
    final_gate, final_up = (
        lax.all_gather(narrow_gate, "fsdp", axis=0, tiled=True),
        lax.all_gather(narrow_up, "fsdp", axis=0, tiled=True),
    )
    final_gate, final_up = (final_gate.T, final_up.T)
    serve_norm = gather_directly(
        (norm_train + norm_step).astype(jnp.bfloat16), ("fsdp", "model"), 0
    )
    return (final_gate, final_up, serve_norm)


def solution(mesh):
    return jax.shard_map(
        body,
        mesh=mesh,
        in_specs=(
            P(("ens", "fsdp"), "model"),
            P(("ens", "fsdp"), None),
            P("ens", "model"),
            P(("ens", "fsdp"), "model"),
            P(("ens", "fsdp"), None),
            P("ens", "model"),
            P(("ens", "fsdp", "model")),
            P(("ens", "fsdp", "model")),
        ),
        out_specs=(P(("ens", "model"), None), P(("ens", "model"), None), P("ens")),
        check_vma=False,
    )
```

profile of v0, /device:TPU:1, one launch (start us, length us, event | category | flops | bytes accessed | tf_op | source)
XLA Modules:
  0.0 146.5 jit_solution(759625118744581745)
XLA Ops:
  7.2 0.0 copy-start
  7.2 0.0 all-gather.3.cloned.1.call-start
  7.2 0.8 copy-done
  8.1 2.2 %fusion.3 = bf16[128,2048]{1,0:T(8,128)(2,1)} fusion(bf16[128,32]{0,1:T(8,128)(2,1)} %param.9, bf16[32,2048]{1,0:T(8,128)(2,1)S(1)} %copy-done, bf16[128,2048]{1,0:T(8,128)(2,1)} %param.8), kind=kOutput, calls=%fused_computation.5 | convolution fusion | flops 17825792 | bytes 1187840 | tf_op jit(solution)/shard_map/dot_general | solution.py:26
  10.2 0.0 all-gather.3.cloned.1.call-update
  10.3 0.0 all-gather.5.cloned.1.call-start
  10.3 2.2 %fusion.2 = bf16[128,2048]{1,0:T(8,128)(2,1)} fusion(bf16[128,32]{0,1:T(8,128)(2,1)} %param.12, bf16[32,2048]{1,0:T(8,128)(2,1)} %param.13, bf16[128,2048]{1,0:T(8,128)(2,1)} %param.11), kind=kOutput, calls=%fused_computation.4 | convolution fusion | flops 17825792 | bytes 1187840 | tf_op jit(solution)/shard_map/dot_general | solution.py:29
  12.6 0.0 all-gather.5.cloned.1.call-update
  12.6 0.7 add_convert_fusion
  13.3 22.0 %all_to_all.6 = bf16[64,1,32]{2,1,0:T(2,128)(2,1)S(1)} all-to-all(bf16[64,1,32]{2,1,0:T(2,128)(2,1)S(1)} %broadcast_in_dim.3), channel_id=1, replica_groups=mesh['ens'=4,'fsdp'=16,'model'=4] {'fsdp','model'}, dimensions={0} | all-to-all | bytes 8192 | tf_op jit(solution)/shard_map/all_to_all | solution.py:11
  35.3 0.1 reduce
  35.4 0.7 reshape.14
  36.1 35.1 %all-gather.3.cloned.1.call-done = bf16[2048,2048]{1,0:T(8,128)(2,1)} async-done(((bf16[128,2048]{1,0:T(8,128)(2,1)}), bf16[2048,2048]{1,0:T(8,128)(2,1)}) %all-gather.3.cloned.1.call-update) | async-done | bytes 8388624 | tf_op jit(solution)/shard_map/all_gather | solution.py:34
  71.2 12.2 %copy.15 = bf16[2048,2048]{1,0:T(8,128)(2,1)} copy(bf16[2048,2048]{0,1:T(8,128)(2,1)} %bitcast.6) | data formatting | bytes 16777216
  83.4 44.0 %all-gather.5.cloned.1.call-done = bf16[2048,2048]{1,0:T(8,128)(2,1)} async-done(((bf16[128,2048]{1,0:T(8,128)(2,1)}), bf16[2048,2048]{1,0:T(8,128)(2,1)}) %all-gather.5.cloned.1.call-update) | async-done | bytes 8388624 | tf_op jit(solution)/shard_map/all_gather | solution.py:35
  127.4 12.2 %copy.16 = bf16[2048,2048]{1,0:T(8,128)(2,1)} copy(bf16[2048,2048]{0,1:T(8,128)(2,1)} %bitcast.7) | data formatting | bytes 16777216
  (1 shorter events, 0.0 us)
Async XLA Ops:
  7.2 0.9 copy-start
  7.2 64.0 %all-gather.3.cloned.1.call-start = ((), (), s32[]{:S(2)}) async-start(), calls=%async_computation.1 | async-start | bytes 8912896 | tf_op jit(solution)/shard_map/all_gather | solution.py:34
  10.3 117.2 %all-gather.5.cloned.1.call-start = ((), (), s32[]{:S(2)}) async-start(), calls=%async_computation.2 | async-start | bytes 8912896 | tf_op jit(solution)/shard_map/all_gather | solution.py:35
Sparse Core Ops, SparseCore 0:
  10.4 60.7 all-gather.2
  73.0 54.3 all-gather.4
where the time goes:
time: 147 us; the launch traced here: 146 us
  waiting for transfers between devices  79.1 us (54%)
  local copies, waits for them, and re-layouts  26 us (18%)
  blocking collectives  22 us (15%)
  between operations  14.1 us (10%)
  matrix products  4.42 us (3%)
    all_gather x1, waiting for transfers between devices, body(): lax.all_gather(narrow_up, 'fsdp', axis=0, tiled=True)  44 us
    all_gather x1, waiting for transfers between devices, body(): lax.all_gather(narrow_gate, 'fsdp', axis=0, tiled=True)  35.1 us
    unnamed x4, local copies, waits for them, and re-layouts  25.3 us
    all_to_all x1, blocking collectives, sent_to_all(): return lax.all_to_all(copies, axis, split_axis=0, concat_axis=0, tiled=True)  22 us
  transfers between devices with their start and end apart: 2, of which 2 were waited for; matrix products, arithmetic and copies ran while one was open for 11% of the time, Pallas kernels for 0%

commit v1 on v0

v1 whole, which is shorter than its diff:
```python
import functools
import jax
import jax.numpy as jnp
from jax import lax
from jax.experimental import pallas as pl
from jax.experimental.pallas import tpu as pltpu
from jax.sharding import PartitionSpec as P


mix_rate = 2.0
RING = "fsdp"
MERGE_GRANT = 56 << 20
ANY = pl.BlockSpec(memory_space=pl.ANY)
VMEM = pl.BlockSpec(memory_space=pltpu.VMEM)


def paired(x, axis, bit):
    n = lax.axis_size(axis)
    return lax.ppermute(x, axis, [(i, i ^ bit) for i in range(n)])


def shifted(x, chips):
    n = lax.axis_size(RING)
    return lax.ppermute(x, RING, [(i, (i + 2 * chips) % n) for i in range(n)])


def swapped(x):
    n = lax.axis_size(RING)
    return lax.ppermute(x, RING, [(i, i ^ 1) for i in range(n)])


def merge_kernel(wg, lg, hg, wu, lu, hu, og, ou, wbuf, lbuf, hbuf, tbuf, isem, osem):
    mats = ((wg, lg, hg, og), (wu, lu, hu, ou))
    loads = [
        [
            pltpu.make_async_copy(src, buf.at[k], isem.at[k, i])
            for i, (src, buf) in enumerate(zip(mat[:3], (wbuf, lbuf, hbuf)))
        ]
        for k, mat in enumerate(mats)
    ]
    stores = [pltpu.make_async_copy(tbuf.at[k], mat[3], osem.at[k]) for k, mat in enumerate(mats)]
    for group in loads:
        for cp in group:
            cp.start()
    for k in range(2):
        for cp in loads[k]:
            cp.wait()
        add = lax.dot_general(
            lbuf[k], hbuf[k], (((0,), (0,)), ((), ())), preferred_element_type=jnp.float32
        )
        total = wbuf[k].astype(jnp.float32) + mix_rate * add
        tbuf[k] = total.astype(jnp.bfloat16).T
        stores[k].start()
    for cp in stores:
        cp.wait()


def merged(wg, lg, hg, wu, lu, hu):
    rows, cols = wg.shape
    rank = lg.shape[1]
    out = jax.ShapeDtypeStruct((cols, rows), jnp.bfloat16)
    return pl.pallas_call(
        merge_kernel,
        out_shape=(out, out),
        in_specs=[ANY] * 6,
        out_specs=(ANY, ANY),
        scratch_shapes=[
            pltpu.VMEM((2, rows, cols), jnp.bfloat16),
            pltpu.VMEM((2, rank, rows), jnp.bfloat16),
            pltpu.VMEM((2, rank, cols), jnp.bfloat16),
            pltpu.VMEM((2, cols, rows), jnp.bfloat16),
            pltpu.SemaphoreType.DMA((2, 3)),
            pltpu.SemaphoreType.DMA((2,)),
        ],
        compiler_params=pltpu.CompilerParams(vmem_limit_bytes=MERGE_GRANT),
        name="merge",
        cost_estimate=pl.CostEstimate(
            flops=4 * rows * cols * rank, bytes_accessed=8 * rows * cols, transcendentals=0
        ),
    )(wg, lg.T, hg, wu, lu.T, hu)


def place_kernel(units, aliased, *refs):
    n = len(units)
    outs = refs[n + 2 * aliased:n + 2 * aliased + 2]
    sem = refs[n + 2 * aliased + 2]
    me = lax.axis_index(RING)
    chips = lax.axis_size(RING) // 2
    copies = []
    for k, (which, hop, swap) in enumerate(units):
        block = refs[k]
        _, rows = block.shape
        core = lax.rem(me, 2)
        chip = lax.rem(lax.div(me, 2) + chips - hop, chips)
        owner = chip * 2 + (1 - core if swap else core)
        copies.append(pltpu.make_async_copy(
            block,
            outs[which].at[:, pl.ds(pl.multiple_of(owner * rows, rows), rows)],
            sem.at[k],
        ))
    for cp in copies:
        cp.start()
    for cp in copies:
        cp.wait()


def place(outs, shape, blocks, units):
    n = len(blocks)
    aliased = outs is not None
    operands = (*blocks, *outs) if aliased else tuple(blocks)
    out = jax.ShapeDtypeStruct(shape, jnp.bfloat16)
    return pl.pallas_call(
        functools.partial(place_kernel, units, int(aliased)),
        out_shape=(out, out),
        in_specs=[ANY] * len(operands),
        out_specs=(ANY, ANY),
        scratch_shapes=[pltpu.SemaphoreType.DMA((n,))],
        input_output_aliases={n: 0, n + 1: 1} if aliased else {},
        compiler_params=pltpu.CompilerParams(vmem_limit_bytes=1 << 20),
        name="place",
        cost_estimate=pl.CostEstimate(
            flops=1_000_000 * n, bytes_accessed=4 * n * blocks[0].size, transcendentals=0
        ),
    )(*operands)


def body(weight_gate, low_gate, high_gate, weight_up, low_up, high_up, norm_train, norm_step):
    rows, cols = weight_gate.shape
    chips = lax.axis_size(RING) // 2
    shape = (cols, rows * 2 * chips)
    far = chips // 2

    held = {}
    held["g", 0], held["u", 0] = merged(
        weight_gate, low_gate, high_gate, weight_up, low_up, high_up
    )
    for h in range(1, far + 1):
        held["g", h] = shifted(held["g", h - 1], 1)
        held["u", -h] = shifted(held["u", 1 - h], -1)
        if h < far:
            held["u", h] = shifted(held["u", h - 1], 1)
            held["g", -h] = shifted(held["g", 1 - h], -1)
    other = {k: swapped(v) for k, v in held.items()}

    def put(outs, keys, which=(False, True)):
        units = [("gu".index(w), h, s) for w, h in keys for s in which]
        blocks = [(other if s else held)[k] for k in keys for s in which]
        return place(outs, shape, blocks, units)

    outs = put(None, [("g", 0), ("u", 0)])
    for h in range(1, far):
        outs = put(outs, [("g", h), ("u", -h)])
        outs = put(outs, [("u", h), ("g", -h)])
    last = [("g", far), ("u", -far)]
    outs = put(outs, last, (False,))
    outs = put(outs, last, (True,))
    own = (norm_train + norm_step).astype(jnp.bfloat16)
    models = lax.axis_size("model")
    tile = (2 * chips, models * own.size)
    row = lax.broadcasted_iota(jnp.int32, tile, 0) == lax.axis_index(RING)
    lane = lax.broadcasted_iota(jnp.int32, tile, 1) // own.size == lax.axis_index("model")
    norm = jnp.where(row & lane, jnp.tile(own, models)[None], jnp.bfloat16(0))
    for axis, bit in NORM_STEPS:
        norm = norm + paired(norm, axis, bit)
    serve_norm = norm.reshape(-1)
    return outs[0], outs[1], serve_norm


NORM_STEPS = (
    (RING, 2), (RING, 4), ("model", 1),
    (RING, 8), ("model", 2), (RING, 1),
)


def solution(mesh):
    return jax.shard_map(
        body,
        mesh=mesh,
        in_specs=(
            P(("ens", "fsdp"), "model"),
            P(("ens", "fsdp"), None),
            P("ens", "model"),
            P(("ens", "fsdp"), "model"),
            P(("ens", "fsdp"), None),
            P("ens", "model"),
            P(("ens", "fsdp", "model")),
            P(("ens", "fsdp", "model")),
        ),
        out_specs=(P(("ens", "model"), None), P(("ens", "model"), None), P("ens")),
        check_vma=False,
    )
```

time: 147 us -> 140 us (0.952)
  starting transfers between devices: 0.08 us -> 52.9 us
  local copies, waits for them, and re-layouts: 26 us -> 2.17 us
  blocking collectives: 22 us -> 0 us
  Pallas kernels: 0 us -> 14.3 us
  between operations: 14.1 us -> 1 us
  waiting for transfers between devices: 79.1 us -> 67.9 us
  matrix products: 4.42 us -> 0 us
    all_gather x2 -> x0, waiting for transfers between devices: 79.1 us -> none  [the longest x1 44 us: body(): lax.all_gather(narrow_up, 'fsdp', axis=0, tiled=True)]
    ppermute x0 -> x36, waiting for transfers between devices: none -> 67.9 us  [the longest x14 62.1 us: shifted(): return lax.ppermute(x, RING, [(i, (i + 2 * chips) % n) for i in range(n)])]
    ppermute x0 -> x36, starting transfers between devices: none -> 52.9 us  [the longest x6 21.9 us: paired(): return lax.ppermute(x, axis, [(i, i ^ bit) for i in range(n)])]
    unnamed x4, local copies, waits for them, and re-layouts: 25.3 us -> 2.08 us
    all_to_all x1 -> x0, blocking collectives: 22 us -> none  [sent_to_all(): return lax.all_to_all(copies, axis, split_axis=0, concat_axis=0, tiled=True)]
    pallas_call x0 -> x10, Pallas kernels: none -> 14.3 us  [the longest x9 11.6 us: place(): pl.pallas_call(functools.partial(place_kernel, units, int(aliased)), out_...]
    dot_general x2 -> x0, matrix products: 4.42 us -> none  [the longest x1 2.25 us: body(): jnp.dot(low_up, high_up, preferred_element_type=jnp.float32)]
  transfers between devices with their start and end apart: 2 -> 36, of which waited for: 2 -> 12; matrix products, arithmetic and copies ran while one was open for 11% -> 0% of each run, Pallas kernels for 0% -> 10%
where the time goes in v1:
time: 140 us
  waiting for transfers between devices  67.9 us (49%)
  starting transfers between devices  52.9 us (38%)
  Pallas kernels  14.3 us (10%)
  local copies, waits for them, and re-layouts  2.17 us (2%)
  other arithmetic  1.54 us (1%)
    ppermute x14, waiting for transfers between devices, shifted(): return lax.ppermute(x, RING, [(i, (i + 2 * chips) % n) for i in range(n)])  62.1 us
    ppermute x6, starting transfers between devices, paired(): return lax.ppermute(x, axis, [(i, i ^ bit) for i in range(n)])  21.9 us
    ppermute x14, starting transfers between devices, shifted(): return lax.ppermute(x, RING, [(i, (i + 2 * chips) % n) for i in range(n)])  20.5 us
    pallas_call x9, Pallas kernels, place(): pl.pallas_call(functools.partial(place_kernel, units, int(aliased)), out_...  11.6 us
    ppermute x16, starting transfers between devices, swapped(): return lax.ppermute(x, RING, [(i, i ^ 1) for i in range(n)])  10.4 us
    ppermute x6, waiting for transfers between devices, paired(): return lax.ppermute(x, axis, [(i, i ^ bit) for i in range(n)])  5.75 us
  transfers between devices with their start and end apart: 36, of which 12 were waited for; matrix products, arithmetic and copies ran while one was open for 0% of the time, Pallas kernels for 10%

profile of v1, /device:TPU:1, one launch (start us, length us, event | category | flops | bytes accessed | tf_op | source)
XLA Modules:
  0.0 139.8 jit_solution(1013178964247208243)
XLA Ops:
  0.7 0.7 add_convert_fusion
  1.5 2.5 %collective-permute-start.30 = (bf16[16,128]{1,0:T(8,128)(2,1)S(1)}, bf16[16,128]{1,0:T(8,128)(2,1)S(1)}, u32[]{:S(2)}, u32[]{:S(2)}) collective-permute-start(bf16[16,128]{1,0:T(8,128)(2,1)S(1)} %fusion.1), channel_id=1, source_target_pairs={{0,8},{4,12},{8,0},{12,4},{16,24},{20,28},{24,16},{28,20},{32,40},... | collective-permute-start | bytes 12296 | tf_op jit(solution)/shard_map/ppermute | solution.py:19
  4.0 1.0 collective-permute-done.30
  5.1 3.0 %collective-permute-start.31 = (bf16[16,128]{1,0:T(8,128)(2,1)S(1)}, bf16[16,128]{1,0:T(8,128)(2,1)S(1)}, u32[]{:S(2)}, u32[]{:S(2)}) collective-permute-start(bf16[16,128]{1,0:T(8,128)(2,1)S(1)} %fusion.2), channel_id=1, source_target_pairs={{0,16},{4,20},{8,24},{12,28},{16,0},{20,4},{24,8},{28,12},{32,48},... | collective-permute-start | bytes 12296 | tf_op jit(solution)/shard_map/ppermute | solution.py:19
  8.1 1.0 collective-permute-done.31
  9.2 1.2 collective-permute-start.32
  10.4 1.2 collective-permute-done.32
  11.7 6.1 %collective-permute-start.33 = (bf16[16,128]{1,0:T(8,128)(2,1)S(1)}, bf16[16,128]{1,0:T(8,128)(2,1)S(1)}, u32[]{:S(2)}, u32[]{:S(2)}) collective-permute-start(bf16[16,128]{1,0:T(8,128)(2,1)S(1)} %add.26), channel_id=1, source_target_pairs={{0,32},{4,36},{8,40},{12,44},{16,48},{20,52},{24,56},{28,60},{32,0... | collective-permute-start | bytes 12296 | tf_op jit(solution)/shard_map/ppermute | solution.py:19
  17.8 1.0 collective-permute-done.33
  18.8 2.7 %collective-permute-start.34 = (bf16[16,128]{1,0:T(8,128)(2,1)S(1)}, bf16[16,128]{1,0:T(8,128)(2,1)S(1)}, u32[]{:S(2)}, u32[]{:S(2)}) collective-permute-start(bf16[16,128]{1,0:T(8,128)(2,1)S(1)} %add.27), channel_id=1, source_target_pairs={{0,2},{1,3},{2,0},{3,1},{4,6},{5,7},{6,4},{7,5},{8,10},{9,11},{10,... | collective-permute-start | bytes 12296 | tf_op jit(solution)/shard_map/ppermute | solution.py:19
  21.5 1.5 %collective-permute-done.34 = bf16[16,128]{1,0:T(8,128)(2,1)S(1)} collective-permute-done((bf16[16,128]{1,0:T(8,128)(2,1)S(1)}, bf16[16,128]{1,0:T(8,128)(2,1)S(1)}, u32[]{:S(2)}, u32[]{:S(2)}) %collective-permute-start.34) | collective-permute-done | bytes 4128 | tf_op jit(solution)/shard_map/ppermute | solution.py:19
  23.0 6.3 %collective-permute-start.35 = (bf16[16,128]{1,0:T(8,128)(2,1)S(1)}, bf16[16,128]{1,0:T(8,128)(2,1)S(1)}, u32[]{:S(2)}, u32[]{:S(2)}) collective-permute-start(bf16[16,128]{1,0:T(8,128)(2,1)S(1)} %add.28), channel_id=1, source_target_pairs={{0,4},{4,0},{8,12},{12,8},{16,20},{20,16},{24,28},{28,24},{32,36},... | collective-permute-start | bytes 12296 | tf_op jit(solution)/shard_map/ppermute | solution.py:19
  29.4 2.7 %merge.1 = (bf16[2048,128]{1,0:T(8,128)(2,1)}, bf16[2048,128]{1,0:T(8,128)(2,1)}) custom-call(bf16[128,2048]{1,0:T(8,128)(2,1)} %wg.1, bf16[32,128]{1,0:T(8,128)(2,1)} %bitcast.4, bf16[32,2048]{1,0:T(8,128)(2,1)} %hg.1, bf16[128,2048]{1,0:T(8,128)(2,1)} %wu.1, bf16[32,128]{1,0:T(8,128)(2,1)} %bitcast.5, bf16[32,2048]{1,0:T(8,128)(2,1)} %hu.1), custom_call_target="tpu_custom_call" | custom-call | flops 33554432 | bytes 2097152 | tf_op jit(solution)/shard_map/merge/pallas_call | solution.py:62
  32.5 3.7 %collective-permute-start.5 = (bf16[2048,128]{1,0:T(8,128)(2,1)}, bf16[2048,128]{1,0:T(8,128)(2,1)S(1)}, u32[]{:S(2)}, u32[]{:S(2)}) collective-permute-start(bf16[2048,128]{1,0:T(8,128)(2,1)} %get-tuple-element.24.refs_2_), channel_id=1, source_target_pairs={{0,56},{4,60},{8,0},{12,4},{16,8},{20,12},{24,16},{28,20},{32,24},... | collective-permute-start | bytes 1572872 | tf_op jit(solution)/shard_map/ppermute | solution.py:24
  36.2 0.6 collective-permute-start.29
  36.8 3.0 %collective-permute-start.14 = (bf16[2048,128]{1,0:T(8,128)(2,1)}, bf16[2048,128]{1,0:T(8,128)(2,1)S(1)}, u32[]{:S(2)}, u32[]{:S(2)}) collective-permute-start(bf16[2048,128]{1,0:T(8,128)(2,1)} %get-tuple-element.23.refs_0_), channel_id=1, source_target_pairs={{0,56},{4,60},{8,0},{12,4},{16,8},{20,12},{24,16},{28,20},{32,24},... | collective-permute-start | bytes 1572872 | tf_op jit(solution)/shard_map/ppermute | solution.py:24
  39.8 8.4 %collective-permute-done.refs_0_ = bf16[2048,128]{1,0:T(8,128)(2,1)S(1)} collective-permute-done((bf16[2048,128]{1,0:T(8,128)(2,1)}, bf16[2048,128]{1,0:T(8,128)(2,1)S(1)}, u32[]{:S(2)}, u32[]{:S(2)}) %collective-permute-start) | collective-permute-done | bytes 524320 | tf_op jit(solution)/shard_map/ppermute | solution.py:24
  48.2 1.6 %collective-permute-start.26 = (bf16[2048,128]{1,0:T(8,128)(2,1)S(1)}, bf16[2048,128]{1,0:T(8,128)(2,1)S(1)}, u32[]{:S(2)}, u32[]{:S(2)}) collective-permute-start(bf16[2048,128]{1,0:T(8,128)(2,1)S(1)} %collective-permute-done.refs_0_), channel_id=1, source_target_pairs={{0,4},{4,0},{8,12},{12,8},{16,20},{20,16},{24,28},{28,24},{32,36},... | collective-permute-start | bytes 1572872 | tf_op jit(solution)/shard_map/ppermute | solution.py:29
  49.8 9.6 %collective-permute-done.10.refs_0_ = bf16[2048,128]{1,0:T(8,128)(2,1)S(1)} collective-permute-done((bf16[2048,128]{1,0:T(8,128)(2,1)}, bf16[2048,128]{1,0:T(8,128)(2,1)S(1)}, u32[]{:S(2)}, u32[]{:S(2)}) %collective-permute-start.10) | collective-permute-done | bytes 524320 | tf_op jit(solution)/shard_map/ppermute | solution.py:24
  59.4 1.0 collective-permute-start.24
  60.5 2.7 %collective-permute-start.6 = (bf16[2048,128]{1,0:T(8,128)(2,1)S(1)}, bf16[2048,128]{1,0:T(8,128)(2,1)S(1)}, u32[]{:S(2)}, u32[]{:S(2)}) collective-permute-start(bf16[2048,128]{1,0:T(8,128)(2,1)S(1)} %collective-permute-done.5.refs_2_), channel_id=1, source_target_pairs={{0,56},{4,60},{8,0},{12,4},{16,8},{20,12},{24,16},{28,20},{32,24},... | collective-permute-start | bytes 1572872 | tf_op jit(solution)/shard_map/ppermute | solution.py:24
  63.1 0.8 collective-permute-start.25
  64.0 2.7 %collective-permute-start.15 = (bf16[2048,128]{1,0:T(8,128)(2,1)S(1)}, bf16[2048,128]{1,0:T(8,128)(2,1)S(1)}, u32[]{:S(2)}, u32[]{:S(2)}) collective-permute-start(bf16[2048,128]{1,0:T(8,128)(2,1)S(1)} %collective-permute-done.14.refs_2_), channel_id=1, source_target_pairs={{0,56},{4,60},{8,0},{12,4},{16,8},{20,12},{24,16},{28,20},{32,24},... | collective-permute-start | bytes 1572872 | tf_op jit(solution)/shard_map/ppermute | solution.py:24
  66.7 8.5 %collective-permute-done.1.refs_0_ = bf16[2048,128]{1,0:T(8,128)(2,1)S(1)} collective-permute-done((bf16[2048,128]{1,0:T(8,128)(2,1)S(1)}, bf16[2048,128]{1,0:T(8,128)(2,1)S(1)}, u32[]{:S(2)}, u32[]{:S(2)}) %collective-permute-start.1) | collective-permute-done | bytes 524320 | tf_op jit(solution)/shard_map/ppermute | solution.py:24
  75.1 1.3 collective-permute-start.22
  76.5 9.9 %collective-permute-done.11.refs_0_ = bf16[2048,128]{1,0:T(8,128)(2,1)S(1)} collective-permute-done((bf16[2048,128]{1,0:T(8,128)(2,1)S(1)}, bf16[2048,128]{1,0:T(8,128)(2,1)S(1)}, u32[]{:S(2)}, u32[]{:S(2)}) %collective-permute-start.11) | collective-permute-done | bytes 524320 | tf_op jit(solution)/shard_map/ppermute | solution.py:24
  86.4 0.9 collective-permute-start.20
  87.4 2.8 %collective-permute-start.7 = (bf16[2048,128]{1,0:T(8,128)(2,1)S(1)}, bf16[2048,128]{1,0:T(8,128)(2,1)S(1)}, u32[]{:S(2)}, u32[]{:S(2)}) collective-permute-start(bf16[2048,128]{1,0:T(8,128)(2,1)S(1)} %collective-permute-done.6.refs_2_), channel_id=1, source_target_pairs={{0,56},{4,60},{8,0},{12,4},{16,8},{20,12},{24,16},{28,20},{32,24},... | collective-permute-start | bytes 1572872 | tf_op jit(solution)/shard_map/ppermute | solution.py:24
  90.2 2.7 %collective-permute-start.16 = (bf16[2048,128]{1,0:T(8,128)(2,1)S(1)}, bf16[2048,128]{1,0:T(8,128)(2,1)S(1)}, u32[]{:S(2)}, u32[]{:S(2)}) collective-permute-start(bf16[2048,128]{1,0:T(8,128)(2,1)S(1)} %collective-permute-done.15.refs_2_), channel_id=1, source_target_pairs={{0,56},{4,60},{8,0},{12,4},{16,8},{20,12},{24,16},{28,20},{32,24},... | collective-permute-start | bytes 1572872 | tf_op jit(solution)/shard_map/ppermute | solution.py:24
  92.9 9.0 %collective-permute-done.2.refs_0_ = bf16[2048,128]{1,0:T(8,128)(2,1)S(1)} collective-permute-done((bf16[2048,128]{1,0:T(8,128)(2,1)S(1)}, bf16[2048,128]{1,0:T(8,128)(2,1)S(1)}, u32[]{:S(2)}, u32[]{:S(2)}) %collective-permute-start.2) | collective-permute-done | bytes 524320 | tf_op jit(solution)/shard_map/ppermute | solution.py:24
  101.9 1.3 collective-permute-start.18
  103.3 2.7 %collective-permute-start.8 = (bf16[2048,128]{1,0:T(8,128)(2,1)S(1)}, bf16[2048,128]{1,0:T(8,128)(2,1)S(1)}, u32[]{:S(2)}, u32[]{:S(2)}) collective-permute-start(bf16[2048,128]{1,0:T(8,128)(2,1)S(1)} %collective-permute-done.7.refs_2_), channel_id=1, source_target_pairs={{0,56},{4,60},{8,0},{12,4},{16,8},{20,12},{24,16},{28,20},{32,24},... | collective-permute-start | bytes 1572872 | tf_op jit(solution)/shard_map/ppermute | solution.py:24
  105.9 7.2 %collective-permute-done.12.refs_0_ = bf16[2048,128]{1,0:T(8,128)(2,1)S(1)} collective-permute-done((bf16[2048,128]{1,0:T(8,128)(2,1)S(1)}, bf16[2048,128]{1,0:T(8,128)(2,1)S(1)}, u32[]{:S(2)}, u32[]{:S(2)}) %collective-permute-start.12) | collective-permute-done | bytes 524320 | tf_op jit(solution)/shard_map/ppermute | solution.py:24
  113.2 1.3 collective-permute-start.19
  115.0 9.4 %collective-permute-done.3.refs_0_ = bf16[2048,128]{1,0:T(8,128)(2,1)S(1)} collective-permute-done((bf16[2048,128]{1,0:T(8,128)(2,1)S(1)}, bf16[2048,128]{1,0:T(8,128)(2,1)S(1)}, u32[]{:S(2)}, u32[]{:S(2)}) %collective-permute-start.3) | collective-permute-done | bytes 524320 | tf_op jit(solution)/shard_map/ppermute | solution.py:24
  124.4 0.9 collective-permute-start.4
  125.3 0.6 add_bitcast_fusion
  125.9 1.0 copy-done
  126.9 1.0 copy-done.1
  127.9 1.3 place.9
  129.3 1.4 place.10
  130.7 1.4 place.11
  132.0 1.4 place.12
  133.4 1.4 place.13
  134.8 1.4 place.14
  136.2 1.4 place.15
  137.6 1.0 place.16
  138.6 1.0 place.17
  (51 shorter events, 1.5 us)
Async XLA Ops:
  1.5 3.5 %collective-permute-start.30 = (bf16[16,128]{1,0:T(8,128)(2,1)S(1)}, bf16[16,128]{1,0:T(8,128)(2,1)S(1)}, u32[]{:S(2)}, u32[]{:S(2)}) collective-permute-start(bf16[16,128]{1,0:T(8,128)(2,1)S(1)} %fusion.1), channel_id=1, source_target_pairs={{0,8},{4,12},{8,0},{12,4},{16,24},{20,28},{24,16},{28,20},{32,40},... | collective-permute-start | bytes 12296 | tf_op jit(solution)/shard_map/ppermute | solution.py:19
  5.1 4.0 %collective-permute-start.31 = (bf16[16,128]{1,0:T(8,128)(2,1)S(1)}, bf16[16,128]{1,0:T(8,128)(2,1)S(1)}, u32[]{:S(2)}, u32[]{:S(2)}) collective-permute-start(bf16[16,128]{1,0:T(8,128)(2,1)S(1)} %fusion.2), channel_id=1, source_target_pairs={{0,16},{4,20},{8,24},{12,28},{16,0},{20,4},{24,8},{28,12},{32,48},... | collective-permute-start | bytes 12296 | tf_op jit(solution)/shard_map/ppermute | solution.py:19
  9.2 2.5 %collective-permute-start.32 = (bf16[16,128]{1,0:T(8,128)(2,1)S(1)}, bf16[16,128]{1,0:T(8,128)(2,1)S(1)}, u32[]{:S(2)}, u32[]{:S(2)}) collective-permute-start(bf16[16,128]{1,0:T(8,128)(2,1)S(1)} %fusion.3), channel_id=1, source_target_pairs={{0,1},{1,0},{2,3},{3,2},{4,5},{5,4},{6,7},{7,6},{8,9},{9,8},{10,11... | collective-permute-start | bytes 12296 | tf_op jit(solution)/shard_map/ppermute | solution.py:19
  11.7 7.1 %collective-permute-start.33 = (bf16[16,128]{1,0:T(8,128)(2,1)S(1)}, bf16[16,128]{1,0:T(8,128)(2,1)S(1)}, u32[]{:S(2)}, u32[]{:S(2)}) collective-permute-start(bf16[16,128]{1,0:T(8,128)(2,1)S(1)} %add.26), channel_id=1, source_target_pairs={{0,32},{4,36},{8,40},{12,44},{16,48},{20,52},{24,56},{28,60},{32,0... | collective-permute-start | bytes 12296 | tf_op jit(solution)/shard_map/ppermute | solution.py:19
  18.8 4.3 %collective-permute-start.34 = (bf16[16,128]{1,0:T(8,128)(2,1)S(1)}, bf16[16,128]{1,0:T(8,128)(2,1)S(1)}, u32[]{:S(2)}, u32[]{:S(2)}) collective-permute-start(bf16[16,128]{1,0:T(8,128)(2,1)S(1)} %add.27), channel_id=1, source_target_pairs={{0,2},{1,3},{2,0},{3,1},{4,6},{5,7},{6,4},{7,5},{8,10},{9,11},{10,... | collective-permute-start | bytes 12296 | tf_op jit(solution)/shard_map/ppermute | solution.py:19
  23.0 13.2 %collective-permute-start.35 = (bf16[16,128]{1,0:T(8,128)(2,1)S(1)}, bf16[16,128]{1,0:T(8,128)(2,1)S(1)}, u32[]{:S(2)}, u32[]{:S(2)}) collective-permute-start(bf16[16,128]{1,0:T(8,128)(2,1)S(1)} %add.28), channel_id=1, source_target_pairs={{0,4},{4,0},{8,12},{12,8},{16,20},{20,16},{24,28},{28,24},{32,36},... | collective-permute-start | bytes 12296 | tf_op jit(solution)/shard_map/ppermute | solution.py:19
  32.1 4.7 %collective-permute-start.28 = (bf16[2048,128]{1,0:T(8,128)(2,1)}, bf16[2048,128]{1,0:T(8,128)(2,1)S(1)}, u32[]{:S(2)}, u32[]{:S(2)}) collective-permute-start(bf16[2048,128]{1,0:T(8,128)(2,1)} %get-tuple-element.23.refs_0_), channel_id=1, source_target_pairs={{0,4},{4,0},{8,12},{12,8},{16,20},{20,16},{24,28},{28,24},{32,36},... | collective-permute-start | bytes 1572872 | tf_op jit(solution)/shard_map/ppermute | solution.py:29
  32.2 16.0 %collective-permute-start = (bf16[2048,128]{1,0:T(8,128)(2,1)}, bf16[2048,128]{1,0:T(8,128)(2,1)S(1)}, u32[]{:S(2)}, u32[]{:S(2)}) collective-permute-start(bf16[2048,128]{1,0:T(8,128)(2,1)} %get-tuple-element.23.refs_0_), channel_id=1, source_target_pairs={{0,8},{4,12},{8,16},{12,20},{16,24},{20,28},{24,32},{28,36},{32,40... | collective-permute-start | bytes 1572872 | tf_op jit(solution)/shard_map/ppermute | solution.py:24
  32.5 17.3 %collective-permute-start.5 = (bf16[2048,128]{1,0:T(8,128)(2,1)}, bf16[2048,128]{1,0:T(8,128)(2,1)S(1)}, u32[]{:S(2)}, u32[]{:S(2)}) collective-permute-start(bf16[2048,128]{1,0:T(8,128)(2,1)} %get-tuple-element.24.refs_2_), channel_id=1, source_target_pairs={{0,56},{4,60},{8,0},{12,4},{16,8},{20,12},{24,16},{28,20},{32,24},... | collective-permute-start | bytes 1572872 | tf_op jit(solution)/shard_map/ppermute | solution.py:24
  36.2 23.2 %collective-permute-start.10 = (bf16[2048,128]{1,0:T(8,128)(2,1)}, bf16[2048,128]{1,0:T(8,128)(2,1)S(1)}, u32[]{:S(2)}, u32[]{:S(2)}) collective-permute-start(bf16[2048,128]{1,0:T(8,128)(2,1)} %get-tuple-element.24.refs_2_), channel_id=1, source_target_pairs={{0,8},{4,12},{8,16},{12,20},{16,24},{20,28},{24,32},{28,36},{32,40... | collective-permute-start | bytes 1572872 | tf_op jit(solution)/shard_map/ppermute | solution.py:24
  36.2 24.2 %collective-permute-start.29 = (bf16[2048,128]{1,0:T(8,128)(2,1)}, bf16[2048,128]{1,0:T(8,128)(2,1)S(1)}, u32[]{:S(2)}, u32[]{:S(2)}) collective-permute-start(bf16[2048,128]{1,0:T(8,128)(2,1)} %get-tuple-element.24.refs_2_), channel_id=1, source_target_pairs={{0,4},{4,0},{8,12},{12,8},{16,20},{20,16},{24,28},{28,24},{32,36},... | collective-permute-start | bytes 1572872 | tf_op jit(solution)/shard_map/ppermute | solution.py:29
  36.8 23.6 %collective-permute-start.14 = (bf16[2048,128]{1,0:T(8,128)(2,1)}, bf16[2048,128]{1,0:T(8,128)(2,1)S(1)}, u32[]{:S(2)}, u32[]{:S(2)}) collective-permute-start(bf16[2048,128]{1,0:T(8,128)(2,1)} %get-tuple-element.23.refs_0_), channel_id=1, source_target_pairs={{0,56},{4,60},{8,0},{12,4},{16,8},{20,12},{24,16},{28,20},{32,24},... | collective-permute-start | bytes 1572872 | tf_op jit(solution)/shard_map/ppermute | solution.py:24
  48.2 14.9 %collective-permute-start.26 = (bf16[2048,128]{1,0:T(8,128)(2,1)S(1)}, bf16[2048,128]{1,0:T(8,128)(2,1)S(1)}, u32[]{:S(2)}, u32[]{:S(2)}) collective-permute-start(bf16[2048,128]{1,0:T(8,128)(2,1)S(1)} %collective-permute-done.refs_0_), channel_id=1, source_target_pairs={{0,4},{4,0},{8,12},{12,8},{16,20},{20,16},{24,28},{28,24},{32,36},... | collective-permute-start | bytes 1572872 | tf_op jit(solution)/shard_map/ppermute | solution.py:29
  49.8 13.3 %collective-permute-start.27 = (bf16[2048,128]{1,0:T(8,128)(2,1)S(1)}, bf16[2048,128]{1,0:T(8,128)(2,1)S(1)}, u32[]{:S(2)}, u32[]{:S(2)}) collective-permute-start(bf16[2048,128]{1,0:T(8,128)(2,1)S(1)} %collective-permute-done.5.refs_2_), channel_id=1, source_target_pairs={{0,4},{4,0},{8,12},{12,8},{16,20},{20,16},{24,28},{28,24},{32,36},... | collective-permute-start | bytes 1572872 | tf_op jit(solution)/shard_map/ppermute | solution.py:29
  59.4 4.5 %collective-permute-start.24 = (bf16[2048,128]{1,0:T(8,128)(2,1)S(1)}, bf16[2048,128]{1,0:T(8,128)(2,1)S(1)}, u32[]{:S(2)}, u32[]{:S(2)}) collective-permute-start(bf16[2048,128]{1,0:T(8,128)(2,1)S(1)} %collective-permute-done.10.refs_0_), channel_id=1, source_target_pairs={{0,4},{4,0},{8,12},{12,8},{16,20},{20,16},{24,28},{28,24},{32,36},... | collective-permute-start | bytes 1572872 | tf_op jit(solution)/shard_map/ppermute | solution.py:29
  60.4 14.7 %collective-permute-start.1 = (bf16[2048,128]{1,0:T(8,128)(2,1)S(1)}, bf16[2048,128]{1,0:T(8,128)(2,1)S(1)}, u32[]{:S(2)}, u32[]{:S(2)}) collective-permute-start(bf16[2048,128]{1,0:T(8,128)(2,1)S(1)} %collective-permute-done.refs_0_), channel_id=1, source_target_pairs={{0,8},{4,12},{8,16},{12,20},{16,24},{20,28},{24,32},{28,36},{32,40... | collective-permute-start | bytes 1572872 | tf_op jit(solution)/shard_map/ppermute | solution.py:24
  60.5 16.0 %collective-permute-start.6 = (bf16[2048,128]{1,0:T(8,128)(2,1)S(1)}, bf16[2048,128]{1,0:T(8,128)(2,1)S(1)}, u32[]{:S(2)}, u32[]{:S(2)}) collective-permute-start(bf16[2048,128]{1,0:T(8,128)(2,1)S(1)} %collective-permute-done.5.refs_2_), channel_id=1, source_target_pairs={{0,56},{4,60},{8,0},{12,4},{16,8},{20,12},{24,16},{28,20},{32,24},... | collective-permute-start | bytes 1572872 | tf_op jit(solution)/shard_map/ppermute | solution.py:24
  63.1 23.2 %collective-permute-start.11 = (bf16[2048,128]{1,0:T(8,128)(2,1)S(1)}, bf16[2048,128]{1,0:T(8,128)(2,1)S(1)}, u32[]{:S(2)}, u32[]{:S(2)}) collective-permute-start(bf16[2048,128]{1,0:T(8,128)(2,1)S(1)} %collective-permute-done.10.refs_0_), channel_id=1, source_target_pairs={{0,8},{4,12},{8,16},{12,20},{16,24},{20,28},{24,32},{28,36},{32,40... | collective-permute-start | bytes 1572872 | tf_op jit(solution)/shard_map/ppermute | solution.py:24
  63.1 24.1 %collective-permute-start.25 = (bf16[2048,128]{1,0:T(8,128)(2,1)S(1)}, bf16[2048,128]{1,0:T(8,128)(2,1)S(1)}, u32[]{:S(2)}, u32[]{:S(2)}) collective-permute-start(bf16[2048,128]{1,0:T(8,128)(2,1)S(1)} %collective-permute-done.14.refs_2_), channel_id=1, source_target_pairs={{0,4},{4,0},{8,12},{12,8},{16,20},{20,16},{24,28},{28,24},{32,36},... | collective-permute-start | bytes 1572872 | tf_op jit(solution)/shard_map/ppermute | solution.py:29
  64.0 23.3 %collective-permute-start.15 = (bf16[2048,128]{1,0:T(8,128)(2,1)S(1)}, bf16[2048,128]{1,0:T(8,128)(2,1)S(1)}, u32[]{:S(2)}, u32[]{:S(2)}) collective-permute-start(bf16[2048,128]{1,0:T(8,128)(2,1)S(1)} %collective-permute-done.14.refs_2_), channel_id=1, source_target_pairs={{0,56},{4,60},{8,0},{12,4},{16,8},{20,12},{24,16},{28,20},{32,24},... | collective-permute-start | bytes 1572872 | tf_op jit(solution)/shard_map/ppermute | solution.py:24
  75.1 12.2 %collective-permute-start.22 = (bf16[2048,128]{1,0:T(8,128)(2,1)S(1)}, bf16[2048,128]{1,0:T(8,128)(2,1)S(1)}, u32[]{:S(2)}, u32[]{:S(2)}) collective-permute-start(bf16[2048,128]{1,0:T(8,128)(2,1)S(1)} %collective-permute-done.1.refs_0_), channel_id=1, source_target_pairs={{0,4},{4,0},{8,12},{12,8},{16,20},{20,16},{24,28},{28,24},{32,36},... | collective-permute-start | bytes 1572872 | tf_op jit(solution)/shard_map/ppermute | solution.py:29
  76.5 13.7 %collective-permute-start.23 = (bf16[2048,128]{1,0:T(8,128)(2,1)S(1)}, bf16[2048,128]{1,0:T(8,128)(2,1)S(1)}, u32[]{:S(2)}, u32[]{:S(2)}) collective-permute-start(bf16[2048,128]{1,0:T(8,128)(2,1)S(1)} %collective-permute-done.6.refs_2_), channel_id=1, source_target_pairs={{0,4},{4,0},{8,12},{12,8},{16,20},{20,16},{24,28},{28,24},{32,36},... | collective-permute-start | bytes 1572872 | tf_op jit(solution)/shard_map/ppermute | solution.py:29
  86.4 3.8 %collective-permute-start.20 = (bf16[2048,128]{1,0:T(8,128)(2,1)S(1)}, bf16[2048,128]{1,0:T(8,128)(2,1)S(1)}, u32[]{:S(2)}, u32[]{:S(2)}) collective-permute-start(bf16[2048,128]{1,0:T(8,128)(2,1)S(1)} %collective-permute-done.11.refs_0_), channel_id=1, source_target_pairs={{0,4},{4,0},{8,12},{12,8},{16,20},{20,16},{24,28},{28,24},{32,36},... | collective-permute-start | bytes 1572872 | tf_op jit(solution)/shard_map/ppermute | solution.py:29
  87.2 14.7 %collective-permute-start.2 = (bf16[2048,128]{1,0:T(8,128)(2,1)S(1)}, bf16[2048,128]{1,0:T(8,128)(2,1)S(1)}, u32[]{:S(2)}, u32[]{:S(2)}) collective-permute-start(bf16[2048,128]{1,0:T(8,128)(2,1)S(1)} %collective-permute-done.1.refs_0_), channel_id=1, source_target_pairs={{0,8},{4,12},{8,16},{12,20},{16,24},{20,28},{24,32},{28,36},{32,40... | collective-permute-start | bytes 1572872 | tf_op jit(solution)/shard_map/ppermute | solution.py:24
  87.2 16.0 %collective-permute-start.21 = (bf16[2048,128]{1,0:T(8,128)(2,1)S(1)}, bf16[2048,128]{1,0:T(8,128)(2,1)S(1)}, u32[]{:S(2)}, u32[]{:S(2)}) collective-permute-start(bf16[2048,128]{1,0:T(8,128)(2,1)S(1)} %collective-permute-done.15.refs_2_), channel_id=1, source_target_pairs={{0,4},{4,0},{8,12},{12,8},{16,20},{20,16},{24,28},{28,24},{32,36},... | collective-permute-start | bytes 1572872 | tf_op jit(solution)/shard_map/ppermute | solution.py:29
  87.4 15.9 %collective-permute-start.7 = (bf16[2048,128]{1,0:T(8,128)(2,1)S(1)}, bf16[2048,128]{1,0:T(8,128)(2,1)S(1)}, u32[]{:S(2)}, u32[]{:S(2)}) collective-permute-start(bf16[2048,128]{1,0:T(8,128)(2,1)S(1)} %collective-permute-done.6.refs_2_), channel_id=1, source_target_pairs={{0,56},{4,60},{8,0},{12,4},{16,8},{20,12},{24,16},{28,20},{32,24},... | collective-permute-start | bytes 1572872 | tf_op jit(solution)/shard_map/ppermute | solution.py:24
  90.2 23.0 %collective-permute-start.12 = (bf16[2048,128]{1,0:T(8,128)(2,1)S(1)}, bf16[2048,128]{1,0:T(8,128)(2,1)S(1)}, u32[]{:S(2)}, u32[]{:S(2)}) collective-permute-start(bf16[2048,128]{1,0:T(8,128)(2,1)S(1)} %collective-permute-done.11.refs_0_), channel_id=1, source_target_pairs={{0,8},{4,12},{8,16},{12,20},{16,24},{20,28},{24,32},{28,36},{32,40... | collective-permute-start | bytes 1572872 | tf_op jit(solution)/shard_map/ppermute | solution.py:24
  90.2 24.3 %collective-permute-start.16 = (bf16[2048,128]{1,0:T(8,128)(2,1)S(1)}, bf16[2048,128]{1,0:T(8,128)(2,1)S(1)}, u32[]{:S(2)}, u32[]{:S(2)}) collective-permute-start(bf16[2048,128]{1,0:T(8,128)(2,1)S(1)} %collective-permute-done.15.refs_2_), channel_id=1, source_target_pairs={{0,56},{4,60},{8,0},{12,4},{16,8},{20,12},{24,16},{28,20},{32,24},... | collective-permute-start | bytes 1572872 | tf_op jit(solution)/shard_map/ppermute | solution.py:24
  101.9 12.6 %collective-permute-start.18 = (bf16[2048,128]{1,0:T(8,128)(2,1)S(1)}, bf16[2048,128]{1,0:T(8,128)(2,1)S(1)}, u32[]{:S(2)}, u32[]{:S(2)}) collective-permute-start(bf16[2048,128]{1,0:T(8,128)(2,1)S(1)} %collective-permute-done.2.refs_0_), channel_id=1, source_target_pairs={{0,4},{4,0},{8,12},{12,8},{16,20},{20,16},{24,28},{28,24},{32,36},... | collective-permute-start | bytes 1572872 | tf_op jit(solution)/shard_map/ppermute | solution.py:29
  103.2 21.1 %collective-permute-start.3 = (bf16[2048,128]{1,0:T(8,128)(2,1)S(1)}, bf16[2048,128]{1,0:T(8,128)(2,1)S(1)}, u32[]{:S(2)}, u32[]{:S(2)}) collective-permute-start(bf16[2048,128]{1,0:T(8,128)(2,1)S(1)} %collective-permute-done.2.refs_0_), channel_id=1, source_target_pairs={{0,8},{4,12},{8,16},{12,20},{16,24},{20,28},{24,32},{28,36},{32,40... | collective-permute-start | bytes 1572872 | tf_op jit(solution)/shard_map/ppermute | solution.py:24
  103.3 22.0 %collective-permute-start.8 = (bf16[2048,128]{1,0:T(8,128)(2,1)S(1)}, bf16[2048,128]{1,0:T(8,128)(2,1)S(1)}, u32[]{:S(2)}, u32[]{:S(2)}) collective-permute-start(bf16[2048,128]{1,0:T(8,128)(2,1)S(1)} %collective-permute-done.7.refs_2_), channel_id=1, source_target_pairs={{0,56},{4,60},{8,0},{12,4},{16,8},{20,12},{24,16},{28,20},{32,24},... | collective-permute-start | bytes 1572872 | tf_op jit(solution)/shard_map/ppermute | solution.py:24
  113.2 21.6 %collective-permute-start.19 = (bf16[2048,128]{1,0:T(8,128)(2,1)S(1)}, bf16[2048,128]{1,0:T(8,128)(2,1)S(1)}, u32[]{:S(2)}, u32[]{:S(2)}) collective-permute-start(bf16[2048,128]{1,0:T(8,128)(2,1)S(1)} %collective-permute-done.7.refs_2_), channel_id=1, source_target_pairs={{0,4},{4,0},{8,12},{12,8},{16,20},{20,16},{24,28},{28,24},{32,36},... | collective-permute-start | bytes 1572872 | tf_op jit(solution)/shard_map/ppermute | solution.py:29
  114.5 21.7 %collective-permute-start.13 = (bf16[2048,128]{1,0:T(8,128)(2,1)S(1)}, bf16[2048,128]{1,0:T(8,128)(2,1)S(1)}, u32[]{:S(2)}, u32[]{:S(2)}) collective-permute-start(bf16[2048,128]{1,0:T(8,128)(2,1)S(1)} %collective-permute-done.12.refs_0_), channel_id=1, source_target_pairs={{0,4},{4,0},{8,12},{12,8},{16,20},{20,16},{24,28},{28,24},{32,36},... | collective-permute-start | bytes 1572872 | tf_op jit(solution)/shard_map/ppermute | solution.py:29
  114.5 21.7 %collective-permute-start.17 = (bf16[2048,128]{1,0:T(8,128)(2,1)S(1)}, bf16[2048,128]{1,0:T(8,128)(2,1)S(1)}, u32[]{:S(2)}, u32[]{:S(2)}) collective-permute-start(bf16[2048,128]{1,0:T(8,128)(2,1)S(1)} %collective-permute-done.16.refs_2_), channel_id=1, source_target_pairs={{0,4},{4,0},{8,12},{12,8},{16,20},{20,16},{24,28},{28,24},{32,36},... | collective-permute-start | bytes 1572872 | tf_op jit(solution)/shard_map/ppermute | solution.py:29
  124.4 14.2 %collective-permute-start.4 = (bf16[2048,128]{1,0:T(8,128)(2,1)S(1)}, bf16[2048,128]{1,0:T(8,128)(2,1)S(1)}, u32[]{:S(2)}, u32[]{:S(2)}) collective-permute-start(bf16[2048,128]{1,0:T(8,128)(2,1)S(1)} %collective-permute-done.3.refs_0_), channel_id=1, source_target_pairs={{0,4},{4,0},{8,12},{12,8},{16,20},{20,16},{24,28},{28,24},{32,36},... | collective-permute-start | bytes 1572872 | tf_op jit(solution)/shard_map/ppermute | solution.py:29
  125.3 13.3 %collective-permute-start.9 = (bf16[2048,128]{1,0:T(8,128)(2,1)S(1)}, bf16[2048,128]{1,0:T(8,128)(2,1)S(1)}, u32[]{:S(2)}, u32[]{:S(2)}) collective-permute-start(bf16[2048,128]{1,0:T(8,128)(2,1)S(1)} %collective-permute-done.8.refs_1_), channel_id=1, source_target_pairs={{0,4},{4,0},{8,12},{12,8},{16,20},{20,16},{24,28},{28,24},{32,36},... | collective-permute-start | bytes 1572872 | tf_op jit(solution)/shard_map/ppermute | solution.py:29
  125.9 1.0 copy-start
  126.9 1.0 copy-start.1

commit v2 on v1

v2 whole, which is shorter than its diff:
```python
import functools
import jax
import jax.numpy as jnp
from jax import lax
from jax.experimental import pallas as pl
from jax.experimental.pallas import tpu as pltpu
from jax.sharding import PartitionSpec as P


mix_rate = 2.0
RING = "fsdp"
LARGE, SMALL = 56 << 20, 8 << 20
ANY = pl.BlockSpec(memory_space=pl.ANY)
VMEM = pl.BlockSpec(memory_space=pltpu.VMEM)


def paired(x, axis, bit):
    n = lax.axis_size(axis)
    return lax.ppermute(x, axis, [(i, i ^ bit) for i in range(n)])


def shifted(x, chips):
    n = lax.axis_size(RING)
    return lax.ppermute(x, RING, [(i, (i + 2 * chips) % n) for i in range(n)])


def swapped(x):
    n = lax.axis_size(RING)
    return lax.ppermute(x, RING, [(i, i ^ 1) for i in range(n)])


def merge_kernel(place_own, wg, lg, hg, wu, lu, hu, og, ou, *refs):
    finals = refs[:2] if place_own else ()
    wbuf, lbuf, hbuf, tbuf, isem, osem = refs[len(finals):]
    mats = ((wg, lg, hg, og), (wu, lu, hu, ou))
    rows = wg.shape[0]
    rank = hg.shape[0]
    loads = [
        [
            pltpu.make_async_copy(src, buf.at[k], isem.at[k, i])
            for i, (src, buf) in enumerate(zip(
                (mat[0], mat[1].at[pl.ds(k * rank, rank), :], mat[2]), (wbuf, lbuf, hbuf)
            ))
        ]
        for k, mat in enumerate(mats)
    ]
    stores = [[pltpu.make_async_copy(tbuf.at[k], mat[3], osem.at[k, 0])] for k, mat in enumerate(mats)]
    for k, final in enumerate(finals):
        mine = pl.multiple_of(lax.axis_index(RING) * rows, rows)
        stores[k].append(
            pltpu.make_async_copy(tbuf.at[k], final.at[:, pl.ds(mine, rows)], osem.at[k, 1])
        )
    for group in loads:
        for cp in group:
            cp.start()
    for k in range(2):
        for cp in loads[k]:
            cp.wait()
        add = lax.dot_general(
            lbuf[k], hbuf[k], (((0,), (0,)), ((), ())), preferred_element_type=jnp.float32
        )
        total = wbuf[k].astype(jnp.float32) + mix_rate * add
        tbuf[k] = total.astype(jnp.bfloat16).T
        for cp in stores[k]:
            cp.start()
    for group in stores:
        for cp in group:
            cp.wait()


def merged(wg, lg, hg, wu, lu, hu, grant, final=None):
    rows, cols = wg.shape
    rank = hg.shape[0]
    out = jax.ShapeDtypeStruct((cols, rows), jnp.bfloat16)
    outs = (out, out)
    if final:
        outs += (jax.ShapeDtypeStruct(final, jnp.bfloat16),) * 2
    return pl.pallas_call(
        functools.partial(merge_kernel, bool(final)),
        out_shape=outs,
        in_specs=[ANY] * 6,
        out_specs=(ANY,) * len(outs),
        scratch_shapes=[
            pltpu.VMEM((2, rows, cols), jnp.bfloat16),
            pltpu.VMEM((2, rank, rows), jnp.bfloat16),
            pltpu.VMEM((2, rank, cols), jnp.bfloat16),
            pltpu.VMEM((2, cols, rows), jnp.bfloat16),
            pltpu.SemaphoreType.DMA((2, 3)),
            pltpu.SemaphoreType.DMA((2, 2)),
        ],
        compiler_params=pltpu.CompilerParams(vmem_limit_bytes=grant),
        name="mix",
        cost_estimate=pl.CostEstimate(flops=4 * rows * cols * rank, bytes_accessed=8 * rows * cols, transcendentals=0),
    )(wg, lg, hg, wu, lu, hu)


def place_kernel(units, *refs):
    n = len(units)
    outs = refs[n + 2:n + 4]
    sem = refs[n + 4]
    me = lax.axis_index(RING)
    chips = lax.axis_size(RING) // 2
    copies = []
    for k, (which, hop, swap, first) in enumerate(units):
        block = refs[k]
        size, rows = block.shape
        core = lax.rem(me, 2)
        chip = lax.rem(lax.div(me, 2) + chips - hop, chips)
        owner = chip * 2 + (1 - core if swap else core)
        copies.append(pltpu.make_async_copy(
            block,
            outs[which].at[pl.ds(first, size), pl.ds(pl.multiple_of(owner * rows, rows), rows)],
            sem.at[k],
        ))
    for cp in copies:
        cp.start()
    for cp in copies:
        cp.wait()


def place(outs, shape, blocks, units):
    n = len(blocks)
    operands = (*blocks, *outs)
    out = jax.ShapeDtypeStruct(shape, jnp.bfloat16)
    return pl.pallas_call(
        functools.partial(place_kernel, units),
        out_shape=(out, out),
        in_specs=[ANY] * len(operands),
        out_specs=(ANY, ANY),
        scratch_shapes=[pltpu.SemaphoreType.DMA((n,))],
        input_output_aliases={n: 0, n + 1: 1},
        compiler_params=pltpu.CompilerParams(vmem_limit_bytes=1 << 20),
        name="place",
        cost_estimate=pl.CostEstimate(
            flops=1_000_000 * n, bytes_accessed=4 * sum(b.size for b in blocks), transcendentals=0
        ),
    )(*operands)


def body(weight_gate, low_gate, high_gate, weight_up, low_up, high_up, norm_train, norm_step):
    rows, cols = weight_gate.shape
    chips = lax.axis_size(RING) // 2
    shape = (cols, rows * 2 * chips)
    far = chips // 2

    gate_above, up_below = shifted(weight_gate, 1), shifted(weight_up, -1)
    low = jnp.concatenate([low_gate.T, low_up.T], axis=0)
    low_above, low_below = shifted(low, 1), shifted(low, -1)
    up_above, gate_below = shifted(weight_up, 1), shifted(weight_gate, -1)

    def mix(gate, gate_low, up, up_low, grant, final=None):
        return merged(gate, gate_low, high_gate, up, up_low, high_up, grant, final)

    held = {}
    held["g", 0], held["u", 0], *outs = mix(weight_gate, low, weight_up, low, LARGE, shape)
    held["g", 1], held["u", -1] = mix(gate_above, low_above, up_below, low_below, SMALL)
    held["g", -1], held["u", 1] = mix(gate_below, low_below, up_above, low_above, SMALL)
    for h in range(2, far):
        held["g", h] = shifted(held["g", h - 1], 1)
        held["u", -h] = shifted(held["u", 1 - h], -1)
        held["u", h] = shifted(held["u", h - 1], 1)
        held["g", -h] = shifted(held["g", 1 - h], -1)
    held = {(*k, 0): v for k, v in held.items()}
    cut = cols - cols // 4
    for first, end in ((0, cut), (cut, cols)):
        held["g", far, first] = shifted(held["g", far - 1, 0][first:end], 1)
        held["u", -far, first] = shifted(held["u", 1 - far, 0][first:end], -1)

    other = {k: swapped(v) for k, v in held.items()}

    def put(outs, keys):
        units = [("gu".index(w), h, s, first) for w, h, first, s in keys]
        blocks = [(other if s else held)[w, h, first] for w, h, first, s in keys]
        return place(outs, shape, blocks, units)

    def both(*keys):
        return [(w, h, 0, s) for w, h in keys for s in (False, True)]

    for h in range(1, far):
        first = [("g", 0, 0, True), ("u", 0, 0, True)] if h == 1 else []
        outs = put(outs, first + both(("g", h), ("u", -h)))
        outs = put(outs, both(("u", h), ("g", -h)))
    last = [("g", far), ("u", -far)]
    outs = put(outs, [(*k, 0, False) for k in last])
    outs = put(outs, [(*k, 0, True) for k in last] + [(*k, cut, False) for k in last])
    outs = put(outs, [(*k, cut, True) for k in last])
    own = (norm_train + norm_step).astype(jnp.bfloat16)
    models = lax.axis_size("model")
    tile = (2 * chips, models * own.size)
    row = lax.broadcasted_iota(jnp.int32, tile, 0) == lax.axis_index(RING)
    lane = lax.broadcasted_iota(jnp.int32, tile, 1) // own.size == lax.axis_index("model")
    norm = jnp.where(row & lane, jnp.tile(own, models)[None], jnp.bfloat16(0))
    for axis, bit in NORM_STEPS:
        norm = norm + paired(norm, axis, bit)
    serve_norm = norm.reshape(-1)
    return outs[0], outs[1], serve_norm


NORM_STEPS = (
    (RING, 2), ("model", 1), (RING, 4),
    (RING, 8), ("model", 2), (RING, 1),
)


def solution(mesh):
    return jax.shard_map(
        body,
        mesh=mesh,
        in_specs=(
            P(("ens", "fsdp"), "model"),
            P(("ens", "fsdp"), None),
            P("ens", "model"),
            P(("ens", "fsdp"), "model"),
            P(("ens", "fsdp"), None),
            P("ens", "model"),
            P(("ens", "fsdp", "model")),
            P(("ens", "fsdp", "model")),
        ),
        out_specs=(P(("ens", "model"), None), P(("ens", "model"), None), P("ens")),
        check_vma=False,
    )
```

time: 140 us -> 138 us (0.986)
  waiting for transfers between devices: 67.9 us -> 61.3 us
  Pallas kernels: 14.3 us -> 17 us
  local copies, waits for them, and re-layouts: 2.17 us -> 3.78 us
    ppermute x14 -> x18, waiting for transfers between devices: 62.1 us -> 43.2 us  [shifted(): return lax.ppermute(x, RING, [(i, (i + 2 * chips) % n) for i in range(n)])]
    ppermute x6, waiting for transfers between devices: 5.75 us -> 18.1 us  [paired(): return lax.ppermute(x, axis, [(i, i ^ bit) for i in range(n)])]
    ppermute x6, starting transfers between devices: 21.9 us -> 11.1 us  [paired(): return lax.ppermute(x, axis, [(i, i ^ bit) for i in range(n)])]
    ppermute x16 -> x18, starting transfers between devices: 10.4 us -> 18.3 us  [swapped(): return lax.ppermute(x, RING, [(i, i ^ 1) for i in range(n)])]
    pallas_call x10 -> x12, Pallas kernels: 14.3 us -> 17 us  [the longest x9 11.2 us: place(): pl.pallas_call(functools.partial(place_kernel, units), out_shape=(out, ou...]
    ppermute x14 -> x18, starting transfers between devices: 20.5 us -> 22.4 us  [shifted(): return lax.ppermute(x, RING, [(i, (i + 2 * chips) % n) for i in range(n)])]
    unnamed x4 -> x10, local copies, waits for them, and re-layouts: 2.08 us -> 3.62 us
  transfers between devices with their start and end apart: 36 -> 42, of which waited for: 12 -> 12; matrix products, arithmetic and copies ran while one was open for 0% -> 1% of each run, Pallas kernels for 10% -> 12%
where the time goes in v2:
time: 138 us; the launch traced here: 137 us
  waiting for transfers between devices  61.3 us (44%)
  starting transfers between devices  51.9 us (38%)
  Pallas kernels  17 us (12%)
  local copies, waits for them, and re-layouts  3.78 us (3%)
  other arithmetic  2.26 us (2%)
    ppermute x18, waiting for transfers between devices, shifted(): return lax.ppermute(x, RING, [(i, (i + 2 * chips) % n) for i in range(n)])  43.2 us
    ppermute x18, starting transfers between devices, shifted(): return lax.ppermute(x, RING, [(i, (i + 2 * chips) % n) for i in range(n)])  22.4 us
    ppermute x18, starting transfers between devices, swapped(): return lax.ppermute(x, RING, [(i, i ^ 1) for i in range(n)])  18.3 us
    ppermute x6, waiting for transfers between devices, paired(): return lax.ppermute(x, axis, [(i, i ^ bit) for i in range(n)])  18.1 us
    pallas_call x9, Pallas kernels, place(): pl.pallas_call(functools.partial(place_kernel, units), out_shape=(out, ou...  11.2 us
    ppermute x6, starting transfers between devices, paired(): return lax.ppermute(x, axis, [(i, i ^ bit) for i in range(n)])  11.1 us
    pallas_call x3, Pallas kernels, merged(): pl.pallas_call(functools.partial(merge_kernel, bool(final)), out_shape=ou...  5.74 us
    unnamed x10, local copies, waits for them, and re-layouts  3.62 us
  transfers between devices with their start and end apart: 42, of which 12 were waited for; matrix products, arithmetic and copies ran while one was open for 1% of the time, Pallas kernels for 12%

profile of v2, /device:TPU:1, one launch (start us, length us, event | category | flops | bytes accessed | tf_op | source)
XLA Modules:
  0.0 137.3 jit_solution(15857359571437091565)
XLA Ops:
  1.5 2.5 %collective-permute-start.36 = (bf16[16,128]{1,0:T(8,128)(2,1)S(1)}, bf16[16,128]{1,0:T(8,128)(2,1)S(1)}, u32[]{:S(2)}, u32[]{:S(2)}) collective-permute-start(bf16[16,128]{1,0:T(8,128)(2,1)S(1)} %fusion.1), channel_id=1, source_target_pairs={{0,8},{4,12},{8,0},{12,4},{16,24},{20,28},{24,16},{28,20},{32,40},... | collective-permute-start | bytes 12296 | tf_op jit(solution)/shard_map/ppermute | solution.py:19
  4.1 4.6 %collective-permute-start.2 = (bf16[128,2048]{1,0:T(8,128)(2,1)}, bf16[128,2048]{1,0:T(8,128)(2,1)S(1)}, u32[]{:S(2)}, u32[]{:S(2)}) collective-permute-start(bf16[128,2048]{1,0:T(8,128)(2,1)} %wu.1), channel_id=1, source_target_pairs={{0,56},{4,60},{8,0},{12,4},{16,8},{20,12},{24,16},{28,20},{32,24},... | collective-permute-start | bytes 1572872 | tf_op jit(solution)/shard_map/ppermute | solution.py:24
  8.8 1.2 collective-permute-start.37
  10.0 1.7 %collective-permute-start.16 = (bf16[128,2048]{1,0:T(8,128)(2,1)}, bf16[128,2048]{1,0:T(8,128)(2,1)S(1)}, u32[]{:S(2)}, u32[]{:S(2)}) collective-permute-start(bf16[128,2048]{1,0:T(8,128)(2,1)} %wg.1), channel_id=1, source_target_pairs={{0,56},{4,60},{8,0},{12,4},{16,8},{20,12},{24,16},{28,20},{32,24},... | collective-permute-start | bytes 1572872 | tf_op jit(solution)/shard_map/ppermute | solution.py:24
  12.7 18.0 %collective-permute-done.38 = bf16[16,128]{1,0:T(8,128)(2,1)S(1)} collective-permute-done((bf16[16,128]{1,0:T(8,128)(2,1)S(1)}, bf16[16,128]{1,0:T(8,128)(2,1)S(1)}, u32[]{:S(2)}, u32[]{:S(2)}) %collective-permute-start.38) | collective-permute-done | bytes 4128 | tf_op jit(solution)/shard_map/ppermute | solution.py:19
  30.8 2.1 %collective-permute-start.1 = (bf16[64,128]{1,0:T(8,128)(2,1)S(1)}, bf16[64,128]{1,0:T(8,128)(2,1)S(1)}, u32[]{:S(2)}, u32[]{:S(2)}) collective-permute-start(bf16[64,128]{1,0:T(8,128)(2,1)S(1)} %pad_maximum_fusion.lg.lu), channel_id=1, source_target_pairs={{0,8},{4,12},{8,16},{12,20},{16,24},{20,28},{24,32},{28,36},{32,40... | collective-permute-start | bytes 49160 | tf_op jit(solution)/shard_map/ppermute | solution.py:24
  32.9 1.7 %collective-permute-done.1.lg.lu = bf16[64,128]{1,0:T(8,128)(2,1)S(1)} collective-permute-done((bf16[64,128]{1,0:T(8,128)(2,1)S(1)}, bf16[64,128]{1,0:T(8,128)(2,1)S(1)}, u32[]{:S(2)}, u32[]{:S(2)}) %collective-permute-start.1) | collective-permute-done | bytes 16416 | tf_op jit(solution)/shard_map/ppermute | solution.py:24
  34.6 1.2 collective-permute-start.3
  35.8 1.6 %collective-permute-done.3.lu.lg = bf16[64,128]{1,0:T(8,128)(2,1)S(1)} collective-permute-done((bf16[64,128]{1,0:T(8,128)(2,1)S(1)}, bf16[64,128]{1,0:T(8,128)(2,1)S(1)}, u32[]{:S(2)}, u32[]{:S(2)}) %collective-permute-start.3) | collective-permute-done | bytes 16416 | tf_op jit(solution)/shard_map/ppermute | solution.py:24
  37.4 4.2 %collective-permute-start.39 = (bf16[16,128]{1,0:T(8,128)(2,1)S(1)}, bf16[16,128]{1,0:T(8,128)(2,1)S(1)}, u32[]{:S(2)}, u32[]{:S(2)}) collective-permute-start(bf16[16,128]{1,0:T(8,128)(2,1)S(1)} %add.26), channel_id=1, source_target_pairs={{0,32},{4,36},{8,40},{12,44},{16,48},{20,52},{24,56},{28,60},{32,0... | collective-permute-start | bytes 12296 | tf_op jit(solution)/shard_map/ppermute | solution.py:19
  41.7 2.9 %mix.5 = (bf16[2048,128]{1,0:T(8,128)(2,1)}, bf16[2048,128]{1,0:T(8,128)(2,1)}, bf16[2048,2048]{1,0:T(8,128)(2,1)}, bf16[2048,2048]{1,0:T(8,128)(2,1)}) custom-call(bf16[128,2048]{1,0:T(8,128)(2,1)} %wg.1, bf16[64,128]{1,0:T(8,128)(2,1)} %copy-done.4, bf16[32,2048]{1,0:T(8,128)(2,1)} %hg.5, bf16[128,2048]{1,0:T(8,128)(2,1)} %wu.1, ...), custom_call_target="tpu_custom_call" | custom-call | flops 33554432 | bytes 2097152 | tf_op jit(solution)/shard_map/mix/pallas_call | solution.py:78
  44.6 4.5 %collective-permute-start.32 = (bf16[2048,128]{1,0:T(8,128)(2,1)}, bf16[2048,128]{1,0:T(8,128)(2,1)S(1)}, u32[]{:S(2)}, u32[]{:S(2)}) collective-permute-start(bf16[2048,128]{1,0:T(8,128)(2,1)} %get-tuple-element.33), channel_id=1, source_target_pairs={{0,4},{4,0},{8,12},{12,8},{16,20},{20,16},{24,28},{28,24},{32,36},... | collective-permute-start | bytes 1572872 | tf_op jit(solution)/shard_map/ppermute | solution.py:29
  49.3 2.8 %collective-permute-start.40 = (bf16[16,128]{1,0:T(8,128)(2,1)S(1)}, bf16[16,128]{1,0:T(8,128)(2,1)S(1)}, u32[]{:S(2)}, u32[]{:S(2)}) collective-permute-start(bf16[16,128]{1,0:T(8,128)(2,1)S(1)} %add.27), channel_id=1, source_target_pairs={{0,2},{1,3},{2,0},{3,1},{4,6},{5,7},{6,4},{7,5},{8,10},{9,11},{10,... | collective-permute-start | bytes 12296 | tf_op jit(solution)/shard_map/ppermute | solution.py:19
  52.1 0.9 copy-done
  53.0 0.9 copy-done.2
  53.9 1.4 %mix.3 = (bf16[2048,128]{1,0:T(8,128)(2,1)S(1)}, bf16[2048,128]{1,0:T(8,128)(2,1)S(1)}) custom-call(bf16[128,2048]{1,0:T(8,128)(2,1)S(1)} %collective-permute-done.wg, bf16[64,128]{1,0:T(8,128)(2,1)S(1)} %collective-permute-done.1.lg.lu, bf16[32,2048]{1,0:T(8,128)(2,1)S(1)} %copy-done, bf16[128,2048]{1,0:T(8,128)(2,1)S(1)} %collective-permute-done.2.wu, ...), custom_call_target="tpu_custom_call" | custom-call | flops 33554432 | bytes 2097152 | tf_op jit(solution)/shard_map/mix/pallas_call | solution.py:78
  56.7 0.9 copy-done.1
  57.6 0.9 copy-done.3
  58.5 1.4 %mix.4 = (bf16[2048,128]{1,0:T(8,128)(2,1)S(1)}, bf16[2048,128]{1,0:T(8,128)(2,1)S(1)}) custom-call(bf16[128,2048]{1,0:T(8,128)(2,1)S(1)} %collective-permute-done.16.wg, bf16[64,128]{1,0:T(8,128)(2,1)S(1)} %collective-permute-done.3.lu.lg, bf16[32,2048]{1,0:T(8,128)(2,1)S(1)} %copy-done.1, bf16[128,2048]{1,0:T(8,128)(2,1)S(1)} %collective-permute-done.17.wu, ...), custom_call_target="tpu_custom_call" | custom-call | flops 33554432 | bytes 2097152 | tf_op jit(solution)/shard_map/mix/pallas_call | solution.py:78
  61.1 1.8 %collective-permute-start.8 = (bf16[2048,128]{1,0:T(8,128)(2,1)S(1)}, bf16[2048,128]{1,0:T(8,128)(2,1)S(1)}, u32[]{:S(2)}, u32[]{:S(2)}) collective-permute-start(bf16[2048,128]{1,0:T(8,128)(2,1)S(1)} %get-tuple-element.30.refs_4_), channel_id=1, source_target_pairs={{0,56},{4,60},{8,0},{12,4},{16,8},{20,12},{24,16},{28,20},{32,24},... | collective-permute-start | bytes 1572872 | tf_op jit(solution)/shard_map/ppermute | solution.py:24
  63.8 2.7 %collective-permute-start.21 = (bf16[2048,128]{1,0:T(8,128)(2,1)S(1)}, bf16[2048,128]{1,0:T(8,128)(2,1)S(1)}, u32[]{:S(2)}, u32[]{:S(2)}) collective-permute-start(bf16[2048,128]{1,0:T(8,128)(2,1)S(1)} %get-tuple-element.32.refs_2_), channel_id=1, source_target_pairs={{0,56},{4,60},{8,0},{12,4},{16,8},{20,12},{24,16},{28,20},{32,24},... | collective-permute-start | bytes 1572872 | tf_op jit(solution)/shard_map/ppermute | solution.py:24
  66.5 8.3 %collective-permute-done.4.refs_0_ = bf16[2048,128]{1,0:T(8,128)(2,1)S(1)} collective-permute-done((bf16[2048,128]{1,0:T(8,128)(2,1)S(1)}, bf16[2048,128]{1,0:T(8,128)(2,1)S(1)}, u32[]{:S(2)}, u32[]{:S(2)}) %collective-permute-start.4) | collective-permute-done | bytes 524320 | tf_op jit(solution)/shard_map/ppermute | solution.py:24
  74.8 1.7 %collective-permute-start.28 = (bf16[2048,128]{1,0:T(8,128)(2,1)S(1)}, bf16[2048,128]{1,0:T(8,128)(2,1)S(1)}, u32[]{:S(2)}, u32[]{:S(2)}) collective-permute-start(bf16[2048,128]{1,0:T(8,128)(2,1)S(1)} %collective-permute-done.4.refs_0_), channel_id=1, source_target_pairs={{0,4},{4,0},{8,12},{12,8},{16,20},{20,16},{24,28},{28,24},{32,36},... | collective-permute-start | bytes 1572872 | tf_op jit(solution)/shard_map/ppermute | solution.py:29
  77.2 8.9 %collective-permute-done.18.refs_0_ = bf16[2048,128]{1,0:T(8,128)(2,1)S(1)} collective-permute-done((bf16[2048,128]{1,0:T(8,128)(2,1)S(1)}, bf16[2048,128]{1,0:T(8,128)(2,1)S(1)}, u32[]{:S(2)}, u32[]{:S(2)}) %collective-permute-start.18) | collective-permute-done | bytes 524320 | tf_op jit(solution)/shard_map/ppermute | solution.py:24
  86.0 1.7 %collective-permute-start.26 = (bf16[2048,128]{1,0:T(8,128)(2,1)S(1)}, bf16[2048,128]{1,0:T(8,128)(2,1)S(1)}, u32[]{:S(2)}, u32[]{:S(2)}) collective-permute-start(bf16[2048,128]{1,0:T(8,128)(2,1)S(1)} %collective-permute-done.18.refs_0_), channel_id=1, source_target_pairs={{0,4},{4,0},{8,12},{12,8},{16,20},{20,16},{24,28},{28,24},{32,36},... | collective-permute-start | bytes 1572872 | tf_op jit(solution)/shard_map/ppermute | solution.py:29
  87.8 0.9 collective-permute-start.9
  88.7 1.4 %collective-permute-start.27 = (bf16[2048,128]{1,0:T(8,128)(2,1)S(1)}, bf16[2048,128]{1,0:T(8,128)(2,1)S(1)}, u32[]{:S(2)}, u32[]{:S(2)}) collective-permute-start(bf16[2048,128]{1,0:T(8,128)(2,1)S(1)} %collective-permute-done.21.refs_2_), channel_id=1, source_target_pairs={{0,4},{4,0},{8,12},{12,8},{16,20},{20,16},{24,28},{28,24},{32,36},... | collective-permute-start | bytes 1572872 | tf_op jit(solution)/shard_map/ppermute | solution.py:29
  90.1 7.2 %collective-permute-done.5.refs_0_ = bf16[2048,128]{1,0:T(8,128)(2,1)S(1)} collective-permute-done((bf16[2048,128]{1,0:T(8,128)(2,1)S(1)}, bf16[2048,128]{1,0:T(8,128)(2,1)S(1)}, u32[]{:S(2)}, u32[]{:S(2)}) %collective-permute-start.5) | collective-permute-done | bytes 524320 | tf_op jit(solution)/shard_map/ppermute | solution.py:24
  98.8 2.4 %collective-permute-done.9.refs_2_ = bf16[2048,128]{1,0:T(8,128)(2,1)S(1)} collective-permute-done((bf16[2048,128]{1,0:T(8,128)(2,1)S(1)}, bf16[2048,128]{1,0:T(8,128)(2,1)S(1)}, u32[]{:S(2)}, u32[]{:S(2)}) %collective-permute-start.9) | collective-permute-done | bytes 524320 | tf_op jit(solution)/shard_map/ppermute | solution.py:24
  101.2 1.3 collective-permute-start.24
  102.6 3.3 %collective-permute-start.10 = (bf16[512,128]{1,0:T(8,128)(2,1)S(1)}, bf16[512,128]{1,0:T(8,128)(2,1)S(1)}, u32[]{:S(2)}, u32[]{:S(2)}) collective-permute-start(bf16[512,128]{1,0:T(8,128)(2,1)S(1)} %slice.17), channel_id=1, source_target_pairs={{0,56},{4,60},{8,0},{12,4},{16,8},{20,12},{24,16},{28,20},{32,24},... | collective-permute-start | bytes 393224 | tf_op jit(solution)/shard_map/ppermute | solution.py:24
  105.9 2.6 %collective-permute-done.19.refs_0_ = bf16[2048,128]{1,0:T(8,128)(2,1)S(1)} collective-permute-done((bf16[2048,128]{1,0:T(8,128)(2,1)S(1)}, bf16[2048,128]{1,0:T(8,128)(2,1)S(1)}, u32[]{:S(2)}, u32[]{:S(2)}) %collective-permute-start.19) | collective-permute-done | bytes 524320 | tf_op jit(solution)/shard_map/ppermute | solution.py:24
  108.5 4.0 %collective-permute-done.22.refs_2_ = bf16[2048,128]{1,0:T(8,128)(2,1)S(1)} collective-permute-done((bf16[2048,128]{1,0:T(8,128)(2,1)S(1)}, bf16[2048,128]{1,0:T(8,128)(2,1)S(1)}, u32[]{:S(2)}, u32[]{:S(2)}) %collective-permute-start.22) | collective-permute-done | bytes 524320 | tf_op jit(solution)/shard_map/ppermute | solution.py:24
  112.5 1.0 collective-permute-start.14
  113.5 1.8 %collective-permute-done.10.refs_3_ = bf16[512,128]{1,0:T(8,128)(2,1)S(1)} collective-permute-done((bf16[512,128]{1,0:T(8,128)(2,1)S(1)}, bf16[512,128]{1,0:T(8,128)(2,1)S(1)}, u32[]{:S(2)}, u32[]{:S(2)}) %collective-permute-start.10) | collective-permute-done | bytes 131104 | tf_op jit(solution)/shard_map/ppermute | solution.py:24
  115.3 1.8 %collective-permute-start.25 = (bf16[2048,128]{1,0:T(8,128)(2,1)S(1)}, bf16[2048,128]{1,0:T(8,128)(2,1)S(1)}, u32[]{:S(2)}, u32[]{:S(2)}) collective-permute-start(bf16[2048,128]{1,0:T(8,128)(2,1)S(1)} %collective-permute-done.9.refs_2_), channel_id=1, source_target_pairs={{0,4},{4,0},{8,12},{12,8},{16,20},{20,16},{24,28},{28,24},{32,36},... | collective-permute-start | bytes 1572872 | tf_op jit(solution)/shard_map/ppermute | solution.py:29
  117.1 2.6 %collective-permute-done.6.refs_2_ = bf16[512,128]{1,0:T(8,128)(2,1)S(1)} collective-permute-done((bf16[512,128]{1,0:T(8,128)(2,1)S(1)}, bf16[512,128]{1,0:T(8,128)(2,1)S(1)}, u32[]{:S(2)}, u32[]{:S(2)}) %collective-permute-start.6) | collective-permute-done | bytes 131104 | tf_op jit(solution)/shard_map/ppermute | solution.py:24
  119.7 1.1 collective-permute-start.20
  120.8 2.2 %collective-permute-done.14.refs_1_ = bf16[1536,128]{1,0:T(8,128)(2,1)S(1)} collective-permute-done((bf16[1536,128]{1,0:T(8,128)(2,1)S(1)}, bf16[1536,128]{1,0:T(8,128)(2,1)S(1)}, u32[]{:S(2)}, u32[]{:S(2)}) %collective-permute-start.14) | collective-permute-done | bytes 393248 | tf_op jit(solution)/shard_map/ppermute | solution.py:24
  123.0 1.6 %collective-permute-start.13 = (bf16[1536,128]{1,0:T(8,128)(2,1)S(1)}, bf16[1536,128]{1,0:T(8,128)(2,1)S(1)}, u32[]{:S(2)}, u32[]{:S(2)}) collective-permute-start(bf16[1536,128]{1,0:T(8,128)(2,1)S(1)} %collective-permute-done.12.refs_0_), channel_id=1, source_target_pairs={{0,4},{4,0},{8,12},{12,8},{16,20},{20,16},{24,28},{28,24},{32,36},... | collective-permute-start | bytes 1179656 | tf_op jit(solution)/shard_map/ppermute | solution.py:29
  125.8 1.7 %place.9 = (bf16[2048,2048]{1,0:T(8,128)(2,1)}, bf16[2048,2048]{1,0:T(8,128)(2,1)}) custom-call(bf16[2048,128]{1,0:T(8,128)(2,1)S(1)} %collective-permute-done.32.refs_0_, bf16[2048,128]{1,0:T(8,128)(2,1)S(1)} %collective-permute-done.33.refs_1_, bf16[2048,128]{1,0:T(8,128)(2,1)S(1)} %get-tuple-element.29.refs_2_, ...), custom_call_target="tpu_custom_call", output_to_operand_aliasing={{0}: (6, {}), {1}: (7, {})} | custom-call | flops 6000000 | bytes 6291456 | tf_op jit(solution)/shard_map/place/pallas_call | solution.py:125
  127.5 1.4 place.10
  128.9 1.4 place.11
  130.3 1.4 place.12
  131.6 1.4 place.13
  133.0 1.4 place.14
  134.4 0.9 place.15
  135.3 1.0 place.16
  (76 shorter events, 9.8 us)
Async XLA Ops:
  1.5 7.2 %collective-permute-start.36 = (bf16[16,128]{1,0:T(8,128)(2,1)S(1)}, bf16[16,128]{1,0:T(8,128)(2,1)S(1)}, u32[]{:S(2)}, u32[]{:S(2)}) collective-permute-start(bf16[16,128]{1,0:T(8,128)(2,1)S(1)} %fusion.1), channel_id=1, source_target_pairs={{0,8},{4,12},{8,0},{12,4},{16,24},{20,28},{24,16},{28,20},{32,40},... | collective-permute-start | bytes 12296 | tf_op jit(solution)/shard_map/ppermute | solution.py:19
  4.0 45.1 %collective-permute-start = (bf16[128,2048]{1,0:T(8,128)(2,1)}, bf16[128,2048]{1,0:T(8,128)(2,1)S(1)}, u32[]{:S(2)}, u32[]{:S(2)}) collective-permute-start(bf16[128,2048]{1,0:T(8,128)(2,1)} %wg.1), channel_id=1, source_target_pairs={{0,8},{4,12},{8,16},{12,20},{16,24},{20,28},{24,32},{28,36},{32,40... | collective-permute-start | bytes 1572872 | tf_op jit(solution)/shard_map/ppermute | solution.py:24
  4.1 45.2 %collective-permute-start.2 = (bf16[128,2048]{1,0:T(8,128)(2,1)}, bf16[128,2048]{1,0:T(8,128)(2,1)S(1)}, u32[]{:S(2)}, u32[]{:S(2)}) collective-permute-start(bf16[128,2048]{1,0:T(8,128)(2,1)} %wu.1), channel_id=1, source_target_pairs={{0,56},{4,60},{8,0},{12,4},{16,8},{20,12},{24,16},{28,20},{32,24},... | collective-permute-start | bytes 1572872 | tf_op jit(solution)/shard_map/ppermute | solution.py:24
  8.8 3.0 %collective-permute-start.37 = (bf16[16,128]{1,0:T(8,128)(2,1)S(1)}, bf16[16,128]{1,0:T(8,128)(2,1)S(1)}, u32[]{:S(2)}, u32[]{:S(2)}) collective-permute-start(bf16[16,128]{1,0:T(8,128)(2,1)S(1)} %fusion.2), channel_id=1, source_target_pairs={{0,1},{1,0},{2,3},{3,2},{4,5},{5,4},{6,7},{7,6},{8,9},{9,8},{10,11... | collective-permute-start | bytes 12296 | tf_op jit(solution)/shard_map/ppermute | solution.py:19
  10.0 46.1 %collective-permute-start.16 = (bf16[128,2048]{1,0:T(8,128)(2,1)}, bf16[128,2048]{1,0:T(8,128)(2,1)S(1)}, u32[]{:S(2)}, u32[]{:S(2)}) collective-permute-start(bf16[128,2048]{1,0:T(8,128)(2,1)} %wg.1), channel_id=1, source_target_pairs={{0,56},{4,60},{8,0},{12,4},{16,8},{20,12},{24,16},{28,20},{32,24},... | collective-permute-start | bytes 1572872 | tf_op jit(solution)/shard_map/ppermute | solution.py:24
  11.7 44.5 %collective-permute-start.17 = (bf16[128,2048]{1,0:T(8,128)(2,1)}, bf16[128,2048]{1,0:T(8,128)(2,1)S(1)}, u32[]{:S(2)}, u32[]{:S(2)}) collective-permute-start(bf16[128,2048]{1,0:T(8,128)(2,1)} %wu.1), channel_id=1, source_target_pairs={{0,8},{4,12},{8,16},{12,20},{16,24},{20,28},{24,32},{28,36},{32,40... | collective-permute-start | bytes 1572872 | tf_op jit(solution)/shard_map/ppermute | solution.py:24
  11.8 19.0 %collective-permute-start.38 = (bf16[16,128]{1,0:T(8,128)(2,1)S(1)}, bf16[16,128]{1,0:T(8,128)(2,1)S(1)}, u32[]{:S(2)}, u32[]{:S(2)}) collective-permute-start(bf16[16,128]{1,0:T(8,128)(2,1)S(1)} %fusion.3), channel_id=1, source_target_pairs={{0,16},{4,20},{8,24},{12,28},{16,0},{20,4},{24,8},{28,12},{32,48},... | collective-permute-start | bytes 12296 | tf_op jit(solution)/shard_map/ppermute | solution.py:19
  12.7 28.9 %copy-start.4 = (bf16[64,128]{1,0:T(8,128)(2,1)}, bf16[64,128]{1,0:T(8,128)(2,1)S(1)}, u32[]{:S(2)}) copy-start(bf16[64,128]{1,0:T(8,128)(2,1)S(1)} %pad_maximum_fusion.lg.lu) | copy-start | bytes 49156
  30.8 3.8 %collective-permute-start.1 = (bf16[64,128]{1,0:T(8,128)(2,1)S(1)}, bf16[64,128]{1,0:T(8,128)(2,1)S(1)}, u32[]{:S(2)}, u32[]{:S(2)}) collective-permute-start(bf16[64,128]{1,0:T(8,128)(2,1)S(1)} %pad_maximum_fusion.lg.lu), channel_id=1, source_target_pairs={{0,8},{4,12},{8,16},{12,20},{16,24},{20,28},{24,32},{28,36},{32,40... | collective-permute-start | bytes 49160 | tf_op jit(solution)/shard_map/ppermute | solution.py:24
  34.6 2.9 %collective-permute-start.3 = (bf16[64,128]{1,0:T(8,128)(2,1)S(1)}, bf16[64,128]{1,0:T(8,128)(2,1)S(1)}, u32[]{:S(2)}, u32[]{:S(2)}) collective-permute-start(bf16[64,128]{1,0:T(8,128)(2,1)S(1)} %pad_maximum_fusion.lg.lu), channel_id=1, source_target_pairs={{0,56},{4,60},{8,0},{12,4},{16,8},{20,12},{24,16},{28,20},{32,24},... | collective-permute-start | bytes 49160 | tf_op jit(solution)/shard_map/ppermute | solution.py:24
  37.4 7.2 %collective-permute-start.39 = (bf16[16,128]{1,0:T(8,128)(2,1)S(1)}, bf16[16,128]{1,0:T(8,128)(2,1)S(1)}, u32[]{:S(2)}, u32[]{:S(2)}) collective-permute-start(bf16[16,128]{1,0:T(8,128)(2,1)S(1)} %add.26), channel_id=1, source_target_pairs={{0,32},{4,36},{8,40},{12,44},{16,48},{20,52},{24,56},{28,60},{32,0... | collective-permute-start | bytes 12296 | tf_op jit(solution)/shard_map/ppermute | solution.py:19
  44.6 15.7 %collective-permute-start.32 = (bf16[2048,128]{1,0:T(8,128)(2,1)}, bf16[2048,128]{1,0:T(8,128)(2,1)S(1)}, u32[]{:S(2)}, u32[]{:S(2)}) collective-permute-start(bf16[2048,128]{1,0:T(8,128)(2,1)} %get-tuple-element.33), channel_id=1, source_target_pairs={{0,4},{4,0},{8,12},{12,8},{16,20},{20,16},{24,28},{28,24},{32,36},... | collective-permute-start | bytes 1572872 | tf_op jit(solution)/shard_map/ppermute | solution.py:29
  49.1 12.0 %collective-permute-start.33 = (bf16[2048,128]{1,0:T(8,128)(2,1)}, bf16[2048,128]{1,0:T(8,128)(2,1)S(1)}, u32[]{:S(2)}, u32[]{:S(2)}) collective-permute-start(bf16[2048,128]{1,0:T(8,128)(2,1)} %get-tuple-element.34), channel_id=1, source_target_pairs={{0,4},{4,0},{8,12},{12,8},{16,20},{20,16},{24,28},{28,24},{32,36},... | collective-permute-start | bytes 1572872 | tf_op jit(solution)/shard_map/ppermute | solution.py:29
  49.3 6.0 %collective-permute-start.40 = (bf16[16,128]{1,0:T(8,128)(2,1)S(1)}, bf16[16,128]{1,0:T(8,128)(2,1)S(1)}, u32[]{:S(2)}, u32[]{:S(2)}) collective-permute-start(bf16[16,128]{1,0:T(8,128)(2,1)S(1)} %add.27), channel_id=1, source_target_pairs={{0,2},{1,3},{2,0},{3,1},{4,6},{5,7},{6,4},{7,5},{8,10},{9,11},{10,... | collective-permute-start | bytes 12296 | tf_op jit(solution)/shard_map/ppermute | solution.py:19
  52.1 0.9 copy-start
  53.0 0.9 copy-start.2
  55.3 7.7 %collective-permute-start.34 = (bf16[2048,128]{1,0:T(8,128)(2,1)S(1)}, bf16[2048,128]{1,0:T(8,128)(2,1)S(1)}, u32[]{:S(2)}, u32[]{:S(2)}) collective-permute-start(bf16[2048,128]{1,0:T(8,128)(2,1)S(1)} %get-tuple-element.29.refs_2_), channel_id=1, source_target_pairs={{0,4},{4,0},{8,12},{12,8},{16,20},{20,16},{24,28},{28,24},{32,36},... | collective-permute-start | bytes 1572872 | tf_op jit(solution)/shard_map/ppermute | solution.py:29
  56.1 3.8 %collective-permute-start.41 = (bf16[16,128]{1,0:T(8,128)(2,1)S(1)}, bf16[16,128]{1,0:T(8,128)(2,1)S(1)}, u32[]{:S(2)}, u32[]{:S(2)}) collective-permute-start(bf16[16,128]{1,0:T(8,128)(2,1)S(1)} %add.28), channel_id=1, source_target_pairs={{0,4},{4,0},{8,12},{12,8},{16,20},{20,16},{24,28},{28,24},{32,36},... | collective-permute-start | bytes 12296 | tf_op jit(solution)/shard_map/ppermute | solution.py:19
  56.2 7.6 %collective-permute-start.35 = (bf16[2048,128]{1,0:T(8,128)(2,1)S(1)}, bf16[2048,128]{1,0:T(8,128)(2,1)S(1)}, u32[]{:S(2)}, u32[]{:S(2)}) collective-permute-start(bf16[2048,128]{1,0:T(8,128)(2,1)S(1)} %get-tuple-element.30.refs_4_), channel_id=1, source_target_pairs={{0,4},{4,0},{8,12},{12,8},{16,20},{20,16},{24,28},{28,24},{32,36},... | collective-permute-start | bytes 1572872 | tf_op jit(solution)/shard_map/ppermute | solution.py:29
  56.7 0.9 copy-start.1
  57.6 0.9 copy-start.3
  59.9 3.9 %collective-permute-start.30 = (bf16[2048,128]{1,0:T(8,128)(2,1)S(1)}, bf16[2048,128]{1,0:T(8,128)(2,1)S(1)}, u32[]{:S(2)}, u32[]{:S(2)}) collective-permute-start(bf16[2048,128]{1,0:T(8,128)(2,1)S(1)} %get-tuple-element.31.refs_0_), channel_id=1, source_target_pairs={{0,4},{4,0},{8,12},{12,8},{16,20},{20,16},{24,28},{28,24},{32,36},... | collective-permute-start | bytes 1572872 | tf_op jit(solution)/shard_map/ppermute | solution.py:29
  60.3 14.5 %collective-permute-start.4 = (bf16[2048,128]{1,0:T(8,128)(2,1)S(1)}, bf16[2048,128]{1,0:T(8,128)(2,1)S(1)}, u32[]{:S(2)}, u32[]{:S(2)}) collective-permute-start(bf16[2048,128]{1,0:T(8,128)(2,1)S(1)} %get-tuple-element.29.refs_2_), channel_id=1, source_target_pairs={{0,8},{4,12},{8,16},{12,20},{16,24},{20,28},{24,32},{28,36},{32,40... | collective-permute-start | bytes 1572872 | tf_op jit(solution)/shard_map/ppermute | solution.py:24
  61.1 15.4 %collective-permute-start.8 = (bf16[2048,128]{1,0:T(8,128)(2,1)S(1)}, bf16[2048,128]{1,0:T(8,128)(2,1)S(1)}, u32[]{:S(2)}, u32[]{:S(2)}) collective-permute-start(bf16[2048,128]{1,0:T(8,128)(2,1)S(1)} %get-tuple-element.30.refs_4_), channel_id=1, source_target_pairs={{0,56},{4,60},{8,0},{12,4},{16,8},{20,12},{24,16},{28,20},{32,24},... | collective-permute-start | bytes 1572872 | tf_op jit(solution)/shard_map/ppermute | solution.py:24
  63.0 13.5 %collective-permute-start.31 = (bf16[2048,128]{1,0:T(8,128)(2,1)S(1)}, bf16[2048,128]{1,0:T(8,128)(2,1)S(1)}, u32[]{:S(2)}, u32[]{:S(2)}) collective-permute-start(bf16[2048,128]{1,0:T(8,128)(2,1)S(1)} %get-tuple-element.32.refs_2_), channel_id=1, source_target_pairs={{0,4},{4,0},{8,12},{12,8},{16,20},{20,16},{24,28},{28,24},{32,36},... | collective-permute-start | bytes 1572872 | tf_op jit(solution)/shard_map/ppermute | solution.py:29
  63.8 22.3 %collective-permute-start.18 = (bf16[2048,128]{1,0:T(8,128)(2,1)S(1)}, bf16[2048,128]{1,0:T(8,128)(2,1)S(1)}, u32[]{:S(2)}, u32[]{:S(2)}) collective-permute-start(bf16[2048,128]{1,0:T(8,128)(2,1)S(1)} %get-tuple-element.31.refs_0_), channel_id=1, source_target_pairs={{0,8},{4,12},{8,16},{12,20},{16,24},{20,28},{24,32},{28,36},{32,40... | collective-permute-start | bytes 1572872 | tf_op jit(solution)/shard_map/ppermute | solution.py:24
  63.8 24.0 %collective-permute-start.21 = (bf16[2048,128]{1,0:T(8,128)(2,1)S(1)}, bf16[2048,128]{1,0:T(8,128)(2,1)S(1)}, u32[]{:S(2)}, u32[]{:S(2)}) collective-permute-start(bf16[2048,128]{1,0:T(8,128)(2,1)S(1)} %get-tuple-element.32.refs_2_), channel_id=1, source_target_pairs={{0,56},{4,60},{8,0},{12,4},{16,8},{20,12},{24,16},{28,20},{32,24},... | collective-permute-start | bytes 1572872 | tf_op jit(solution)/shard_map/ppermute | solution.py:24
  74.8 13.9 %collective-permute-start.28 = (bf16[2048,128]{1,0:T(8,128)(2,1)S(1)}, bf16[2048,128]{1,0:T(8,128)(2,1)S(1)}, u32[]{:S(2)}, u32[]{:S(2)}) collective-permute-start(bf16[2048,128]{1,0:T(8,128)(2,1)S(1)} %collective-permute-done.4.refs_0_), channel_id=1, source_target_pairs={{0,4},{4,0},{8,12},{12,8},{16,20},{20,16},{24,28},{28,24},{32,36},... | collective-permute-start | bytes 1572872 | tf_op jit(solution)/shard_map/ppermute | solution.py:29
  76.5 13.5 %collective-permute-start.29 = (bf16[2048,128]{1,0:T(8,128)(2,1)S(1)}, bf16[2048,128]{1,0:T(8,128)(2,1)S(1)}, u32[]{:S(2)}, u32[]{:S(2)}) collective-permute-start(bf16[2048,128]{1,0:T(8,128)(2,1)S(1)} %collective-permute-done.8.refs_2_), channel_id=1, source_target_pairs={{0,4},{4,0},{8,12},{12,8},{16,20},{20,16},{24,28},{28,24},{32,36},... | collective-permute-start | bytes 1572872 | tf_op jit(solution)/shard_map/ppermute | solution.py:29
  76.5 20.7 %collective-permute-start.5 = (bf16[2048,128]{1,0:T(8,128)(2,1)S(1)}, bf16[2048,128]{1,0:T(8,128)(2,1)S(1)}, u32[]{:S(2)}, u32[]{:S(2)}) collective-permute-start(bf16[2048,128]{1,0:T(8,128)(2,1)S(1)} %collective-permute-done.4.refs_0_), channel_id=1, source_target_pairs={{0,8},{4,12},{8,16},{12,20},{16,24},{20,28},{24,32},{28,36},{32,40... | collective-permute-start | bytes 1572872 | tf_op jit(solution)/shard_map/ppermute | solution.py:24
  86.0 12.1 %collective-permute-start.26 = (bf16[2048,128]{1,0:T(8,128)(2,1)S(1)}, bf16[2048,128]{1,0:T(8,128)(2,1)S(1)}, u32[]{:S(2)}, u32[]{:S(2)}) collective-permute-start(bf16[2048,128]{1,0:T(8,128)(2,1)S(1)} %collective-permute-done.18.refs_0_), channel_id=1, source_target_pairs={{0,4},{4,0},{8,12},{12,8},{16,20},{20,16},{24,28},{28,24},{32,36},... | collective-permute-start | bytes 1572872 | tf_op jit(solution)/shard_map/ppermute | solution.py:29
  87.8 13.5 %collective-permute-start.9 = (bf16[2048,128]{1,0:T(8,128)(2,1)S(1)}, bf16[2048,128]{1,0:T(8,128)(2,1)S(1)}, u32[]{:S(2)}, u32[]{:S(2)}) collective-permute-start(bf16[2048,128]{1,0:T(8,128)(2,1)S(1)} %collective-permute-done.8.refs_2_), channel_id=1, source_target_pairs={{0,56},{4,60},{8,0},{12,4},{16,8},{20,12},{24,16},{28,20},{32,24},... | collective-permute-start | bytes 1572872 | tf_op jit(solution)/shard_map/ppermute | solution.py:24
  88.7 13.9 %collective-permute-start.27 = (bf16[2048,128]{1,0:T(8,128)(2,1)S(1)}, bf16[2048,128]{1,0:T(8,128)(2,1)S(1)}, u32[]{:S(2)}, u32[]{:S(2)}) collective-permute-start(bf16[2048,128]{1,0:T(8,128)(2,1)S(1)} %collective-permute-done.21.refs_2_), channel_id=1, source_target_pairs={{0,4},{4,0},{8,12},{12,8},{16,20},{20,16},{24,28},{28,24},{32,36},... | collective-permute-start | bytes 1572872 | tf_op jit(solution)/shard_map/ppermute | solution.py:29
  90.1 18.4 %collective-permute-start.19 = (bf16[2048,128]{1,0:T(8,128)(2,1)S(1)}, bf16[2048,128]{1,0:T(8,128)(2,1)S(1)}, u32[]{:S(2)}, u32[]{:S(2)}) collective-permute-start(bf16[2048,128]{1,0:T(8,128)(2,1)S(1)} %collective-permute-done.18.refs_0_), channel_id=1, source_target_pairs={{0,8},{4,12},{8,16},{12,20},{16,24},{20,28},{24,32},{28,36},{32,40... | collective-permute-start | bytes 1572872 | tf_op jit(solution)/shard_map/ppermute | solution.py:24
  97.3 15.2 %collective-permute-start.22 = (bf16[2048,128]{1,0:T(8,128)(2,1)S(1)}, bf16[2048,128]{1,0:T(8,128)(2,1)S(1)}, u32[]{:S(2)}, u32[]{:S(2)}) collective-permute-start(bf16[2048,128]{1,0:T(8,128)(2,1)S(1)} %collective-permute-done.21.refs_2_), channel_id=1, source_target_pairs={{0,56},{4,60},{8,0},{12,4},{16,8},{20,12},{24,16},{28,20},{32,24},... | collective-permute-start | bytes 1572872 | tf_op jit(solution)/shard_map/ppermute | solution.py:24
  98.2 22.6 %collective-permute-start.12 = (bf16[1536,128]{1,0:T(8,128)(2,1)S(1)}, bf16[1536,128]{1,0:T(8,128)(2,1)S(1)}, u32[]{:S(2)}, u32[]{:S(2)}) collective-permute-start(bf16[1536,128]{1,0:T(8,128)(2,1)S(1)} %slice.18), channel_id=1, source_target_pairs={{0,8},{4,12},{8,16},{12,20},{16,24},{20,28},{24,32},{28,36},{32,40... | collective-permute-start | bytes 1179656 | tf_op jit(solution)/shard_map/ppermute | solution.py:24
  101.2 23.3 %collective-permute-start.24 = (bf16[2048,128]{1,0:T(8,128)(2,1)S(1)}, bf16[2048,128]{1,0:T(8,128)(2,1)S(1)}, u32[]{:S(2)}, u32[]{:S(2)}) collective-permute-start(bf16[2048,128]{1,0:T(8,128)(2,1)S(1)} %collective-permute-done.5.refs_0_), channel_id=1, source_target_pairs={{0,4},{4,0},{8,12},{12,8},{16,20},{20,16},{24,28},{28,24},{32,36},... | collective-permute-start | bytes 1572872 | tf_op jit(solution)/shard_map/ppermute | solution.py:29
  102.6 12.7 %collective-permute-start.10 = (bf16[512,128]{1,0:T(8,128)(2,1)S(1)}, bf16[512,128]{1,0:T(8,128)(2,1)S(1)}, u32[]{:S(2)}, u32[]{:S(2)}) collective-permute-start(bf16[512,128]{1,0:T(8,128)(2,1)S(1)} %slice.17), channel_id=1, source_target_pairs={{0,56},{4,60},{8,0},{12,4},{16,8},{20,12},{24,16},{28,20},{32,24},... | collective-permute-start | bytes 393224 | tf_op jit(solution)/shard_map/ppermute | solution.py:24
  108.5 11.2 %collective-permute-start.6 = (bf16[512,128]{1,0:T(8,128)(2,1)S(1)}, bf16[512,128]{1,0:T(8,128)(2,1)S(1)}, u32[]{:S(2)}, u32[]{:S(2)}) collective-permute-start(bf16[512,128]{1,0:T(8,128)(2,1)S(1)} %slice.16), channel_id=1, source_target_pairs={{0,8},{4,12},{8,16},{12,20},{16,24},{20,28},{24,32},{28,36},{32,40... | collective-permute-start | bytes 393224 | tf_op jit(solution)/shard_map/ppermute | solution.py:24
  112.5 10.5 %collective-permute-start.14 = (bf16[1536,128]{1,0:T(8,128)(2,1)S(1)}, bf16[1536,128]{1,0:T(8,128)(2,1)S(1)}, u32[]{:S(2)}, u32[]{:S(2)}) collective-permute-start(bf16[1536,128]{1,0:T(8,128)(2,1)S(1)} %slice.19), channel_id=1, source_target_pairs={{0,56},{4,60},{8,0},{12,4},{16,8},{20,12},{24,16},{28,20},{32,24},... | collective-permute-start | bytes 1179656 | tf_op jit(solution)/shard_map/ppermute | solution.py:24
  115.3 9.3 %collective-permute-start.25 = (bf16[2048,128]{1,0:T(8,128)(2,1)S(1)}, bf16[2048,128]{1,0:T(8,128)(2,1)S(1)}, u32[]{:S(2)}, u32[]{:S(2)}) collective-permute-start(bf16[2048,128]{1,0:T(8,128)(2,1)S(1)} %collective-permute-done.9.refs_2_), channel_id=1, source_target_pairs={{0,4},{4,0},{8,12},{12,8},{16,20},{20,16},{24,28},{28,24},{32,36},... | collective-permute-start | bytes 1572872 | tf_op jit(solution)/shard_map/ppermute | solution.py:29
  119.7 5.4 %collective-permute-start.20 = (bf16[2048,128]{1,0:T(8,128)(2,1)S(1)}, bf16[2048,128]{1,0:T(8,128)(2,1)S(1)}, u32[]{:S(2)}, u32[]{:S(2)}) collective-permute-start(bf16[2048,128]{1,0:T(8,128)(2,1)S(1)} %collective-permute-done.19.refs_0_), channel_id=1, source_target_pairs={{0,4},{4,0},{8,12},{12,8},{16,20},{20,16},{24,28},{28,24},{32,36},... | collective-permute-start | bytes 1572872 | tf_op jit(solution)/shard_map/ppermute | solution.py:29
  120.8 12.2 %collective-permute-start.23 = (bf16[2048,128]{1,0:T(8,128)(2,1)S(1)}, bf16[2048,128]{1,0:T(8,128)(2,1)S(1)}, u32[]{:S(2)}, u32[]{:S(2)}) collective-permute-start(bf16[2048,128]{1,0:T(8,128)(2,1)S(1)} %collective-permute-done.22.refs_2_), channel_id=1, source_target_pairs={{0,4},{4,0},{8,12},{12,8},{16,20},{20,16},{24,28},{28,24},{32,36},... | collective-permute-start | bytes 1572872 | tf_op jit(solution)/shard_map/ppermute | solution.py:29
  123.0 12.3 %collective-permute-start.13 = (bf16[1536,128]{1,0:T(8,128)(2,1)S(1)}, bf16[1536,128]{1,0:T(8,128)(2,1)S(1)}, u32[]{:S(2)}, u32[]{:S(2)}) collective-permute-start(bf16[1536,128]{1,0:T(8,128)(2,1)S(1)} %collective-permute-done.12.refs_0_), channel_id=1, source_target_pairs={{0,4},{4,0},{8,12},{12,8},{16,20},{20,16},{24,28},{28,24},{32,36},... | collective-permute-start | bytes 1179656 | tf_op jit(solution)/shard_map/ppermute | solution.py:29
  124.6 10.7 %collective-permute-start.15 = (bf16[1536,128]{1,0:T(8,128)(2,1)S(1)}, bf16[1536,128]{1,0:T(8,128)(2,1)S(1)}, u32[]{:S(2)}, u32[]{:S(2)}) collective-permute-start(bf16[1536,128]{1,0:T(8,128)(2,1)S(1)} %collective-permute-done.14.refs_1_), channel_id=1, source_target_pairs={{0,4},{4,0},{8,12},{12,8},{16,20},{20,16},{24,28},{28,24},{32,36},... | collective-permute-start | bytes 1179656 | tf_op jit(solution)/shard_map/ppermute | solution.py:29
  124.6 11.8 %collective-permute-start.11 = (bf16[512,128]{1,0:T(8,128)(2,1)S(1)}, bf16[512,128]{1,0:T(8,128)(2,1)S(1)}, u32[]{:S(2)}, u32[]{:S(2)}) collective-permute-start(bf16[512,128]{1,0:T(8,128)(2,1)S(1)} %collective-permute-done.10.refs_3_), channel_id=1, source_target_pairs={{0,4},{4,0},{8,12},{12,8},{16,20},{20,16},{24,28},{28,24},{32,36},... | collective-permute-start | bytes 393224 | tf_op jit(solution)/shard_map/ppermute | solution.py:29
  125.1 11.3 %collective-permute-start.7 = (bf16[512,128]{1,0:T(8,128)(2,1)S(1)}, bf16[512,128]{1,0:T(8,128)(2,1)S(1)}, u32[]{:S(2)}, u32[]{:S(2)}) collective-permute-start(bf16[512,128]{1,0:T(8,128)(2,1)S(1)} %collective-permute-done.6.refs_2_), channel_id=1, source_target_pairs={{0,4},{4,0},{8,12},{12,8},{16,20},{20,16},{24,28},{28,24},{32,36},... | collective-permute-start | bytes 393224 | tf_op jit(solution)/shard_map/ppermute | solution.py:29

commit v3 on v2

v3 whole, which is shorter than its diff:
```python
import functools
import jax
import jax.numpy as jnp
from jax import lax
from jax.experimental import pallas as pl
from jax.experimental.pallas import tpu as pltpu
from jax.sharding import PartitionSpec as P


mix_rate = 2.0
RING = "fsdp"
LARGE, SMALL = 56 << 20, 8 << 20
LAST = (2048, 1536, 512)
ANY = pl.BlockSpec(memory_space=pl.ANY)
VMEM = pl.BlockSpec(memory_space=pltpu.VMEM)


def paired(x, axis, bit):
    n = lax.axis_size(axis)
    return lax.ppermute(x, axis, [(i, i ^ bit) for i in range(n)])


def onward(x):
    n = lax.axis_size(RING)
    return lax.ppermute(x, RING, [(i, (i + (2 if i % 2 == 0 else n - 2)) % n) for i in range(n)])


def swapped(x):
    n = lax.axis_size(RING)
    return lax.ppermute(x, RING, [(i, i ^ 1) for i in range(n)])


def merge_kernel(place_own, wg, wu, low, hg, hu, unit, *refs):
    finals = refs[:2] if place_own else ()
    wbuf, lbuf, hbuf, tbuf, lsem, isem, osem = refs[len(finals):]
    rows, cols = wg.shape
    rank = hg.shape[0]
    lows = pltpu.make_async_copy(low, lbuf, lsem)
    loads = [
        [
            pltpu.make_async_copy(src, buf.at[k], isem.at[k, i])
            for i, (src, buf) in enumerate(((w, wbuf), (h, hbuf)))
        ]
        for k, (w, h) in enumerate(((wg, hg), (wu, hu)))
    ]
    stores = [
        [pltpu.make_async_copy(tbuf.at[k], unit.at[pl.ds(k * cols, cols), :], osem.at[k, 0])]
        for k in range(2)
    ]
    for k, final in enumerate(finals):
        mine = pl.multiple_of(lax.axis_index(RING) * rows, rows)
        stores[k].append(
            pltpu.make_async_copy(tbuf.at[k], final.at[:, pl.ds(mine, rows)], osem.at[k, 1])
        )
    lows.start()
    for group in loads:
        for cp in group:
            cp.start()
    lows.wait()
    for k in range(2):
        for cp in loads[k]:
            cp.wait()
        add = lax.dot_general(
            lbuf[pl.ds(k * rank, rank), :], hbuf[k], (((0,), (0,)), ((), ())),
            preferred_element_type=jnp.float32,
        )
        total = wbuf[k].astype(jnp.float32) + mix_rate * add
        tbuf[k] = total.astype(jnp.bfloat16).T
        for cp in stores[k]:
            cp.start()
    for group in stores:
        for cp in group:
            cp.wait()


def merged(wg, wu, low, hg, hu, grant, final=None):
    rows, cols = wg.shape
    rank = hg.shape[0]
    outs = (jax.ShapeDtypeStruct((2 * cols, rows), jnp.bfloat16),)
    if final:
        outs += (jax.ShapeDtypeStruct(final, jnp.bfloat16),) * 2
    return pl.pallas_call(
        functools.partial(merge_kernel, bool(final)),
        out_shape=outs,
        in_specs=[ANY] * 5,
        out_specs=(ANY,) * len(outs),
        scratch_shapes=[
            pltpu.VMEM((2, rows, cols), jnp.bfloat16),
            pltpu.VMEM((2 * rank, rows), jnp.bfloat16),
            pltpu.VMEM((2, rank, cols), jnp.bfloat16),
            pltpu.VMEM((2, cols, rows), jnp.bfloat16),
            pltpu.SemaphoreType.DMA,
            pltpu.SemaphoreType.DMA((2, 2)),
            pltpu.SemaphoreType.DMA((2, 2)),
        ],
        compiler_params=pltpu.CompilerParams(vmem_limit_bytes=grant),
        name="mix",
        cost_estimate=pl.CostEstimate(
            flops=4 * rows * cols * rank, bytes_accessed=8 * rows * cols, transcendentals=0
        ),
    )(wg, wu, low, hg, hu)


def place_kernel(units, *refs):
    n = len(units)
    outs = refs[n + 2:n + 4]
    sem = refs[n + 4]
    me = lax.axis_index(RING)
    chips = lax.axis_size(RING) // 2
    z, core = lax.div(me, 2), lax.rem(me, 2)
    copies = []
    for k, (hops, kind, swap, first) in enumerate(units):
        size, rows = refs[k].shape
        cols = outs[0].shape[0]
        via = 1 - core if swap else core
        chip = lax.rem(z + chips - hops * (1 - 2 * via), chips)
        owner = chip * 2 + (1 - via if kind else via)
        for w in range(2):
            lo, hi = max(first, w * cols), min(first + size, (w + 1) * cols)
            if lo < hi:
                copies.append(pltpu.make_async_copy(
                    refs[k].at[pl.ds(lo - first, hi - lo), :],
                    outs[w].at[
                        pl.ds(lo - w * cols, hi - lo), pl.ds(pl.multiple_of(owner * rows, rows), rows)
                    ],
                    sem.at[k, w],
                ))
    for cp in copies:
        cp.start()
    for cp in copies:
        cp.wait()


def place(outs, blocks, units):
    n = len(blocks)
    operands = (*blocks, *outs)
    out = jax.ShapeDtypeStruct(outs[0].shape, jnp.bfloat16)
    return pl.pallas_call(
        functools.partial(place_kernel, units),
        out_shape=(out, out),
        in_specs=[ANY] * len(operands),
        out_specs=(ANY, ANY),
        scratch_shapes=[pltpu.SemaphoreType.DMA((n, 2))],
        input_output_aliases={n: 0, n + 1: 1},
        compiler_params=pltpu.CompilerParams(vmem_limit_bytes=1 << 20),
        name="place",
        cost_estimate=pl.CostEstimate(
            flops=1_000_000 * n, bytes_accessed=4 * sum(b.size for b in blocks), transcendentals=0
        ),
    )(*operands)


def body(weight_gate, low_gate, high_gate, weight_up, low_up, high_up, norm_train, norm_step):
    rows, cols = weight_gate.shape
    chips = lax.axis_size(RING) // 2
    shape = (cols, rows * 2 * chips)
    far = chips // 2

    raw_gate, raw_up = onward(weight_gate), onward(weight_up)
    low = jnp.concatenate([low_gate.T, low_up.T], axis=0)
    raw_low = onward(low)
    held, other = {}, {}
    held["A", 0], *outs = merged(weight_gate, weight_up, low, high_gate, high_up, LARGE, shape)
    other["A", 0] = swapped(held["A", 0])
    held["A", 1], = merged(raw_gate, raw_up, raw_low, high_gate, high_up, SMALL)
    held["B", 1] = onward(other["A", 0])
    for h in range(2, far):
        held["A", h] = onward(held["A", h - 1])
        held["B", h] = onward(held["B", h - 1])
    first_row, row = {}, 0
    for part, size in zip("abc", LAST):
        kind = f"A4{part}"
        held[kind, far] = onward(held["A", far - 1][row:row + size])
        first_row[kind], row = row, row + size
    for kind, h in held:
        if h:
            other[kind, h] = swapped(held[kind, h])

    def put(outs, keys):
        blocks = [(other if s else held)[kind, h] for kind, h, s in keys]
        units = [(h, int(kind == "B"), s, first_row.get(kind, 0)) for kind, h, s in keys]
        return place(outs, blocks, units)

    outs = put(outs, [("A", 0, True), ("A", 1, False), ("A", 1, True)])
    for h in range(1, far):
        if h > 1:
            outs = put(outs, [("A", h, False), ("A", h, True)])
        outs = put(outs, [("B", h, False), ("B", h, True)])
    outs = put(outs, [("A4a", far, False)])
    outs = put(outs, [("A4a", far, True), ("A4b", far, False)])
    outs = put(outs, [("A4b", far, True), ("A4c", far, False)])
    outs = put(outs, [("A4c", far, True)])
    own = (norm_train + norm_step).astype(jnp.bfloat16)
    models = lax.axis_size("model")
    tile = (2 * chips, models * own.size)
    row = lax.broadcasted_iota(jnp.int32, tile, 0) == lax.axis_index(RING)
    lane = lax.broadcasted_iota(jnp.int32, tile, 1) // own.size == lax.axis_index("model")
    norm = jnp.where(row & lane, jnp.tile(own, models)[None], jnp.bfloat16(0))
    for axis, bit in NORM_STEPS:
        norm = norm + paired(norm, axis, bit)
    serve_norm = norm.reshape(-1)
    return outs[0], outs[1], serve_norm


NORM_STEPS = (
    (RING, 2), ("model", 1), (RING, 4),
    (RING, 8), ("model", 2), (RING, 1),
)


def solution(mesh):
    return jax.shard_map(
        body,
        mesh=mesh,
        in_specs=(
            P(("ens", "fsdp"), "model"),
            P(("ens", "fsdp"), None),
            P("ens", "model"),
            P(("ens", "fsdp"), "model"),
            P(("ens", "fsdp"), None),
            P("ens", "model"),
            P(("ens", "fsdp", "model")),
            P(("ens", "fsdp", "model")),
        ),
        out_specs=(P(("ens", "model"), None), P(("ens", "model"), None), P("ens")),
        check_vma=False,
    )
```

time: 138 us -> 238 us (1.72)
  Pallas kernels: 17 us -> 111 us
  waiting for transfers between devices: 61.3 us -> 76.1 us
  starting transfers between devices: 51.9 us -> 45.2 us
    pallas_call x9 -> x10, Pallas kernels: 11.2 us -> 107 us  [place(): pl.pallas_call(functools.partial(place_kernel, units), out_shape=(out, ou...]
    ppermute x18 -> x10, starting transfers between devices: 18.3 us -> 8.65 us  [swapped(): return lax.ppermute(x, RING, [(i, i ^ 1) for i in range(n)])]
    ppermute x6, waiting for transfers between devices: 18.1 us -> 26.6 us  [paired(): return lax.ppermute(x, axis, [(i, i ^ bit) for i in range(n)])]
    ppermute x18 -> x11, waiting for transfers between devices: 43.2 us -> 49.5 us  [onward(): lax.ppermute(x, RING, [(i, (i + (2 if i % 2 == 0 else n - 2)) % n) for i...]
    ppermute x18 -> x11, starting transfers between devices: 22.4 us -> 24.1 us  [onward(): lax.ppermute(x, RING, [(i, (i + (2 if i % 2 == 0 else n - 2)) % n) for i...]
    pallas_call x3 -> x2, Pallas kernels: 5.74 us -> 4.29 us  [merged(): pl.pallas_call(functools.partial(merge_kernel, bool(final)), out_shape=ou...]
  transfers between devices with their start and end apart: 42 -> 27, of which waited for: 12 -> 10; matrix products, arithmetic and copies ran while one was open for 1% -> 1% of each run, Pallas kernels for 12% -> 45%
where the time goes in v3:
time: 238 us
  Pallas kernels  111 us (47%)
  waiting for transfers between devices  76.1 us (32%)
  starting transfers between devices  45.2 us (19%)
  other arithmetic  2.85 us (1%)
    pallas_call x10, Pallas kernels, place(): pl.pallas_call(functools.partial(place_kernel, units), out_shape=(out, ou...  107 us
    ppermute x11, waiting for transfers between devices, onward(): lax.ppermute(x, RING, [(i, (i + (2 if i % 2 == 0 else n - 2)) % n) for i...  49.5 us
    ppermute x6, waiting for transfers between devices, paired(): return lax.ppermute(x, axis, [(i, i ^ bit) for i in range(n)])  26.6 us
    ppermute x11, starting transfers between devices, onward(): lax.ppermute(x, RING, [(i, (i + (2 if i % 2 == 0 else n - 2)) % n) for i...  24.1 us
    ppermute x6, starting transfers between devices, paired(): return lax.ppermute(x, axis, [(i, i ^ bit) for i in range(n)])  12.4 us
    ppermute x10, starting transfers between devices, swapped(): return lax.ppermute(x, RING, [(i, i ^ 1) for i in range(n)])  8.65 us
  transfers between devices with their start and end apart: 27, of which 10 were waited for; matrix products, arithmetic and copies ran while one was open for 1% of the time, Pallas kernels for 45%

profile of v3, /device:TPU:1, one launch (start us, length us, event | category | flops | bytes accessed | tf_op | source)
XLA Modules:
  0.0 238.0 jit_solution(13784089530654248035)
XLA Ops:
  0.6 1.3 pad_maximum_fusion.low
  1.9 2.9 %mix.3 = (bf16[4096,128]{1,0:T(8,128)(2,1)}, bf16[2048,2048]{1,0:T(8,128)(2,1)}, bf16[2048,2048]{1,0:T(8,128)(2,1)}) custom-call(bf16[128,2048]{1,0:T(8,128)(2,1)} %wg.1, bf16[128,2048]{1,0:T(8,128)(2,1)} %wu.1, bf16[64,128]{1,0:T(8,128)(2,1)} %pad_maximum_fusion.low, bf16[32,2048]{1,0:T(8,128)(2,1)} %hg.3, bf16[32,2048]{1,0:T(8,128)(2,1)} %hu.3), custom_call_target="tpu_custom_call" | custom-call | flops 33554432 | bytes 2097152 | tf_op jit(solution)/shard_map/mix/pallas_call | solution.py:82
  4.9 3.3 %collective-permute-start.11 = (bf16[4096,128]{1,0:T(8,128)(2,1)}, bf16[4096,128]{1,0:T(8,128)(2,1)S(1)}, u32[]{:S(2)}, u32[]{:S(2)}) collective-permute-start(bf16[4096,128]{1,0:T(8,128)(2,1)} %get-tuple-element.26), channel_id=1, source_target_pairs={{0,4},{4,0},{8,12},{12,8},{16,20},{20,16},{24,28},{28,24},{32,36},... | collective-permute-start | bytes 3145736 | tf_op jit(solution)/shard_map/ppermute | solution.py:30
  8.2 3.9 %collective-permute-start = (bf16[128,2048]{1,0:T(8,128)(2,1)}, bf16[128,2048]{1,0:T(8,128)(2,1)S(1)}, u32[]{:S(2)}, u32[]{:S(2)}) collective-permute-start(bf16[128,2048]{1,0:T(8,128)(2,1)} %wg.1), channel_id=1, source_target_pairs={{0,8},{4,60},{8,16},{12,4},{16,24},{20,12},{24,32},{28,20},{32,40}... | collective-permute-start | bytes 1572872 | tf_op jit(solution)/shard_map/ppermute | solution.py:25
  12.0 0.7 collective-permute-start.1
  12.8 1.8 collective-permute-start.12
  14.5 0.7 collective-permute-start.2
  15.3 20.1 %collective-permute-done.2.low = bf16[64,128]{1,0:T(8,128)(2,1)S(1)} collective-permute-done((bf16[64,128]{1,0:T(8,128)(2,1)}, bf16[64,128]{1,0:T(8,128)(2,1)S(1)}, u32[]{:S(2)}, u32[]{:S(2)}) %collective-permute-start.2) | collective-permute-done | bytes 16416 | tf_op jit(solution)/shard_map/ppermute | solution.py:25
  35.4 0.9 copy-done
  36.3 0.9 copy-done.1
  37.2 1.4 mix.2.refs_1_
  38.6 3.2 %collective-permute-start.3 = (bf16[4096,128]{1,0:T(8,128)(2,1)S(1)}, bf16[4096,128]{1,0:T(8,128)(2,1)}, u32[]{:S(2)}, u32[]{:S(2)}) collective-permute-start(bf16[4096,128]{1,0:T(8,128)(2,1)S(1)} %mix.2.refs_1_), channel_id=1, source_target_pairs={{0,8},{4,60},{8,16},{12,4},{16,24},{20,12},{24,32},{28,20},{32,40}... | collective-permute-start | bytes 3145736 | tf_op jit(solution)/shard_map/ppermute | solution.py:25
  41.9 11.6 %collective-permute-done.3.refs_0_ = bf16[4096,128]{1,0:T(8,128)(2,1)} collective-permute-done((bf16[4096,128]{1,0:T(8,128)(2,1)S(1)}, bf16[4096,128]{1,0:T(8,128)(2,1)}, u32[]{:S(2)}, u32[]{:S(2)}) %collective-permute-start.3) | collective-permute-done | bytes 1048608 | tf_op jit(solution)/shard_map/ppermute | solution.py:25
  53.5 3.2 %collective-permute-start.4 = (bf16[4096,128]{1,0:T(8,128)(2,1)}, bf16[4096,128]{1,0:T(8,128)(2,1)S(1)}, u32[]{:S(2)}, u32[]{:S(2)}) collective-permute-start(bf16[4096,128]{1,0:T(8,128)(2,1)} %collective-permute-done.3.refs_0_), channel_id=1, source_target_pairs={{0,8},{4,60},{8,16},{12,4},{16,24},{20,12},{24,32},{28,20},{32,40}... | collective-permute-start | bytes 3145736 | tf_op jit(solution)/shard_map/ppermute | solution.py:25
  56.8 0.7 add_convert_fusion
  57.6 0.5 collective-permute-start.18
  58.1 6.8 %collective-permute-done.13.refs_0_ = bf16[4096,128]{1,0:T(8,128)(2,1)} collective-permute-done((bf16[4096,128]{1,0:T(8,128)(2,1)}, bf16[4096,128]{1,0:T(8,128)(2,1)}, u32[]{:S(2)}, u32[]{:S(2)}) %collective-permute-start.13) | collective-permute-done | bytes 1048608 | tf_op jit(solution)/shard_map/ppermute | solution.py:25
  64.9 3.1 %collective-permute-start.14 = (bf16[4096,128]{1,0:T(8,128)(2,1)}, bf16[4096,128]{1,0:T(8,128)(2,1)S(1)}, u32[]{:S(2)}, u32[]{:S(2)}) collective-permute-start(bf16[4096,128]{1,0:T(8,128)(2,1)} %collective-permute-done.13.refs_0_), channel_id=1, source_target_pairs={{0,8},{4,60},{8,16},{12,4},{16,24},{20,12},{24,32},{28,20},{32,40}... | collective-permute-start | bytes 3145736 | tf_op jit(solution)/shard_map/ppermute | solution.py:25
  68.1 18.3 %collective-permute-done.21 = bf16[16,128]{1,0:T(8,128)(2,1)S(1)} collective-permute-done((bf16[16,128]{1,0:T(8,128)(2,1)S(1)}, bf16[16,128]{1,0:T(8,128)(2,1)S(1)}, u32[]{:S(2)}, u32[]{:S(2)}) %collective-permute-start.21) | collective-permute-done | bytes 4128 | tf_op jit(solution)/shard_map/ppermute | solution.py:20
  86.5 1.2 collective-permute-start.22
  87.7 1.5 collective-permute-done.22
  89.3 0.6 collective-permute-start.23
  90.0 2.8 %collective-permute-done.23 = bf16[16,128]{1,0:T(8,128)(2,1)S(1)} collective-permute-done((bf16[16,128]{1,0:T(8,128)(2,1)S(1)}, bf16[16,128]{1,0:T(8,128)(2,1)S(1)}, u32[]{:S(2)}, u32[]{:S(2)}) %collective-permute-start.23) | collective-permute-done | bytes 4128 | tf_op jit(solution)/shard_map/ppermute | solution.py:20
  92.7 3.6 %collective-permute-start.24 = (bf16[16,128]{1,0:T(8,128)(2,1)S(1)}, bf16[16,128]{1,0:T(8,128)(2,1)S(1)}, u32[]{:S(2)}, u32[]{:S(2)}) collective-permute-start(bf16[16,128]{1,0:T(8,128)(2,1)S(1)} %add.26), channel_id=1, source_target_pairs={{0,32},{4,36},{8,40},{12,44},{16,48},{20,52},{24,56},{28,60},{32,0... | collective-permute-start | bytes 12296 | tf_op jit(solution)/shard_map/ppermute | solution.py:20
  96.4 2.7 %collective-permute-done.24 = bf16[16,128]{1,0:T(8,128)(2,1)S(1)} collective-permute-done((bf16[16,128]{1,0:T(8,128)(2,1)S(1)}, bf16[16,128]{1,0:T(8,128)(2,1)S(1)}, u32[]{:S(2)}, u32[]{:S(2)}) %collective-permute-start.24) | collective-permute-done | bytes 4128 | tf_op jit(solution)/shard_map/ppermute | solution.py:20
  99.1 2.8 %collective-permute-start.25 = (bf16[16,128]{1,0:T(8,128)(2,1)S(1)}, bf16[16,128]{1,0:T(8,128)(2,1)S(1)}, u32[]{:S(2)}, u32[]{:S(2)}) collective-permute-start(bf16[16,128]{1,0:T(8,128)(2,1)S(1)} %add.27), channel_id=1, source_target_pairs={{0,2},{1,3},{2,0},{3,1},{4,6},{5,7},{6,4},{7,5},{8,10},{9,11},{10,... | collective-permute-start | bytes 12296 | tf_op jit(solution)/shard_map/ppermute | solution.py:20
  101.9 1.2 collective-permute-done.25
  103.1 4.2 %collective-permute-start.26 = (bf16[16,128]{1,0:T(8,128)(2,1)S(1)}, bf16[16,128]{1,0:T(8,128)(2,1)S(1)}, u32[]{:S(2)}, u32[]{:S(2)}) collective-permute-start(bf16[16,128]{1,0:T(8,128)(2,1)S(1)} %add.28), channel_id=1, source_target_pairs={{0,4},{4,0},{8,12},{12,8},{16,20},{20,16},{24,28},{28,24},{32,36},... | collective-permute-start | bytes 12296 | tf_op jit(solution)/shard_map/ppermute | solution.py:20
  107.3 4.2 %collective-permute-start.7 = (bf16[1536,128]{1,0:T(8,128)(2,1)S(1)}, bf16[1536,128]{1,0:T(8,128)(2,1)S(1)}, u32[]{:S(2)}, u32[]{:S(2)}) collective-permute-start(bf16[1536,128]{1,0:T(8,128)(2,1)S(1)} %slice.13), channel_id=1, source_target_pairs={{0,8},{4,60},{8,16},{12,4},{16,24},{20,12},{24,32},{28,20},{32,40}... | collective-permute-start | bytes 1179656 | tf_op jit(solution)/shard_map/ppermute | solution.py:25
  111.5 0.5 collective-permute-start.17
  112.0 0.8 collective-permute-start.5
  112.8 4.8 %collective-permute-done.5.refs_1_ = bf16[512,128]{1,0:T(8,128)(2,1)S(1)} collective-permute-done((bf16[512,128]{1,0:T(8,128)(2,1)S(1)}, bf16[512,128]{1,0:T(8,128)(2,1)S(1)}, u32[]{:S(2)}, u32[]{:S(2)}) %collective-permute-start.5) | collective-permute-done | bytes 131104 | tf_op jit(solution)/shard_map/ppermute | solution.py:25
  117.6 1.3 collective-permute-start.16
  119.0 2.4 collective-permute-start.9
  121.4 6.1 %collective-permute-done.9.refs_0_ = bf16[2048,128]{1,0:T(8,128)(2,1)S(1)} collective-permute-done((bf16[2048,128]{1,0:T(8,128)(2,1)S(1)}, bf16[2048,128]{1,0:T(8,128)(2,1)S(1)}, u32[]{:S(2)}, u32[]{:S(2)}) %collective-permute-start.9) | collective-permute-done | bytes 524320 | tf_op jit(solution)/shard_map/ppermute | solution.py:25
  127.5 2.5 %collective-permute-start.10 = (bf16[2048,128]{1,0:T(8,128)(2,1)S(1)}, bf16[2048,128]{1,0:T(8,128)(2,1)S(1)}, u32[]{:S(2)}, u32[]{:S(2)}) collective-permute-start(bf16[2048,128]{1,0:T(8,128)(2,1)S(1)} %collective-permute-done.9.refs_0_), channel_id=1, source_target_pairs={{0,4},{4,0},{8,12},{12,8},{16,20},{20,16},{24,28},{28,24},{32,36},... | collective-permute-start | bytes 1572872 | tf_op jit(solution)/shard_map/ppermute | solution.py:30
  130.0 0.5 collective-permute-start.6
  130.5 0.6 add_bitcast_fusion
  131.1 1.7 place.10
  132.8 32.9 %place.11 = (bf16[2048,2048]{1,0:T(8,128)(2,1)}, bf16[2048,2048]{1,0:T(8,128)(2,1)}) custom-call(bf16[4096,128]{1,0:T(8,128)(2,1)} %collective-permute-done.12.refs_0_, bf16[4096,128]{1,0:T(8,128)(2,1)S(1)} %collective-permute-done.19.refs_1_, bf16[2048,2048]{1,0:T(8,128)(2,1)} %get-tuple-element.29.refs_2_, ...), custom_call_target="tpu_custom_call", output_to_operand_aliasing={{0}: (2, {}), {1}: (3, {})} | custom-call | flops 2000000 | bytes 4194304 | tf_op jit(solution)/shard_map/place/pallas_call | solution.py:138
  165.7 32.9 %place.12 = (bf16[2048,2048]{1,0:T(8,128)(2,1)}, bf16[2048,2048]{1,0:T(8,128)(2,1)}) custom-call(bf16[4096,128]{1,0:T(8,128)(2,1)} %collective-permute-done.3.refs_0_, bf16[4096,128]{1,0:T(8,128)(2,1)S(1)} %collective-permute-done.18.refs_1_, bf16[2048,2048]{1,0:T(8,128)(2,1)} %get-tuple-element.31.refs_2_, ...), custom_call_target="tpu_custom_call", output_to_operand_aliasing={{0}: (2, {}), {1}: (3, {})} | custom-call | flops 2000000 | bytes 4194304 | tf_op jit(solution)/shard_map/place/pallas_call | solution.py:138
  198.7 32.9 %place.13 = (bf16[2048,2048]{1,0:T(8,128)(2,1)}, bf16[2048,2048]{1,0:T(8,128)(2,1)}) custom-call(bf16[4096,128]{1,0:T(8,128)(2,1)} %collective-permute-done.13.refs_0_, bf16[4096,128]{1,0:T(8,128)(2,1)S(1)} %collective-permute-done.17.refs_1_, bf16[2048,2048]{1,0:T(8,128)(2,1)} %get-tuple-element.33.refs_2_, ...), custom_call_target="tpu_custom_call", output_to_operand_aliasing={{0}: (2, {}), {1}: (3, {})} | custom-call | flops 2000000 | bytes 4194304 | tf_op jit(solution)/shard_map/place/pallas_call | solution.py:138
  231.6 1.4 place.14
  233.0 1.4 place.15
  234.4 0.8 place.16
  235.2 1.0 place.17
  236.2 0.8 place.18
  237.1 0.7 place.19
  (39 shorter events, 0.6 us)
Async XLA Ops:
  4.9 7.9 %collective-permute-start.11 = (bf16[4096,128]{1,0:T(8,128)(2,1)}, bf16[4096,128]{1,0:T(8,128)(2,1)S(1)}, u32[]{:S(2)}, u32[]{:S(2)}) collective-permute-start(bf16[4096,128]{1,0:T(8,128)(2,1)} %get-tuple-element.26), channel_id=1, source_target_pairs={{0,4},{4,0},{8,12},{12,8},{16,20},{20,16},{24,28},{28,24},{32,36},... | collective-permute-start | bytes 3145736 | tf_op jit(solution)/shard_map/ppermute | solution.py:30
  8.2 27.2 %collective-permute-start = (bf16[128,2048]{1,0:T(8,128)(2,1)}, bf16[128,2048]{1,0:T(8,128)(2,1)S(1)}, u32[]{:S(2)}, u32[]{:S(2)}) collective-permute-start(bf16[128,2048]{1,0:T(8,128)(2,1)} %wg.1), channel_id=1, source_target_pairs={{0,8},{4,60},{8,16},{12,4},{16,24},{20,12},{24,32},{28,20},{32,40}... | collective-permute-start | bytes 1572872 | tf_op jit(solution)/shard_map/ppermute | solution.py:25
  12.0 23.4 %collective-permute-start.1 = (bf16[128,2048]{1,0:T(8,128)(2,1)}, bf16[128,2048]{1,0:T(8,128)(2,1)S(1)}, u32[]{:S(2)}, u32[]{:S(2)}) collective-permute-start(bf16[128,2048]{1,0:T(8,128)(2,1)} %wu.1), channel_id=1, source_target_pairs={{0,8},{4,60},{8,16},{12,4},{16,24},{20,12},{24,32},{28,20},{32,40}... | collective-permute-start | bytes 1572872 | tf_op jit(solution)/shard_map/ppermute | solution.py:25
  12.8 29.0 %collective-permute-start.12 = (bf16[4096,128]{1,0:T(8,128)(2,1)S(1)}, bf16[4096,128]{1,0:T(8,128)(2,1)}, u32[]{:S(2)}, u32[]{:S(2)}) collective-permute-start(bf16[4096,128]{1,0:T(8,128)(2,1)S(1)} %collective-permute-done.11.refs_0_), channel_id=1, source_target_pairs={{0,8},{4,60},{8,16},{12,4},{16,24},{20,12},{24,32},{28,20},{32,40}... | collective-permute-start | bytes 3145736 | tf_op jit(solution)/shard_map/ppermute | solution.py:25
  14.5 20.9 %collective-permute-start.2 = (bf16[64,128]{1,0:T(8,128)(2,1)}, bf16[64,128]{1,0:T(8,128)(2,1)S(1)}, u32[]{:S(2)}, u32[]{:S(2)}) collective-permute-start(bf16[64,128]{1,0:T(8,128)(2,1)} %pad_maximum_fusion.low), channel_id=1, source_target_pairs={{0,8},{4,60},{8,16},{12,4},{16,24},{20,12},{24,32},{28,20},{32,40}... | collective-permute-start | bytes 49160 | tf_op jit(solution)/shard_map/ppermute | solution.py:25
  35.4 0.9 copy-start
  36.3 0.9 copy-start.1
  38.6 14.9 %collective-permute-start.3 = (bf16[4096,128]{1,0:T(8,128)(2,1)S(1)}, bf16[4096,128]{1,0:T(8,128)(2,1)}, u32[]{:S(2)}, u32[]{:S(2)}) collective-permute-start(bf16[4096,128]{1,0:T(8,128)(2,1)S(1)} %mix.2.refs_1_), channel_id=1, source_target_pairs={{0,8},{4,60},{8,16},{12,4},{16,24},{20,12},{24,32},{28,20},{32,40}... | collective-permute-start | bytes 3145736 | tf_op jit(solution)/shard_map/ppermute | solution.py:25
  41.8 23.1 %collective-permute-start.13 = (bf16[4096,128]{1,0:T(8,128)(2,1)}, bf16[4096,128]{1,0:T(8,128)(2,1)}, u32[]{:S(2)}, u32[]{:S(2)}) collective-permute-start(bf16[4096,128]{1,0:T(8,128)(2,1)} %collective-permute-done.12.refs_0_), channel_id=1, source_target_pairs={{0,8},{4,60},{8,16},{12,4},{16,24},{20,12},{24,32},{28,20},{32,40}... | collective-permute-start | bytes 3145736 | tf_op jit(solution)/shard_map/ppermute | solution.py:25
  53.5 53.7 %collective-permute-start.4 = (bf16[4096,128]{1,0:T(8,128)(2,1)}, bf16[4096,128]{1,0:T(8,128)(2,1)S(1)}, u32[]{:S(2)}, u32[]{:S(2)}) collective-permute-start(bf16[4096,128]{1,0:T(8,128)(2,1)} %collective-permute-done.3.refs_0_), channel_id=1, source_target_pairs={{0,8},{4,60},{8,16},{12,4},{16,24},{20,12},{24,32},{28,20},{32,40}... | collective-permute-start | bytes 3145736 | tf_op jit(solution)/shard_map/ppermute | solution.py:25
  57.5 54.0 %collective-permute-start.20 = (bf16[4096,128]{1,0:T(8,128)(2,1)S(1)}, bf16[4096,128]{1,0:T(8,128)(2,1)S(1)}, u32[]{:S(2)}, u32[]{:S(2)}) collective-permute-start(bf16[4096,128]{1,0:T(8,128)(2,1)S(1)} %mix.2.refs_1_), channel_id=1, source_target_pairs={{0,4},{4,0},{8,12},{12,8},{16,20},{20,16},{24,28},{28,24},{32,36},... | collective-permute-start | bytes 3145736 | tf_op jit(solution)/shard_map/ppermute | solution.py:30
  57.6 54.5 %collective-permute-start.18 = (bf16[4096,128]{1,0:T(8,128)(2,1)}, bf16[4096,128]{1,0:T(8,128)(2,1)S(1)}, u32[]{:S(2)}, u32[]{:S(2)}) collective-permute-start(bf16[4096,128]{1,0:T(8,128)(2,1)} %collective-permute-done.3.refs_0_), channel_id=1, source_target_pairs={{0,4},{4,0},{8,12},{12,8},{16,20},{20,16},{24,28},{28,24},{32,36},... | collective-permute-start | bytes 3145736 | tf_op jit(solution)/shard_map/ppermute | solution.py:30
  64.9 54.1 %collective-permute-start.14 = (bf16[4096,128]{1,0:T(8,128)(2,1)}, bf16[4096,128]{1,0:T(8,128)(2,1)S(1)}, u32[]{:S(2)}, u32[]{:S(2)}) collective-permute-start(bf16[4096,128]{1,0:T(8,128)(2,1)} %collective-permute-done.13.refs_0_), channel_id=1, source_target_pairs={{0,8},{4,60},{8,16},{12,4},{16,24},{20,12},{24,32},{28,20},{32,40}... | collective-permute-start | bytes 3145736 | tf_op jit(solution)/shard_map/ppermute | solution.py:25
  68.1 18.3 %collective-permute-start.21 = (bf16[16,128]{1,0:T(8,128)(2,1)S(1)}, bf16[16,128]{1,0:T(8,128)(2,1)S(1)}, u32[]{:S(2)}, u32[]{:S(2)}) collective-permute-start(bf16[16,128]{1,0:T(8,128)(2,1)S(1)} %fusion.1), channel_id=1, source_target_pairs={{0,8},{4,12},{8,0},{12,4},{16,24},{20,28},{24,16},{28,20},{32,40},... | collective-permute-start | bytes 12296 | tf_op jit(solution)/shard_map/ppermute | solution.py:20
  86.5 2.8 %collective-permute-start.22 = (bf16[16,128]{1,0:T(8,128)(2,1)S(1)}, bf16[16,128]{1,0:T(8,128)(2,1)S(1)}, u32[]{:S(2)}, u32[]{:S(2)}) collective-permute-start(bf16[16,128]{1,0:T(8,128)(2,1)S(1)} %fusion.2), channel_id=1, source_target_pairs={{0,1},{1,0},{2,3},{3,2},{4,5},{5,4},{6,7},{7,6},{8,9},{9,8},{10,11... | collective-permute-start | bytes 12296 | tf_op jit(solution)/shard_map/ppermute | solution.py:20
  89.3 3.4 %collective-permute-start.23 = (bf16[16,128]{1,0:T(8,128)(2,1)S(1)}, bf16[16,128]{1,0:T(8,128)(2,1)S(1)}, u32[]{:S(2)}, u32[]{:S(2)}) collective-permute-start(bf16[16,128]{1,0:T(8,128)(2,1)S(1)} %fusion.3), channel_id=1, source_target_pairs={{0,16},{4,20},{8,24},{12,28},{16,0},{20,4},{24,8},{28,12},{32,48},... | collective-permute-start | bytes 12296 | tf_op jit(solution)/shard_map/ppermute | solution.py:20
  92.7 6.4 %collective-permute-start.24 = (bf16[16,128]{1,0:T(8,128)(2,1)S(1)}, bf16[16,128]{1,0:T(8,128)(2,1)S(1)}, u32[]{:S(2)}, u32[]{:S(2)}) collective-permute-start(bf16[16,128]{1,0:T(8,128)(2,1)S(1)} %add.26), channel_id=1, source_target_pairs={{0,32},{4,36},{8,40},{12,44},{16,48},{20,52},{24,56},{28,60},{32,0... | collective-permute-start | bytes 12296 | tf_op jit(solution)/shard_map/ppermute | solution.py:20
  99.1 4.0 %collective-permute-start.25 = (bf16[16,128]{1,0:T(8,128)(2,1)S(1)}, bf16[16,128]{1,0:T(8,128)(2,1)S(1)}, u32[]{:S(2)}, u32[]{:S(2)}) collective-permute-start(bf16[16,128]{1,0:T(8,128)(2,1)S(1)} %add.27), channel_id=1, source_target_pairs={{0,2},{1,3},{2,0},{3,1},{4,6},{5,7},{6,4},{7,5},{8,10},{9,11},{10,... | collective-permute-start | bytes 12296 | tf_op jit(solution)/shard_map/ppermute | solution.py:20
  103.1 8.4 %collective-permute-start.26 = (bf16[16,128]{1,0:T(8,128)(2,1)S(1)}, bf16[16,128]{1,0:T(8,128)(2,1)S(1)}, u32[]{:S(2)}, u32[]{:S(2)}) collective-permute-start(bf16[16,128]{1,0:T(8,128)(2,1)S(1)} %add.28), channel_id=1, source_target_pairs={{0,4},{4,0},{8,12},{12,8},{16,20},{20,16},{24,28},{28,24},{32,36},... | collective-permute-start | bytes 12296 | tf_op jit(solution)/shard_map/ppermute | solution.py:20
  107.3 11.7 %collective-permute-start.7 = (bf16[1536,128]{1,0:T(8,128)(2,1)S(1)}, bf16[1536,128]{1,0:T(8,128)(2,1)S(1)}, u32[]{:S(2)}, u32[]{:S(2)}) collective-permute-start(bf16[1536,128]{1,0:T(8,128)(2,1)S(1)} %slice.13), channel_id=1, source_target_pairs={{0,8},{4,60},{8,16},{12,4},{16,24},{20,12},{24,32},{28,20},{32,40}... | collective-permute-start | bytes 1179656 | tf_op jit(solution)/shard_map/ppermute | solution.py:25
  111.5 18.5 %collective-permute-start.19 = (bf16[4096,128]{1,0:T(8,128)(2,1)}, bf16[4096,128]{1,0:T(8,128)(2,1)S(1)}, u32[]{:S(2)}, u32[]{:S(2)}) collective-permute-start(bf16[4096,128]{1,0:T(8,128)(2,1)} %collective-permute-done.12.refs_0_), channel_id=1, source_target_pairs={{0,4},{4,0},{8,12},{12,8},{16,20},{20,16},{24,28},{28,24},{32,36},... | collective-permute-start | bytes 3145736 | tf_op jit(solution)/shard_map/ppermute | solution.py:30
  111.5 18.5 %collective-permute-start.17 = (bf16[4096,128]{1,0:T(8,128)(2,1)}, bf16[4096,128]{1,0:T(8,128)(2,1)S(1)}, u32[]{:S(2)}, u32[]{:S(2)}) collective-permute-start(bf16[4096,128]{1,0:T(8,128)(2,1)} %collective-permute-done.13.refs_0_), channel_id=1, source_target_pairs={{0,4},{4,0},{8,12},{12,8},{16,20},{20,16},{24,28},{28,24},{32,36},... | collective-permute-start | bytes 3145736 | tf_op jit(solution)/shard_map/ppermute | solution.py:30
  112.0 5.6 %collective-permute-start.5 = (bf16[512,128]{1,0:T(8,128)(2,1)S(1)}, bf16[512,128]{1,0:T(8,128)(2,1)S(1)}, u32[]{:S(2)}, u32[]{:S(2)}) collective-permute-start(bf16[512,128]{1,0:T(8,128)(2,1)S(1)} %slice.12), channel_id=1, source_target_pairs={{0,8},{4,60},{8,16},{12,4},{16,24},{20,12},{24,32},{28,20},{32,40}... | collective-permute-start | bytes 393224 | tf_op jit(solution)/shard_map/ppermute | solution.py:25
  117.6 114.0 %collective-permute-start.16 = (bf16[4096,128]{1,0:T(8,128)(2,1)S(1)}, bf16[4096,128]{1,0:T(8,128)(2,1)S(1)}, u32[]{:S(2)}, u32[]{:S(2)}) collective-permute-start(bf16[4096,128]{1,0:T(8,128)(2,1)S(1)} %collective-permute-done.4.refs_0_), channel_id=1, source_target_pairs={{0,4},{4,0},{8,12},{12,8},{16,20},{20,16},{24,28},{28,24},{32,36},... | collective-permute-start | bytes 3145736 | tf_op jit(solution)/shard_map/ppermute | solution.py:30
  118.9 114.1 %collective-permute-start.15 = (bf16[4096,128]{1,0:T(8,128)(2,1)S(1)}, bf16[4096,128]{1,0:T(8,128)(2,1)S(1)}, u32[]{:S(2)}, u32[]{:S(2)}) collective-permute-start(bf16[4096,128]{1,0:T(8,128)(2,1)S(1)} %collective-permute-done.14.refs_0_), channel_id=1, source_target_pairs={{0,4},{4,0},{8,12},{12,8},{16,20},{20,16},{24,28},{28,24},{32,36},... | collective-permute-start | bytes 3145736 | tf_op jit(solution)/shard_map/ppermute | solution.py:30
  119.0 8.5 %collective-permute-start.9 = (bf16[2048,128]{1,0:T(8,128)(2,1)S(1)}, bf16[2048,128]{1,0:T(8,128)(2,1)S(1)}, u32[]{:S(2)}, u32[]{:S(2)}) collective-permute-start(bf16[2048,128]{1,0:T(8,128)(2,1)S(1)} %slice.14), channel_id=1, source_target_pairs={{0,8},{4,60},{8,16},{12,4},{16,24},{20,12},{24,32},{28,20},{32,40}... | collective-permute-start | bytes 1572872 | tf_op jit(solution)/shard_map/ppermute | solution.py:25
  127.5 107.7 %collective-permute-start.10 = (bf16[2048,128]{1,0:T(8,128)(2,1)S(1)}, bf16[2048,128]{1,0:T(8,128)(2,1)S(1)}, u32[]{:S(2)}, u32[]{:S(2)}) collective-permute-start(bf16[2048,128]{1,0:T(8,128)(2,1)S(1)} %collective-permute-done.9.refs_0_), channel_id=1, source_target_pairs={{0,4},{4,0},{8,12},{12,8},{16,20},{20,16},{24,28},{28,24},{32,36},... | collective-permute-start | bytes 1572872 | tf_op jit(solution)/shard_map/ppermute | solution.py:30
  130.0 106.2 %collective-permute-start.8 = (bf16[1536,128]{1,0:T(8,128)(2,1)S(1)}, bf16[1536,128]{1,0:T(8,128)(2,1)S(1)}, u32[]{:S(2)}, u32[]{:S(2)}) collective-permute-start(bf16[1536,128]{1,0:T(8,128)(2,1)S(1)} %collective-permute-done.7.refs_1_), channel_id=1, source_target_pairs={{0,4},{4,0},{8,12},{12,8},{16,20},{20,16},{24,28},{28,24},{32,36},... | collective-permute-start | bytes 1179656 | tf_op jit(solution)/shard_map/ppermute | solution.py:30
  130.0 107.1 %collective-permute-start.6 = (bf16[512,128]{1,0:T(8,128)(2,1)S(1)}, bf16[512,128]{1,0:T(8,128)(2,1)S(1)}, u32[]{:S(2)}, u32[]{:S(2)}) collective-permute-start(bf16[512,128]{1,0:T(8,128)(2,1)S(1)} %collective-permute-done.5.refs_1_), channel_id=1, source_target_pairs={{0,4},{4,0},{8,12},{12,8},{16,20},{20,16},{24,28},{28,24},{32,36},... | collective-permute-start | bytes 393224 | tf_op jit(solution)/shard_map/ppermute | solution.py:30

commit v4 on v3

--- a/solution.py
+++ b/solution.py
@@ -22,7 +22,7 @@
 
 def onward(x):
     n = lax.axis_size(RING)
-    return lax.ppermute(x, RING, [(i, (i + (2 if i % 2 == 0 else n - 2)) % n) for i in range(n)])
+    return lax.ppermute(x, RING, [(i, (i + (2 if i % 2 == 1 else n - 2)) % n) for i in range(n)])
 
 
 def swapped(x):
@@ -113,7 +113,7 @@
         size, rows = refs[k].shape
         cols = outs[0].shape[0]
         via = 1 - core if swap else core
-        chip = lax.rem(z + chips - hops * (1 - 2 * via), chips)
+        chip = lax.rem(z + chips - hops * (2 * via - 1), chips)
         owner = chip * 2 + (1 - via if kind else via)
         for w in range(2):
             lo, hi = max(first, w * cols), min(first + size, (w + 1) * cols)
@@ -138,11 +138,13 @@
     return pl.pallas_call(
         functools.partial(place_kernel, units),
         out_shape=(out, out),
-        in_specs=[ANY] * len(operands),
+        in_specs=[VMEM] * n + [ANY] * 2,
         out_specs=(ANY, ANY),
         scratch_shapes=[pltpu.SemaphoreType.DMA((n, 2))],
         input_output_aliases={n: 0, n + 1: 1},
-        compiler_params=pltpu.CompilerParams(vmem_limit_bytes=1 << 20),
+        compiler_params=pltpu.CompilerParams(
+            vmem_limit_bytes=(1 << 20) + 2 * sum(b.size for b in blocks)
+        ),
         name="place",
         cost_estimate=pl.CostEstimate(
             flops=1_000_000 * n, bytes_accessed=4 * sum(b.size for b in blocks), transcendentals=0
@@ -203,8 +205,8 @@
 
 
 NORM_STEPS = (
-    (RING, 2), ("model", 1), (RING, 4),
-    (RING, 8), ("model", 2), (RING, 1),
+    ("model", 1), ("model", 2), (RING, 2),
+    (RING, 4), (RING, 8), (RING, 1),
 )
 
 

time: 238 us -> 137 us (0.58)
  Pallas kernels: 111 us -> 19.8 us
  starting transfers between devices: 45.2 us -> 31.8 us
  waiting for transfers between devices: 76.1 us -> 79 us
    pallas_call x10, Pallas kernels: 107 us -> 15.5 us  [place(): pl.pallas_call(functools.partial(place_kernel, units), out_shape=(out, ou...]
    ppermute x11, starting transfers between devices: 24.1 us -> 6 us  [onward(): lax.ppermute(x, RING, [(i, (i + (2 if i % 2 == 1 else n - 2)) % n) for i...]
    ppermute x11, waiting for transfers between devices: 49.5 us -> 58 us  [onward(): lax.ppermute(x, RING, [(i, (i + (2 if i % 2 == 1 else n - 2)) % n) for i...]
    ppermute x6, waiting for transfers between devices: 26.6 us -> 20.1 us  [paired(): return lax.ppermute(x, axis, [(i, i ^ bit) for i in range(n)])]
    ppermute x6, starting transfers between devices: 12.4 us -> 15.3 us  [paired(): return lax.ppermute(x, axis, [(i, i ^ bit) for i in range(n)])]
  transfers between devices with their start and end apart: 27 -> 27, of which waited for: 10 -> 12; matrix products, arithmetic and copies ran while one was open for 1% -> 1% of each run, Pallas kernels for 45% -> 12%
where the time goes in v4:
time: 137 us; the launch traced here: 136 us
  waiting for transfers between devices  79 us (58%)
  starting transfers between devices  31.8 us (23%)
  Pallas kernels  19.8 us (14%)
  other arithmetic  2.85 us (2%)
  local copies, waits for them, and re-layouts  1.97 us (1%)
    ppermute x11, waiting for transfers between devices, onward(): lax.ppermute(x, RING, [(i, (i + (2 if i % 2 == 1 else n - 2)) % n) for i...  58 us
    ppermute x6, waiting for transfers between devices, paired(): return lax.ppermute(x, axis, [(i, i ^ bit) for i in range(n)])  20.1 us
    pallas_call x10, Pallas kernels, place(): pl.pallas_call(functools.partial(place_kernel, units), out_shape=(out, ou...  15.5 us
    ppermute x6, starting transfers between devices, paired(): return lax.ppermute(x, axis, [(i, i ^ bit) for i in range(n)])  15.3 us
    ppermute x10, starting transfers between devices, swapped(): return lax.ppermute(x, RING, [(i, i ^ 1) for i in range(n)])  10.5 us
    ppermute x11, starting transfers between devices, onward(): lax.ppermute(x, RING, [(i, (i + (2 if i % 2 == 1 else n - 2)) % n) for i...  6 us
    pallas_call x2, Pallas kernels, merged(): pl.pallas_call(functools.partial(merge_kernel, bool(final)), out_shape=ou...  4.3 us
  transfers between devices with their start and end apart: 27, of which 12 were waited for; matrix products, arithmetic and copies ran while one was open for 1% of the time, Pallas kernels for 12%

profile of v4, /device:TPU:1, one launch (start us, length us, event | category | flops | bytes accessed | tf_op | source)
XLA Modules:
  0.0 136.5 jit_solution(6265145627799192174)
XLA Ops:
  0.6 1.3 pad_maximum_fusion.low
  1.9 2.9 %mix.3 = (bf16[4096,128]{1,0:T(8,128)(2,1)}, bf16[2048,2048]{1,0:T(8,128)(2,1)}, bf16[2048,2048]{1,0:T(8,128)(2,1)}) custom-call(bf16[128,2048]{1,0:T(8,128)(2,1)} %wg.1, bf16[128,2048]{1,0:T(8,128)(2,1)} %wu.1, bf16[64,128]{1,0:T(8,128)(2,1)} %pad_maximum_fusion.low, bf16[32,2048]{1,0:T(8,128)(2,1)} %hg.3, bf16[32,2048]{1,0:T(8,128)(2,1)} %hu.3), custom_call_target="tpu_custom_call" | custom-call | flops 33554432 | bytes 2097152 | tf_op jit(solution)/shard_map/mix/pallas_call | solution.py:82
  4.9 3.3 %collective-permute-start.11 = (bf16[4096,128]{1,0:T(8,128)(2,1)}, bf16[4096,128]{1,0:T(8,128)(2,1)S(1)}, u32[]{:S(2)}, u32[]{:S(2)}) collective-permute-start(bf16[4096,128]{1,0:T(8,128)(2,1)} %get-tuple-element.26), channel_id=1, source_target_pairs={{0,4},{4,0},{8,12},{12,8},{16,20},{20,16},{24,28},{28,24},{32,36},... | collective-permute-start | bytes 3145736 | tf_op jit(solution)/shard_map/ppermute | solution.py:30
  8.2 1.6 %collective-permute-start.1 = (bf16[128,2048]{1,0:T(8,128)(2,1)}, bf16[128,2048]{1,0:T(8,128)(2,1)S(1)}, u32[]{:S(2)}, u32[]{:S(2)}) collective-permute-start(bf16[128,2048]{1,0:T(8,128)(2,1)} %wu.1), channel_id=1, source_target_pairs={{0,56},{4,12},{8,0},{12,20},{16,8},{20,28},{24,16},{28,36},{32,24}... | collective-permute-start | bytes 1572872 | tf_op jit(solution)/shard_map/ppermute | solution.py:25
  9.7 0.9 collective-permute-done.11.refs_0_
  10.7 0.7 collective-permute-start.12
  11.4 2.8 %collective-permute-start.2 = (bf16[64,128]{1,0:T(8,128)(2,1)}, bf16[64,128]{1,0:T(8,128)(2,1)S(1)}, u32[]{:S(2)}, u32[]{:S(2)}) collective-permute-start(bf16[64,128]{1,0:T(8,128)(2,1)} %pad_maximum_fusion.low), channel_id=1, source_target_pairs={{0,56},{4,12},{8,0},{12,20},{16,8},{20,28},{24,16},{28,36},{32,24}... | collective-permute-start | bytes 49160 | tf_op jit(solution)/shard_map/ppermute | solution.py:25
  14.2 21.6 %collective-permute-done.2.low = bf16[64,128]{1,0:T(8,128)(2,1)S(1)} collective-permute-done((bf16[64,128]{1,0:T(8,128)(2,1)}, bf16[64,128]{1,0:T(8,128)(2,1)S(1)}, u32[]{:S(2)}, u32[]{:S(2)}) %collective-permute-start.2) | collective-permute-done | bytes 16416 | tf_op jit(solution)/shard_map/ppermute | solution.py:25
  35.9 0.9 copy-done
  36.8 0.9 copy-done.1
  37.7 1.4 %mix.2.refs_1_ = bf16[4096,128]{1,0:T(8,128)(2,1)S(1)} custom-call(bf16[128,2048]{1,0:T(8,128)(2,1)S(1)} %collective-permute-done.wg, bf16[128,2048]{1,0:T(8,128)(2,1)S(1)} %collective-permute-done.1.wu, bf16[64,128]{1,0:T(8,128)(2,1)S(1)} %collective-permute-done.2.low, bf16[32,2048]{1,0:T(8,128)(2,1)S(1)} %copy-done, bf16[32,2048]{1,0:T(8,128)(2,1)S(1)} %copy-done.1), custom_call_target="tpu_custom_call" | custom-call | flops 33554432 | bytes 2097152 | tf_op jit(solution)/shard_map/mix/pallas_call | solution.py:82
  39.0 0.1 collective-permute-start.3
  39.2 14.8 %collective-permute-done.3.refs_0_ = bf16[4096,128]{1,0:T(8,128)(2,1)} collective-permute-done((bf16[4096,128]{1,0:T(8,128)(2,1)S(1)}, bf16[4096,128]{1,0:T(8,128)(2,1)}, u32[]{:S(2)}, u32[]{:S(2)}) %collective-permute-start.3) | collective-permute-done | bytes 1048608 | tf_op jit(solution)/shard_map/ppermute | solution.py:25
  54.1 0.7 add_convert_fusion
  54.8 0.1 broadcast_in_dim.14
  54.9 5.3 %collective-permute-start.20 = (bf16[4096,128]{1,0:T(8,128)(2,1)S(1)}, bf16[4096,128]{1,0:T(8,128)(2,1)S(1)}, u32[]{:S(2)}, u32[]{:S(2)}) collective-permute-start(bf16[4096,128]{1,0:T(8,128)(2,1)S(1)} %mix.2.refs_1_), channel_id=1, source_target_pairs={{0,4},{4,0},{8,12},{12,8},{16,20},{20,16},{24,28},{28,24},{32,36},... | collective-permute-start | bytes 3145736 | tf_op jit(solution)/shard_map/ppermute | solution.py:30
  60.2 0.1 collective-permute-start.18
  60.3 5.0 %collective-permute-done.13.refs_0_ = bf16[4096,128]{1,0:T(8,128)(2,1)} collective-permute-done((bf16[4096,128]{1,0:T(8,128)(2,1)}, bf16[4096,128]{1,0:T(8,128)(2,1)}, u32[]{:S(2)}, u32[]{:S(2)}) %collective-permute-start.13) | collective-permute-done | bytes 1048608 | tf_op jit(solution)/shard_map/ppermute | solution.py:25
  65.4 1.2 collective-permute-start.21
  66.6 1.5 %collective-permute-done.21 = bf16[16,128]{1,0:T(8,128)(2,1)S(1)} collective-permute-done((bf16[16,128]{1,0:T(8,128)(2,1)S(1)}, bf16[16,128]{1,0:T(8,128)(2,1)S(1)}, u32[]{:S(2)}, u32[]{:S(2)}) %collective-permute-start.21) | collective-permute-done | bytes 4128 | tf_op jit(solution)/shard_map/ppermute | solution.py:20
  68.3 2.8 %collective-permute-start.22 = (bf16[16,128]{1,0:T(8,128)(2,1)S(1)}, bf16[16,128]{1,0:T(8,128)(2,1)S(1)}, u32[]{:S(2)}, u32[]{:S(2)}) collective-permute-start(bf16[16,128]{1,0:T(8,128)(2,1)S(1)} %fusion.2), channel_id=1, source_target_pairs={{0,2},{1,3},{2,0},{3,1},{4,6},{5,7},{6,4},{7,5},{8,10},{9,11},{10,... | collective-permute-start | bytes 12296 | tf_op jit(solution)/shard_map/ppermute | solution.py:20
  71.0 1.2 collective-permute-done.22
  72.4 12.4 %collective-permute-done.23 = bf16[16,128]{1,0:T(8,128)(2,1)S(1)} collective-permute-done((bf16[16,128]{1,0:T(8,128)(2,1)S(1)}, bf16[16,128]{1,0:T(8,128)(2,1)S(1)}, u32[]{:S(2)}, u32[]{:S(2)}) %collective-permute-start.23) | collective-permute-done | bytes 4128 | tf_op jit(solution)/shard_map/ppermute | solution.py:20
  84.7 1.4 %collective-permute-start.24 = (bf16[16,128]{1,0:T(8,128)(2,1)S(1)}, bf16[16,128]{1,0:T(8,128)(2,1)S(1)}, u32[]{:S(2)}, u32[]{:S(2)}) collective-permute-start(bf16[16,128]{1,0:T(8,128)(2,1)S(1)} %add.26), channel_id=1, source_target_pairs={{0,16},{4,20},{8,24},{12,28},{16,0},{20,4},{24,8},{28,12},{32,48},... | collective-permute-start | bytes 12296 | tf_op jit(solution)/shard_map/ppermute | solution.py:20
  86.2 1.9 %collective-permute-done.24 = bf16[16,128]{1,0:T(8,128)(2,1)S(1)} collective-permute-done((bf16[16,128]{1,0:T(8,128)(2,1)S(1)}, bf16[16,128]{1,0:T(8,128)(2,1)S(1)}, u32[]{:S(2)}, u32[]{:S(2)}) %collective-permute-start.24) | collective-permute-done | bytes 4128 | tf_op jit(solution)/shard_map/ppermute | solution.py:20
  88.1 4.0 %collective-permute-start.25 = (bf16[16,128]{1,0:T(8,128)(2,1)S(1)}, bf16[16,128]{1,0:T(8,128)(2,1)S(1)}, u32[]{:S(2)}, u32[]{:S(2)}) collective-permute-start(bf16[16,128]{1,0:T(8,128)(2,1)S(1)} %add.27), channel_id=1, source_target_pairs={{0,32},{4,36},{8,40},{12,44},{16,48},{20,52},{24,56},{28,60},{32,0... | collective-permute-start | bytes 12296 | tf_op jit(solution)/shard_map/ppermute | solution.py:20
  92.1 2.3 %collective-permute-done.25 = bf16[16,128]{1,0:T(8,128)(2,1)S(1)} collective-permute-done((bf16[16,128]{1,0:T(8,128)(2,1)S(1)}, bf16[16,128]{1,0:T(8,128)(2,1)S(1)}, u32[]{:S(2)}, u32[]{:S(2)}) %collective-permute-start.25) | collective-permute-done | bytes 4128 | tf_op jit(solution)/shard_map/ppermute | solution.py:20
  94.5 5.8 %collective-permute-start.26 = (bf16[16,128]{1,0:T(8,128)(2,1)S(1)}, bf16[16,128]{1,0:T(8,128)(2,1)S(1)}, u32[]{:S(2)}, u32[]{:S(2)}) collective-permute-start(bf16[16,128]{1,0:T(8,128)(2,1)S(1)} %add.28), channel_id=1, source_target_pairs={{0,4},{4,0},{8,12},{12,8},{16,20},{20,16},{24,28},{28,24},{32,36},... | collective-permute-start | bytes 12296 | tf_op jit(solution)/shard_map/ppermute | solution.py:20
  100.4 0.7 collective-permute-done.26
  101.1 0.6 collective-permute-start.19
  101.7 0.1 collective-permute-start.17
  101.8 0.5 collective-permute-start.5
  102.3 7.3 %collective-permute-done.5.refs_1_ = bf16[512,128]{1,0:T(8,128)(2,1)S(1)} collective-permute-done((bf16[512,128]{1,0:T(8,128)(2,1)S(1)}, bf16[512,128]{1,0:T(8,128)(2,1)S(1)}, u32[]{:S(2)}, u32[]{:S(2)}) %collective-permute-start.5) | collective-permute-done | bytes 131104 | tf_op jit(solution)/shard_map/ppermute | solution.py:25
  109.6 0.5 collective-permute-start.15
  110.3 9.2 %collective-permute-done.9.refs_0_ = bf16[2048,128]{1,0:T(8,128)(2,1)S(1)} collective-permute-done((bf16[2048,128]{1,0:T(8,128)(2,1)S(1)}, bf16[2048,128]{1,0:T(8,128)(2,1)S(1)}, u32[]{:S(2)}, u32[]{:S(2)}) %collective-permute-start.9) | collective-permute-done | bytes 524320 | tf_op jit(solution)/shard_map/ppermute | solution.py:25
  119.5 0.5 collective-permute-start.8
  120.0 0.1 collective-permute-start.6
  120.1 0.6 add_bitcast_fusion
  120.7 1.7 %place.10 = (bf16[2048,2048]{1,0:T(8,128)(2,1)}, bf16[2048,2048]{1,0:T(8,128)(2,1)}) custom-call(bf16[4096,128]{1,0:T(8,128)(2,1)S(1)} %collective-permute-done.11.refs_0_, bf16[4096,128]{1,0:T(8,128)(2,1)S(1)} %mix.2.refs_1_, bf16[4096,128]{1,0:T(8,128)(2,1)S(1)} %collective-permute-done.20.refs_2_, ...), custom_call_target="tpu_custom_call", output_to_operand_aliasing={{0}: (3, {}), {1}: (4, {})} | custom-call | flops 3000000 | bytes 6291456 | tf_op jit(solution)/shard_map/place/pallas_call | solution.py:138
  122.4 2.6 %place.11 = (bf16[2048,2048]{1,0:T(8,128)(2,1)}, bf16[2048,2048]{1,0:T(8,128)(2,1)}) custom-call(bf16[4096,128]{1,0:T(8,128)(2,1)} %collective-permute-done.12.refs_0_, bf16[4096,128]{1,0:T(8,128)(2,1)S(1)} %collective-permute-done.19.refs_1_, bf16[2048,2048]{1,0:T(8,128)(2,1)} %get-tuple-element.29.refs_2_, ...), custom_call_target="tpu_custom_call", output_to_operand_aliasing={{0}: (2, {}), {1}: (3, {})} | custom-call | flops 2000000 | bytes 4194304 | tf_op jit(solution)/shard_map/place/pallas_call | solution.py:138
  125.0 2.6 %place.12 = (bf16[2048,2048]{1,0:T(8,128)(2,1)}, bf16[2048,2048]{1,0:T(8,128)(2,1)}) custom-call(bf16[4096,128]{1,0:T(8,128)(2,1)} %collective-permute-done.3.refs_0_, bf16[4096,128]{1,0:T(8,128)(2,1)S(1)} %collective-permute-done.18.refs_1_, bf16[2048,2048]{1,0:T(8,128)(2,1)} %get-tuple-element.31.refs_2_, ...), custom_call_target="tpu_custom_call", output_to_operand_aliasing={{0}: (2, {}), {1}: (3, {})} | custom-call | flops 2000000 | bytes 4194304 | tf_op jit(solution)/shard_map/place/pallas_call | solution.py:138
  127.6 2.6 %place.13 = (bf16[2048,2048]{1,0:T(8,128)(2,1)}, bf16[2048,2048]{1,0:T(8,128)(2,1)}) custom-call(bf16[4096,128]{1,0:T(8,128)(2,1)} %collective-permute-done.13.refs_0_, bf16[4096,128]{1,0:T(8,128)(2,1)S(1)} %collective-permute-done.17.refs_1_, bf16[2048,2048]{1,0:T(8,128)(2,1)} %get-tuple-element.33.refs_2_, ...), custom_call_target="tpu_custom_call", output_to_operand_aliasing={{0}: (2, {}), {1}: (3, {})} | custom-call | flops 2000000 | bytes 4194304 | tf_op jit(solution)/shard_map/place/pallas_call | solution.py:138
  130.2 1.4 %place.14 = (bf16[2048,2048]{1,0:T(8,128)(2,1)}, bf16[2048,2048]{1,0:T(8,128)(2,1)}) custom-call(bf16[4096,128]{1,0:T(8,128)(2,1)S(1)} %collective-permute-done.4.refs_0_, bf16[4096,128]{1,0:T(8,128)(2,1)S(1)} %collective-permute-done.16.refs_1_, bf16[2048,2048]{1,0:T(8,128)(2,1)} %get-tuple-element.35.refs_2_, ...), custom_call_target="tpu_custom_call", output_to_operand_aliasing={{0}: (2, {}), {1}: (3, {})} | custom-call | flops 2000000 | bytes 4194304 | tf_op jit(solution)/shard_map/place/pallas_call | solution.py:138
  131.5 1.4 %place.15 = (bf16[2048,2048]{1,0:T(8,128)(2,1)}, bf16[2048,2048]{1,0:T(8,128)(2,1)}) custom-call(bf16[4096,128]{1,0:T(8,128)(2,1)S(1)} %collective-permute-done.14.refs_0_, bf16[4096,128]{1,0:T(8,128)(2,1)S(1)} %collective-permute-done.15.refs_1_, bf16[2048,2048]{1,0:T(8,128)(2,1)} %get-tuple-element.37.refs_2_, ...), custom_call_target="tpu_custom_call", output_to_operand_aliasing={{0}: (2, {}), {1}: (3, {})} | custom-call | flops 2000000 | bytes 4194304 | tf_op jit(solution)/shard_map/place/pallas_call | solution.py:138
  132.9 0.8 place.16
  133.8 1.0 place.17
  134.8 0.8 place.18
  135.6 0.7 place.19
  (39 shorter events, 0.7 us)
Async XLA Ops:
  4.9 5.8 %collective-permute-start.11 = (bf16[4096,128]{1,0:T(8,128)(2,1)}, bf16[4096,128]{1,0:T(8,128)(2,1)S(1)}, u32[]{:S(2)}, u32[]{:S(2)}) collective-permute-start(bf16[4096,128]{1,0:T(8,128)(2,1)} %get-tuple-element.26), channel_id=1, source_target_pairs={{0,4},{4,0},{8,12},{12,8},{16,20},{20,16},{24,28},{28,24},{32,36},... | collective-permute-start | bytes 3145736 | tf_op jit(solution)/shard_map/ppermute | solution.py:30
  8.2 27.7 %collective-permute-start = (bf16[128,2048]{1,0:T(8,128)(2,1)}, bf16[128,2048]{1,0:T(8,128)(2,1)S(1)}, u32[]{:S(2)}, u32[]{:S(2)}) collective-permute-start(bf16[128,2048]{1,0:T(8,128)(2,1)} %wg.1), channel_id=1, source_target_pairs={{0,56},{4,12},{8,0},{12,20},{16,8},{20,28},{24,16},{28,36},{32,24}... | collective-permute-start | bytes 1572872 | tf_op jit(solution)/shard_map/ppermute | solution.py:25
  8.2 27.7 %collective-permute-start.1 = (bf16[128,2048]{1,0:T(8,128)(2,1)}, bf16[128,2048]{1,0:T(8,128)(2,1)S(1)}, u32[]{:S(2)}, u32[]{:S(2)}) collective-permute-start(bf16[128,2048]{1,0:T(8,128)(2,1)} %wu.1), channel_id=1, source_target_pairs={{0,56},{4,12},{8,0},{12,20},{16,8},{20,28},{24,16},{28,36},{32,24}... | collective-permute-start | bytes 1572872 | tf_op jit(solution)/shard_map/ppermute | solution.py:25
  10.7 28.5 %collective-permute-start.12 = (bf16[4096,128]{1,0:T(8,128)(2,1)S(1)}, bf16[4096,128]{1,0:T(8,128)(2,1)}, u32[]{:S(2)}, u32[]{:S(2)}) collective-permute-start(bf16[4096,128]{1,0:T(8,128)(2,1)S(1)} %collective-permute-done.11.refs_0_), channel_id=1, source_target_pairs={{0,56},{4,12},{8,0},{12,20},{16,8},{20,28},{24,16},{28,36},{32,24}... | collective-permute-start | bytes 3145736 | tf_op jit(solution)/shard_map/ppermute | solution.py:25
  11.4 24.5 %collective-permute-start.2 = (bf16[64,128]{1,0:T(8,128)(2,1)}, bf16[64,128]{1,0:T(8,128)(2,1)S(1)}, u32[]{:S(2)}, u32[]{:S(2)}) collective-permute-start(bf16[64,128]{1,0:T(8,128)(2,1)} %pad_maximum_fusion.low), channel_id=1, source_target_pairs={{0,56},{4,12},{8,0},{12,20},{16,8},{20,28},{24,16},{28,36},{32,24}... | collective-permute-start | bytes 49160 | tf_op jit(solution)/shard_map/ppermute | solution.py:25
  35.8 0.9 copy-start
  36.8 0.9 copy-start.1
  39.0 15.0 %collective-permute-start.3 = (bf16[4096,128]{1,0:T(8,128)(2,1)S(1)}, bf16[4096,128]{1,0:T(8,128)(2,1)}, u32[]{:S(2)}, u32[]{:S(2)}) collective-permute-start(bf16[4096,128]{1,0:T(8,128)(2,1)S(1)} %mix.2.refs_1_), channel_id=1, source_target_pairs={{0,56},{4,12},{8,0},{12,20},{16,8},{20,28},{24,16},{28,36},{32,24}... | collective-permute-start | bytes 3145736 | tf_op jit(solution)/shard_map/ppermute | solution.py:25
  39.1 26.2 %collective-permute-start.13 = (bf16[4096,128]{1,0:T(8,128)(2,1)}, bf16[4096,128]{1,0:T(8,128)(2,1)}, u32[]{:S(2)}, u32[]{:S(2)}) collective-permute-start(bf16[4096,128]{1,0:T(8,128)(2,1)} %collective-permute-done.12.refs_0_), channel_id=1, source_target_pairs={{0,56},{4,12},{8,0},{12,20},{16,8},{20,28},{24,16},{28,36},{32,24}... | collective-permute-start | bytes 3145736 | tf_op jit(solution)/shard_map/ppermute | solution.py:25
  54.1 46.2 %collective-permute-start.4 = (bf16[4096,128]{1,0:T(8,128)(2,1)}, bf16[4096,128]{1,0:T(8,128)(2,1)S(1)}, u32[]{:S(2)}, u32[]{:S(2)}) collective-permute-start(bf16[4096,128]{1,0:T(8,128)(2,1)} %collective-permute-done.3.refs_0_), channel_id=1, source_target_pairs={{0,56},{4,12},{8,0},{12,20},{16,8},{20,28},{24,16},{28,36},{32,24}... | collective-permute-start | bytes 3145736 | tf_op jit(solution)/shard_map/ppermute | solution.py:25
  54.9 46.8 %collective-permute-start.20 = (bf16[4096,128]{1,0:T(8,128)(2,1)S(1)}, bf16[4096,128]{1,0:T(8,128)(2,1)S(1)}, u32[]{:S(2)}, u32[]{:S(2)}) collective-permute-start(bf16[4096,128]{1,0:T(8,128)(2,1)S(1)} %mix.2.refs_1_), channel_id=1, source_target_pairs={{0,4},{4,0},{8,12},{12,8},{16,20},{20,16},{24,28},{28,24},{32,36},... | collective-permute-start | bytes 3145736 | tf_op jit(solution)/shard_map/ppermute | solution.py:30
  60.2 41.5 %collective-permute-start.18 = (bf16[4096,128]{1,0:T(8,128)(2,1)}, bf16[4096,128]{1,0:T(8,128)(2,1)S(1)}, u32[]{:S(2)}, u32[]{:S(2)}) collective-permute-start(bf16[4096,128]{1,0:T(8,128)(2,1)} %collective-permute-done.3.refs_0_), channel_id=1, source_target_pairs={{0,4},{4,0},{8,12},{12,8},{16,20},{20,16},{24,28},{28,24},{32,36},... | collective-permute-start | bytes 3145736 | tf_op jit(solution)/shard_map/ppermute | solution.py:30
  65.3 44.3 %collective-permute-start.14 = (bf16[4096,128]{1,0:T(8,128)(2,1)}, bf16[4096,128]{1,0:T(8,128)(2,1)S(1)}, u32[]{:S(2)}, u32[]{:S(2)}) collective-permute-start(bf16[4096,128]{1,0:T(8,128)(2,1)} %collective-permute-done.13.refs_0_), channel_id=1, source_target_pairs={{0,56},{4,12},{8,0},{12,20},{16,8},{20,28},{24,16},{28,36},{32,24}... | collective-permute-start | bytes 3145736 | tf_op jit(solution)/shard_map/ppermute | solution.py:25
  65.4 2.8 %collective-permute-start.21 = (bf16[16,128]{1,0:T(8,128)(2,1)S(1)}, bf16[16,128]{1,0:T(8,128)(2,1)S(1)}, u32[]{:S(2)}, u32[]{:S(2)}) collective-permute-start(bf16[16,128]{1,0:T(8,128)(2,1)S(1)} %fusion.1), channel_id=1, source_target_pairs={{0,1},{1,0},{2,3},{3,2},{4,5},{5,4},{6,7},{7,6},{8,9},{9,8},{10,11... | collective-permute-start | bytes 12296 | tf_op jit(solution)/shard_map/ppermute | solution.py:20
  68.3 4.0 %collective-permute-start.22 = (bf16[16,128]{1,0:T(8,128)(2,1)S(1)}, bf16[16,128]{1,0:T(8,128)(2,1)S(1)}, u32[]{:S(2)}, u32[]{:S(2)}) collective-permute-start(bf16[16,128]{1,0:T(8,128)(2,1)S(1)} %fusion.2), channel_id=1, source_target_pairs={{0,2},{1,3},{2,0},{3,1},{4,6},{5,7},{6,4},{7,5},{8,10},{9,11},{10,... | collective-permute-start | bytes 12296 | tf_op jit(solution)/shard_map/ppermute | solution.py:20
  72.3 12.4 %collective-permute-start.23 = (bf16[16,128]{1,0:T(8,128)(2,1)S(1)}, bf16[16,128]{1,0:T(8,128)(2,1)S(1)}, u32[]{:S(2)}, u32[]{:S(2)}) collective-permute-start(bf16[16,128]{1,0:T(8,128)(2,1)S(1)} %fusion.3), channel_id=1, source_target_pairs={{0,8},{4,12},{8,0},{12,4},{16,24},{20,28},{24,16},{28,20},{32,40},... | collective-permute-start | bytes 12296 | tf_op jit(solution)/shard_map/ppermute | solution.py:20
  84.7 3.4 %collective-permute-start.24 = (bf16[16,128]{1,0:T(8,128)(2,1)S(1)}, bf16[16,128]{1,0:T(8,128)(2,1)S(1)}, u32[]{:S(2)}, u32[]{:S(2)}) collective-permute-start(bf16[16,128]{1,0:T(8,128)(2,1)S(1)} %add.26), channel_id=1, source_target_pairs={{0,16},{4,20},{8,24},{12,28},{16,0},{20,4},{24,8},{28,12},{32,48},... | collective-permute-start | bytes 12296 | tf_op jit(solution)/shard_map/ppermute | solution.py:20
  88.1 6.4 %collective-permute-start.25 = (bf16[16,128]{1,0:T(8,128)(2,1)S(1)}, bf16[16,128]{1,0:T(8,128)(2,1)S(1)}, u32[]{:S(2)}, u32[]{:S(2)}) collective-permute-start(bf16[16,128]{1,0:T(8,128)(2,1)S(1)} %add.27), channel_id=1, source_target_pairs={{0,32},{4,36},{8,40},{12,44},{16,48},{20,52},{24,56},{28,60},{32,0... | collective-permute-start | bytes 12296 | tf_op jit(solution)/shard_map/ppermute | solution.py:20
  94.5 6.6 %collective-permute-start.26 = (bf16[16,128]{1,0:T(8,128)(2,1)S(1)}, bf16[16,128]{1,0:T(8,128)(2,1)S(1)}, u32[]{:S(2)}, u32[]{:S(2)}) collective-permute-start(bf16[16,128]{1,0:T(8,128)(2,1)S(1)} %add.28), channel_id=1, source_target_pairs={{0,4},{4,0},{8,12},{12,8},{16,20},{20,16},{24,28},{28,24},{32,36},... | collective-permute-start | bytes 12296 | tf_op jit(solution)/shard_map/ppermute | solution.py:20
  100.3 9.9 %collective-permute-start.7 = (bf16[1536,128]{1,0:T(8,128)(2,1)S(1)}, bf16[1536,128]{1,0:T(8,128)(2,1)S(1)}, u32[]{:S(2)}, u32[]{:S(2)}) collective-permute-start(bf16[1536,128]{1,0:T(8,128)(2,1)S(1)} %slice.13), channel_id=1, source_target_pairs={{0,56},{4,12},{8,0},{12,20},{16,8},{20,28},{24,16},{28,36},{32,24}... | collective-permute-start | bytes 1179656 | tf_op jit(solution)/shard_map/ppermute | solution.py:25
  101.1 18.4 %collective-permute-start.19 = (bf16[4096,128]{1,0:T(8,128)(2,1)}, bf16[4096,128]{1,0:T(8,128)(2,1)S(1)}, u32[]{:S(2)}, u32[]{:S(2)}) collective-permute-start(bf16[4096,128]{1,0:T(8,128)(2,1)} %collective-permute-done.12.refs_0_), channel_id=1, source_target_pairs={{0,4},{4,0},{8,12},{12,8},{16,20},{20,16},{24,28},{28,24},{32,36},... | collective-permute-start | bytes 3145736 | tf_op jit(solution)/shard_map/ppermute | solution.py:30
  101.7 18.3 %collective-permute-start.17 = (bf16[4096,128]{1,0:T(8,128)(2,1)}, bf16[4096,128]{1,0:T(8,128)(2,1)S(1)}, u32[]{:S(2)}, u32[]{:S(2)}) collective-permute-start(bf16[4096,128]{1,0:T(8,128)(2,1)} %collective-permute-done.13.refs_0_), channel_id=1, source_target_pairs={{0,4},{4,0},{8,12},{12,8},{16,20},{20,16},{24,28},{28,24},{32,36},... | collective-permute-start | bytes 3145736 | tf_op jit(solution)/shard_map/ppermute | solution.py:30
  101.8 7.8 %collective-permute-start.5 = (bf16[512,128]{1,0:T(8,128)(2,1)S(1)}, bf16[512,128]{1,0:T(8,128)(2,1)S(1)}, u32[]{:S(2)}, u32[]{:S(2)}) collective-permute-start(bf16[512,128]{1,0:T(8,128)(2,1)S(1)} %slice.12), channel_id=1, source_target_pairs={{0,56},{4,12},{8,0},{12,20},{16,8},{20,28},{24,16},{28,36},{32,24}... | collective-permute-start | bytes 393224 | tf_op jit(solution)/shard_map/ppermute | solution.py:25
  109.6 20.5 %collective-permute-start.16 = (bf16[4096,128]{1,0:T(8,128)(2,1)S(1)}, bf16[4096,128]{1,0:T(8,128)(2,1)S(1)}, u32[]{:S(2)}, u32[]{:S(2)}) collective-permute-start(bf16[4096,128]{1,0:T(8,128)(2,1)S(1)} %collective-permute-done.4.refs_0_), channel_id=1, source_target_pairs={{0,4},{4,0},{8,12},{12,8},{16,20},{20,16},{24,28},{28,24},{32,36},... | collective-permute-start | bytes 3145736 | tf_op jit(solution)/shard_map/ppermute | solution.py:30
  109.6 21.9 %collective-permute-start.15 = (bf16[4096,128]{1,0:T(8,128)(2,1)S(1)}, bf16[4096,128]{1,0:T(8,128)(2,1)S(1)}, u32[]{:S(2)}, u32[]{:S(2)}) collective-permute-start(bf16[4096,128]{1,0:T(8,128)(2,1)S(1)} %collective-permute-done.14.refs_0_), channel_id=1, source_target_pairs={{0,4},{4,0},{8,12},{12,8},{16,20},{20,16},{24,28},{28,24},{32,36},... | collective-permute-start | bytes 3145736 | tf_op jit(solution)/shard_map/ppermute | solution.py:30
  110.2 9.3 %collective-permute-start.9 = (bf16[2048,128]{1,0:T(8,128)(2,1)S(1)}, bf16[2048,128]{1,0:T(8,128)(2,1)S(1)}, u32[]{:S(2)}, u32[]{:S(2)}) collective-permute-start(bf16[2048,128]{1,0:T(8,128)(2,1)S(1)} %slice.14), channel_id=1, source_target_pairs={{0,56},{4,12},{8,0},{12,20},{16,8},{20,28},{24,16},{28,36},{32,24}... | collective-permute-start | bytes 1572872 | tf_op jit(solution)/shard_map/ppermute | solution.py:25
  119.5 14.3 %collective-permute-start.10 = (bf16[2048,128]{1,0:T(8,128)(2,1)S(1)}, bf16[2048,128]{1,0:T(8,128)(2,1)S(1)}, u32[]{:S(2)}, u32[]{:S(2)}) collective-permute-start(bf16[2048,128]{1,0:T(8,128)(2,1)S(1)} %collective-permute-done.9.refs_0_), channel_id=1, source_target_pairs={{0,4},{4,0},{8,12},{12,8},{16,20},{20,16},{24,28},{28,24},{32,36},... | collective-permute-start | bytes 1572872 | tf_op jit(solution)/shard_map/ppermute | solution.py:30
  119.5 15.3 %collective-permute-start.8 = (bf16[1536,128]{1,0:T(8,128)(2,1)S(1)}, bf16[1536,128]{1,0:T(8,128)(2,1)S(1)}, u32[]{:S(2)}, u32[]{:S(2)}) collective-permute-start(bf16[1536,128]{1,0:T(8,128)(2,1)S(1)} %collective-permute-done.7.refs_1_), channel_id=1, source_target_pairs={{0,4},{4,0},{8,12},{12,8},{16,20},{20,16},{24,28},{28,24},{32,36},... | collective-permute-start | bytes 1179656 | tf_op jit(solution)/shard_map/ppermute | solution.py:30
  120.0 15.6 %collective-permute-start.6 = (bf16[512,128]{1,0:T(8,128)(2,1)S(1)}, bf16[512,128]{1,0:T(8,128)(2,1)S(1)}, u32[]{:S(2)}, u32[]{:S(2)}) collective-permute-start(bf16[512,128]{1,0:T(8,128)(2,1)S(1)} %collective-permute-done.5.refs_1_), channel_id=1, source_target_pairs={{0,4},{4,0},{8,12},{12,8},{16,20},{20,16},{24,28},{28,24},{32,36},... | collective-permute-start | bytes 393224 | tf_op jit(solution)/shard_map/ppermute | solution.py:30

commit v5 on v4

--- a/solution.py
+++ b/solution.py
@@ -30,12 +30,17 @@
     return lax.ppermute(x, RING, [(i, i ^ 1) for i in range(n)])
 
 
-def merge_kernel(place_own, wg, wu, low, hg, hu, unit, *refs):
+def merge_kernel(parts, place_own, *refs):
+    lows, (wg, wu, hg, hu, unit), refs = refs[:parts], refs[parts:parts + 5], refs[parts + 5:]
     finals = refs[:2] if place_own else ()
     wbuf, lbuf, hbuf, tbuf, lsem, isem, osem = refs[len(finals):]
     rows, cols = wg.shape
     rank = hg.shape[0]
-    lows = pltpu.make_async_copy(low, lbuf, lsem)
+    size = 2 * rank // parts
+    lows = [
+        pltpu.make_async_copy(low, lbuf.at[pl.ds(i * size, size), :], lsem.at[i])
+        for i, low in enumerate(lows)
+    ]
     loads = [
         [
             pltpu.make_async_copy(src, buf.at[k], isem.at[k, i])
@@ -52,11 +57,11 @@
         stores[k].append(
             pltpu.make_async_copy(tbuf.at[k], final.at[:, pl.ds(mine, rows)], osem.at[k, 1])
         )
-    lows.start()
-    for group in loads:
+    for group in (lows, *loads):
         for cp in group:
             cp.start()
-    lows.wait()
+    for cp in lows:
+        cp.wait()
     for k in range(2):
         for cp in loads[k]:
             cp.wait()
@@ -73,32 +78,30 @@
             cp.wait()
 
 
-def merged(wg, wu, low, hg, hu, grant, final=None):
+def merged(wg, wu, lows, hg, hu, grant, final=None):
     rows, cols = wg.shape
     rank = hg.shape[0]
     outs = (jax.ShapeDtypeStruct((2 * cols, rows), jnp.bfloat16),)
     if final:
         outs += (jax.ShapeDtypeStruct(final, jnp.bfloat16),) * 2
     return pl.pallas_call(
-        functools.partial(merge_kernel, bool(final)),
+        functools.partial(merge_kernel, len(lows), bool(final)),
         out_shape=outs,
-        in_specs=[ANY] * 5,
+        in_specs=[ANY] * (4 + len(lows)),
         out_specs=(ANY,) * len(outs),
         scratch_shapes=[
             pltpu.VMEM((2, rows, cols), jnp.bfloat16),
             pltpu.VMEM((2 * rank, rows), jnp.bfloat16),
             pltpu.VMEM((2, rank, cols), jnp.bfloat16),
             pltpu.VMEM((2, cols, rows), jnp.bfloat16),
-            pltpu.SemaphoreType.DMA,
+            pltpu.SemaphoreType.DMA((2,)),
             pltpu.SemaphoreType.DMA((2, 2)),
             pltpu.SemaphoreType.DMA((2, 2)),
         ],
         compiler_params=pltpu.CompilerParams(vmem_limit_bytes=grant),
         name="mix",
-        cost_estimate=pl.CostEstimate(
-            flops=4 * rows * cols * rank, bytes_accessed=8 * rows * cols, transcendentals=0
-        ),
-    )(wg, wu, low, hg, hu)
+        cost_estimate=pl.CostEstimate(flops=4 * rows * cols * rank, bytes_accessed=8 * rows * cols, transcendentals=0),
+    )(*lows, wg, wu, hg, hu)
 
 
 def place_kernel(units, *refs):
@@ -162,9 +165,9 @@
     low = jnp.concatenate([low_gate.T, low_up.T], axis=0)
     raw_low = onward(low)
     held, other = {}, {}
-    held["A", 0], *outs = merged(weight_gate, weight_up, low, high_gate, high_up, LARGE, shape)
+    held["A", 0], *outs = merged(weight_gate, weight_up, (low_gate.T, low_up.T), high_gate, high_up, LARGE, shape)
     other["A", 0] = swapped(held["A", 0])
-    held["A", 1], = merged(raw_gate, raw_up, raw_low, high_gate, high_up, SMALL)
+    held["A", 1], = merged(raw_gate, raw_up, (raw_low,), high_gate, high_up, SMALL)
     held["B", 1] = onward(other["A", 0])
     for h in range(2, far):
         held["A", h] = onward(held["A", h - 1])

time: 137 us -> 136 us (level)
  transfers between devices with their start and end apart: 27 -> 27, of which waited for: 12 -> 12; matrix products, arithmetic and copies ran while one was open for 1% -> 2% of each run, Pallas kernels for 12% -> 12%
where the time goes in v5:
time: 136 us; the launch traced here: 135 us
  waiting for transfers between devices  78.3 us (58%)
  starting transfers between devices  31.8 us (23%)
  Pallas kernels  19.8 us (15%)
  other arithmetic  2.25 us (2%)
  local copies, waits for them, and re-layouts  1.97 us (1%)
    ppermute x11, waiting for transfers between devices, onward(): lax.ppermute(x, RING, [(i, (i + (2 if i % 2 == 1 else n - 2)) % n) for i...  57.3 us
    ppermute x6, waiting for transfers between devices, paired(): return lax.ppermute(x, axis, [(i, i ^ bit) for i in range(n)])  20.1 us
    pallas_call x10, Pallas kernels, place(): pl.pallas_call(functools.partial(place_kernel, units), out_shape=(out, ou...  15.5 us
    ppermute x6, starting transfers between devices, paired(): return lax.ppermute(x, axis, [(i, i ^ bit) for i in range(n)])  15.3 us
    ppermute x10, starting transfers between devices, swapped(): return lax.ppermute(x, RING, [(i, i ^ 1) for i in range(n)])  10.5 us
    ppermute x11, starting transfers between devices, onward(): lax.ppermute(x, RING, [(i, (i + (2 if i % 2 == 1 else n - 2)) % n) for i...  6.01 us
    pallas_call x2, Pallas kernels, merged(): pl.pallas_call(functools.partial(merge_kernel, len(lows), bool(final)), o...  4.31 us
  transfers between devices with their start and end apart: 27, of which 12 were waited for; matrix products, arithmetic and copies ran while one was open for 2% of the time, Pallas kernels for 12%

profile of v5, /device:TPU:1, one launch (start us, length us, event | category | flops | bytes accessed | tf_op | source)
XLA Modules:
  0.0 135.2 jit_solution(9025304932164496047)
XLA Ops:
  0.6 2.9 %mix.3 = (bf16[4096,128]{1,0:T(8,128)(2,1)}, bf16[2048,2048]{1,0:T(8,128)(2,1)}, bf16[2048,2048]{1,0:T(8,128)(2,1)}) custom-call(bf16[32,128]{1,0:T(8,128)(2,1)} %bitcast.6, bf16[32,128]{1,0:T(8,128)(2,1)} %bitcast.4, bf16[128,2048]{1,0:T(8,128)(2,1)} %refs_2_.1, bf16[128,2048]{1,0:T(8,128)(2,1)} %refs_3_.3, bf16[32,2048]{1,0:T(8,128)(2,1)} %refs_4_.3, ...), custom_call_target="tpu_custom_call" | custom-call | flops 33554432 | bytes 2097152 | tf_op jit(solution)/shard_map/mix/pallas_call | solution.py:87
  3.6 3.3 %collective-permute-start.11 = (bf16[4096,128]{1,0:T(8,128)(2,1)}, bf16[4096,128]{1,0:T(8,128)(2,1)S(1)}, u32[]{:S(2)}, u32[]{:S(2)}) collective-permute-start(bf16[4096,128]{1,0:T(8,128)(2,1)} %get-tuple-element.26), channel_id=1, source_target_pairs={{0,4},{4,0},{8,12},{12,8},{16,20},{20,16},{24,28},{28,24},{32,36},... | collective-permute-start | bytes 3145736 | tf_op jit(solution)/shard_map/ppermute | solution.py:30
  6.9 1.6 %collective-permute-start.2 = (bf16[128,2048]{1,0:T(8,128)(2,1)}, bf16[128,2048]{1,0:T(8,128)(2,1)S(1)}, u32[]{:S(2)}, u32[]{:S(2)}) collective-permute-start(bf16[128,2048]{1,0:T(8,128)(2,1)} %refs_3_.3), channel_id=1, source_target_pairs={{0,56},{4,12},{8,0},{12,20},{16,8},{20,28},{24,16},{28,36},{32,24}... | collective-permute-start | bytes 1572872 | tf_op jit(solution)/shard_map/ppermute | solution.py:25
  8.4 0.9 collective-permute-done.11.refs_0_
  9.4 0.7 collective-permute-start.12
  10.1 0.7 pad_maximum_fusion
  10.8 2.8 %collective-permute-start = (bf16[64,128]{1,0:T(8,128)(2,1)S(1)}, bf16[64,128]{1,0:T(8,128)(2,1)S(1)}, u32[]{:S(2)}, u32[]{:S(2)}) collective-permute-start(bf16[64,128]{1,0:T(8,128)(2,1)S(1)} %pad_maximum_fusion), channel_id=1, source_target_pairs={{0,56},{4,12},{8,0},{12,20},{16,8},{20,28},{24,16},{28,36},{32,24}... | collective-permute-start | bytes 49160 | tf_op jit(solution)/shard_map/ppermute | solution.py:25
  13.6 20.9 %collective-permute-done.refs_0_ = bf16[64,128]{1,0:T(8,128)(2,1)S(1)} collective-permute-done((bf16[64,128]{1,0:T(8,128)(2,1)S(1)}, bf16[64,128]{1,0:T(8,128)(2,1)S(1)}, u32[]{:S(2)}, u32[]{:S(2)}) %collective-permute-start) | collective-permute-done | bytes 16416 | tf_op jit(solution)/shard_map/ppermute | solution.py:25
  34.5 0.9 copy-done
  35.5 0.9 copy-done.1
  36.4 1.4 %mix.2.refs_1_ = bf16[4096,128]{1,0:T(8,128)(2,1)S(1)} custom-call(bf16[64,128]{1,0:T(8,128)(2,1)S(1)} %collective-permute-done.refs_0_, bf16[128,2048]{1,0:T(8,128)(2,1)S(1)} %collective-permute-done.1.refs_1_, bf16[128,2048]{1,0:T(8,128)(2,1)S(1)} %collective-permute-done.2.refs_2_, bf16[32,2048]{1,0:T(8,128)(2,1)S(1)} %copy-done, ...), custom_call_target="tpu_custom_call" | custom-call | flops 33554432 | bytes 2097152 | tf_op jit(solution)/shard_map/mix/pallas_call | solution.py:87
  37.7 0.1 collective-permute-start.3
  37.9 14.8 %collective-permute-done.3.refs_0_ = bf16[4096,128]{1,0:T(8,128)(2,1)} collective-permute-done((bf16[4096,128]{1,0:T(8,128)(2,1)S(1)}, bf16[4096,128]{1,0:T(8,128)(2,1)}, u32[]{:S(2)}, u32[]{:S(2)}) %collective-permute-start.3) | collective-permute-done | bytes 1048608 | tf_op jit(solution)/shard_map/ppermute | solution.py:25
  52.8 0.7 add_convert_fusion
  53.5 0.1 broadcast_in_dim.14
  53.6 5.4 %collective-permute-start.20 = (bf16[4096,128]{1,0:T(8,128)(2,1)S(1)}, bf16[4096,128]{1,0:T(8,128)(2,1)S(1)}, u32[]{:S(2)}, u32[]{:S(2)}) collective-permute-start(bf16[4096,128]{1,0:T(8,128)(2,1)S(1)} %mix.2.refs_1_), channel_id=1, source_target_pairs={{0,4},{4,0},{8,12},{12,8},{16,20},{20,16},{24,28},{28,24},{32,36},... | collective-permute-start | bytes 3145736 | tf_op jit(solution)/shard_map/ppermute | solution.py:30
  58.9 0.1 collective-permute-start.18
  59.0 5.0 %collective-permute-done.13.refs_0_ = bf16[4096,128]{1,0:T(8,128)(2,1)} collective-permute-done((bf16[4096,128]{1,0:T(8,128)(2,1)}, bf16[4096,128]{1,0:T(8,128)(2,1)}, u32[]{:S(2)}, u32[]{:S(2)}) %collective-permute-start.13) | collective-permute-done | bytes 1048608 | tf_op jit(solution)/shard_map/ppermute | solution.py:25
  64.1 1.2 collective-permute-start.21
  65.3 1.5 %collective-permute-done.21 = bf16[16,128]{1,0:T(8,128)(2,1)S(1)} collective-permute-done((bf16[16,128]{1,0:T(8,128)(2,1)S(1)}, bf16[16,128]{1,0:T(8,128)(2,1)S(1)}, u32[]{:S(2)}, u32[]{:S(2)}) %collective-permute-start.21) | collective-permute-done | bytes 4128 | tf_op jit(solution)/shard_map/ppermute | solution.py:20
  67.0 2.8 %collective-permute-start.22 = (bf16[16,128]{1,0:T(8,128)(2,1)S(1)}, bf16[16,128]{1,0:T(8,128)(2,1)S(1)}, u32[]{:S(2)}, u32[]{:S(2)}) collective-permute-start(bf16[16,128]{1,0:T(8,128)(2,1)S(1)} %fusion.2), channel_id=1, source_target_pairs={{0,2},{1,3},{2,0},{3,1},{4,6},{5,7},{6,4},{7,5},{8,10},{9,11},{10,... | collective-permute-start | bytes 12296 | tf_op jit(solution)/shard_map/ppermute | solution.py:20
  69.7 1.2 collective-permute-done.22
  71.1 12.4 %collective-permute-done.23 = bf16[16,128]{1,0:T(8,128)(2,1)S(1)} collective-permute-done((bf16[16,128]{1,0:T(8,128)(2,1)S(1)}, bf16[16,128]{1,0:T(8,128)(2,1)S(1)}, u32[]{:S(2)}, u32[]{:S(2)}) %collective-permute-start.23) | collective-permute-done | bytes 4128 | tf_op jit(solution)/shard_map/ppermute | solution.py:20
  83.4 1.5 %collective-permute-start.24 = (bf16[16,128]{1,0:T(8,128)(2,1)S(1)}, bf16[16,128]{1,0:T(8,128)(2,1)S(1)}, u32[]{:S(2)}, u32[]{:S(2)}) collective-permute-start(bf16[16,128]{1,0:T(8,128)(2,1)S(1)} %add.26), channel_id=1, source_target_pairs={{0,16},{4,20},{8,24},{12,28},{16,0},{20,4},{24,8},{28,12},{32,48},... | collective-permute-start | bytes 12296 | tf_op jit(solution)/shard_map/ppermute | solution.py:20
  84.9 1.9 %collective-permute-done.24 = bf16[16,128]{1,0:T(8,128)(2,1)S(1)} collective-permute-done((bf16[16,128]{1,0:T(8,128)(2,1)S(1)}, bf16[16,128]{1,0:T(8,128)(2,1)S(1)}, u32[]{:S(2)}, u32[]{:S(2)}) %collective-permute-start.24) | collective-permute-done | bytes 4128 | tf_op jit(solution)/shard_map/ppermute | solution.py:20
  86.8 4.0 %collective-permute-start.25 = (bf16[16,128]{1,0:T(8,128)(2,1)S(1)}, bf16[16,128]{1,0:T(8,128)(2,1)S(1)}, u32[]{:S(2)}, u32[]{:S(2)}) collective-permute-start(bf16[16,128]{1,0:T(8,128)(2,1)S(1)} %add.27), channel_id=1, source_target_pairs={{0,32},{4,36},{8,40},{12,44},{16,48},{20,52},{24,56},{28,60},{32,0... | collective-permute-start | bytes 12296 | tf_op jit(solution)/shard_map/ppermute | solution.py:20
  90.8 2.4 %collective-permute-done.25 = bf16[16,128]{1,0:T(8,128)(2,1)S(1)} collective-permute-done((bf16[16,128]{1,0:T(8,128)(2,1)S(1)}, bf16[16,128]{1,0:T(8,128)(2,1)S(1)}, u32[]{:S(2)}, u32[]{:S(2)}) %collective-permute-start.25) | collective-permute-done | bytes 4128 | tf_op jit(solution)/shard_map/ppermute | solution.py:20
  93.2 5.8 %collective-permute-start.26 = (bf16[16,128]{1,0:T(8,128)(2,1)S(1)}, bf16[16,128]{1,0:T(8,128)(2,1)S(1)}, u32[]{:S(2)}, u32[]{:S(2)}) collective-permute-start(bf16[16,128]{1,0:T(8,128)(2,1)S(1)} %add.28), channel_id=1, source_target_pairs={{0,4},{4,0},{8,12},{12,8},{16,20},{20,16},{24,28},{28,24},{32,36},... | collective-permute-start | bytes 12296 | tf_op jit(solution)/shard_map/ppermute | solution.py:20
  99.1 0.7 collective-permute-done.26
  99.8 0.6 collective-permute-start.19
  100.4 0.1 collective-permute-start.17
  100.5 0.5 collective-permute-start.5
  101.0 7.3 %collective-permute-done.5.refs_1_ = bf16[512,128]{1,0:T(8,128)(2,1)S(1)} collective-permute-done((bf16[512,128]{1,0:T(8,128)(2,1)S(1)}, bf16[512,128]{1,0:T(8,128)(2,1)S(1)}, u32[]{:S(2)}, u32[]{:S(2)}) %collective-permute-start.5) | collective-permute-done | bytes 131104 | tf_op jit(solution)/shard_map/ppermute | solution.py:25
  108.3 0.5 collective-permute-start.15
  109.0 9.2 %collective-permute-done.9.refs_0_ = bf16[2048,128]{1,0:T(8,128)(2,1)S(1)} collective-permute-done((bf16[2048,128]{1,0:T(8,128)(2,1)S(1)}, bf16[2048,128]{1,0:T(8,128)(2,1)S(1)}, u32[]{:S(2)}, u32[]{:S(2)}) %collective-permute-start.9) | collective-permute-done | bytes 524320 | tf_op jit(solution)/shard_map/ppermute | solution.py:25
  118.2 0.5 collective-permute-start.8
  118.7 0.1 collective-permute-start.6
  118.8 0.6 add_bitcast_fusion
  119.4 1.7 %place.10 = (bf16[2048,2048]{1,0:T(8,128)(2,1)}, bf16[2048,2048]{1,0:T(8,128)(2,1)}) custom-call(bf16[4096,128]{1,0:T(8,128)(2,1)S(1)} %collective-permute-done.11.refs_0_, bf16[4096,128]{1,0:T(8,128)(2,1)S(1)} %mix.2.refs_1_, bf16[4096,128]{1,0:T(8,128)(2,1)S(1)} %collective-permute-done.20.refs_2_, ...), custom_call_target="tpu_custom_call", output_to_operand_aliasing={{0}: (3, {}), {1}: (4, {})} | custom-call | flops 3000000 | bytes 6291456 | tf_op jit(solution)/shard_map/place/pallas_call | solution.py:141
  121.1 2.6 %place.11 = (bf16[2048,2048]{1,0:T(8,128)(2,1)}, bf16[2048,2048]{1,0:T(8,128)(2,1)}) custom-call(bf16[4096,128]{1,0:T(8,128)(2,1)} %collective-permute-done.12.refs_0_, bf16[4096,128]{1,0:T(8,128)(2,1)S(1)} %collective-permute-done.19.refs_1_, bf16[2048,2048]{1,0:T(8,128)(2,1)} %get-tuple-element.29.refs_2_, ...), custom_call_target="tpu_custom_call", output_to_operand_aliasing={{0}: (2, {}), {1}: (3, {})} | custom-call | flops 2000000 | bytes 4194304 | tf_op jit(solution)/shard_map/place/pallas_call | solution.py:141
  123.7 2.6 %place.12 = (bf16[2048,2048]{1,0:T(8,128)(2,1)}, bf16[2048,2048]{1,0:T(8,128)(2,1)}) custom-call(bf16[4096,128]{1,0:T(8,128)(2,1)} %collective-permute-done.3.refs_0_, bf16[4096,128]{1,0:T(8,128)(2,1)S(1)} %collective-permute-done.18.refs_1_, bf16[2048,2048]{1,0:T(8,128)(2,1)} %get-tuple-element.31.refs_2_, ...), custom_call_target="tpu_custom_call", output_to_operand_aliasing={{0}: (2, {}), {1}: (3, {})} | custom-call | flops 2000000 | bytes 4194304 | tf_op jit(solution)/shard_map/place/pallas_call | solution.py:141
  126.3 2.6 %place.13 = (bf16[2048,2048]{1,0:T(8,128)(2,1)}, bf16[2048,2048]{1,0:T(8,128)(2,1)}) custom-call(bf16[4096,128]{1,0:T(8,128)(2,1)} %collective-permute-done.13.refs_0_, bf16[4096,128]{1,0:T(8,128)(2,1)S(1)} %collective-permute-done.17.refs_1_, bf16[2048,2048]{1,0:T(8,128)(2,1)} %get-tuple-element.33.refs_2_, ...), custom_call_target="tpu_custom_call", output_to_operand_aliasing={{0}: (2, {}), {1}: (3, {})} | custom-call | flops 2000000 | bytes 4194304 | tf_op jit(solution)/shard_map/place/pallas_call | solution.py:141
  128.9 1.4 %place.14 = (bf16[2048,2048]{1,0:T(8,128)(2,1)}, bf16[2048,2048]{1,0:T(8,128)(2,1)}) custom-call(bf16[4096,128]{1,0:T(8,128)(2,1)S(1)} %collective-permute-done.4.refs_0_, bf16[4096,128]{1,0:T(8,128)(2,1)S(1)} %collective-permute-done.16.refs_1_, bf16[2048,2048]{1,0:T(8,128)(2,1)} %get-tuple-element.35.refs_2_, ...), custom_call_target="tpu_custom_call", output_to_operand_aliasing={{0}: (2, {}), {1}: (3, {})} | custom-call | flops 2000000 | bytes 4194304 | tf_op jit(solution)/shard_map/place/pallas_call | solution.py:141
  130.3 1.4 %place.15 = (bf16[2048,2048]{1,0:T(8,128)(2,1)}, bf16[2048,2048]{1,0:T(8,128)(2,1)}) custom-call(bf16[4096,128]{1,0:T(8,128)(2,1)S(1)} %collective-permute-done.14.refs_0_, bf16[4096,128]{1,0:T(8,128)(2,1)S(1)} %collective-permute-done.15.refs_1_, bf16[2048,2048]{1,0:T(8,128)(2,1)} %get-tuple-element.37.refs_2_, ...), custom_call_target="tpu_custom_call", output_to_operand_aliasing={{0}: (2, {}), {1}: (3, {})} | custom-call | flops 2000000 | bytes 4194304 | tf_op jit(solution)/shard_map/place/pallas_call | solution.py:141
  131.6 0.8 place.16
  132.5 1.0 place.17
  133.5 0.8 place.18
  134.3 0.7 place.19
  (39 shorter events, 0.7 us)
Async XLA Ops:
  3.6 5.8 %collective-permute-start.11 = (bf16[4096,128]{1,0:T(8,128)(2,1)}, bf16[4096,128]{1,0:T(8,128)(2,1)S(1)}, u32[]{:S(2)}, u32[]{:S(2)}) collective-permute-start(bf16[4096,128]{1,0:T(8,128)(2,1)} %get-tuple-element.26), channel_id=1, source_target_pairs={{0,4},{4,0},{8,12},{12,8},{16,20},{20,16},{24,28},{28,24},{32,36},... | collective-permute-start | bytes 3145736 | tf_op jit(solution)/shard_map/ppermute | solution.py:30
  6.9 27.7 %collective-permute-start.1 = (bf16[128,2048]{1,0:T(8,128)(2,1)}, bf16[128,2048]{1,0:T(8,128)(2,1)S(1)}, u32[]{:S(2)}, u32[]{:S(2)}) collective-permute-start(bf16[128,2048]{1,0:T(8,128)(2,1)} %refs_2_.1), channel_id=1, source_target_pairs={{0,56},{4,12},{8,0},{12,20},{16,8},{20,28},{24,16},{28,36},{32,24}... | collective-permute-start | bytes 1572872 | tf_op jit(solution)/shard_map/ppermute | solution.py:25
  6.9 27.7 %collective-permute-start.2 = (bf16[128,2048]{1,0:T(8,128)(2,1)}, bf16[128,2048]{1,0:T(8,128)(2,1)S(1)}, u32[]{:S(2)}, u32[]{:S(2)}) collective-permute-start(bf16[128,2048]{1,0:T(8,128)(2,1)} %refs_3_.3), channel_id=1, source_target_pairs={{0,56},{4,12},{8,0},{12,20},{16,8},{20,28},{24,16},{28,36},{32,24}... | collective-permute-start | bytes 1572872 | tf_op jit(solution)/shard_map/ppermute | solution.py:25
  9.4 28.5 %collective-permute-start.12 = (bf16[4096,128]{1,0:T(8,128)(2,1)S(1)}, bf16[4096,128]{1,0:T(8,128)(2,1)}, u32[]{:S(2)}, u32[]{:S(2)}) collective-permute-start(bf16[4096,128]{1,0:T(8,128)(2,1)S(1)} %collective-permute-done.11.refs_0_), channel_id=1, source_target_pairs={{0,56},{4,12},{8,0},{12,20},{16,8},{20,28},{24,16},{28,36},{32,24}... | collective-permute-start | bytes 3145736 | tf_op jit(solution)/shard_map/ppermute | solution.py:25
  10.8 23.7 %collective-permute-start = (bf16[64,128]{1,0:T(8,128)(2,1)S(1)}, bf16[64,128]{1,0:T(8,128)(2,1)S(1)}, u32[]{:S(2)}, u32[]{:S(2)}) collective-permute-start(bf16[64,128]{1,0:T(8,128)(2,1)S(1)} %pad_maximum_fusion), channel_id=1, source_target_pairs={{0,56},{4,12},{8,0},{12,20},{16,8},{20,28},{24,16},{28,36},{32,24}... | collective-permute-start | bytes 49160 | tf_op jit(solution)/shard_map/ppermute | solution.py:25
  34.5 0.9 copy-start
  35.4 0.9 copy-start.1
  37.7 15.0 %collective-permute-start.3 = (bf16[4096,128]{1,0:T(8,128)(2,1)S(1)}, bf16[4096,128]{1,0:T(8,128)(2,1)}, u32[]{:S(2)}, u32[]{:S(2)}) collective-permute-start(bf16[4096,128]{1,0:T(8,128)(2,1)S(1)} %mix.2.refs_1_), channel_id=1, source_target_pairs={{0,56},{4,12},{8,0},{12,20},{16,8},{20,28},{24,16},{28,36},{32,24}... | collective-permute-start | bytes 3145736 | tf_op jit(solution)/shard_map/ppermute | solution.py:25
  37.8 26.2 %collective-permute-start.13 = (bf16[4096,128]{1,0:T(8,128)(2,1)}, bf16[4096,128]{1,0:T(8,128)(2,1)}, u32[]{:S(2)}, u32[]{:S(2)}) collective-permute-start(bf16[4096,128]{1,0:T(8,128)(2,1)} %collective-permute-done.12.refs_0_), channel_id=1, source_target_pairs={{0,56},{4,12},{8,0},{12,20},{16,8},{20,28},{24,16},{28,36},{32,24}... | collective-permute-start | bytes 3145736 | tf_op jit(solution)/shard_map/ppermute | solution.py:25
  52.8 46.2 %collective-permute-start.4 = (bf16[4096,128]{1,0:T(8,128)(2,1)}, bf16[4096,128]{1,0:T(8,128)(2,1)S(1)}, u32[]{:S(2)}, u32[]{:S(2)}) collective-permute-start(bf16[4096,128]{1,0:T(8,128)(2,1)} %collective-permute-done.3.refs_0_), channel_id=1, source_target_pairs={{0,56},{4,12},{8,0},{12,20},{16,8},{20,28},{24,16},{28,36},{32,24}... | collective-permute-start | bytes 3145736 | tf_op jit(solution)/shard_map/ppermute | solution.py:25
  53.6 46.8 %collective-permute-start.20 = (bf16[4096,128]{1,0:T(8,128)(2,1)S(1)}, bf16[4096,128]{1,0:T(8,128)(2,1)S(1)}, u32[]{:S(2)}, u32[]{:S(2)}) collective-permute-start(bf16[4096,128]{1,0:T(8,128)(2,1)S(1)} %mix.2.refs_1_), channel_id=1, source_target_pairs={{0,4},{4,0},{8,12},{12,8},{16,20},{20,16},{24,28},{28,24},{32,36},... | collective-permute-start | bytes 3145736 | tf_op jit(solution)/shard_map/ppermute | solution.py:30
  58.9 41.5 %collective-permute-start.18 = (bf16[4096,128]{1,0:T(8,128)(2,1)}, bf16[4096,128]{1,0:T(8,128)(2,1)S(1)}, u32[]{:S(2)}, u32[]{:S(2)}) collective-permute-start(bf16[4096,128]{1,0:T(8,128)(2,1)} %collective-permute-done.3.refs_0_), channel_id=1, source_target_pairs={{0,4},{4,0},{8,12},{12,8},{16,20},{20,16},{24,28},{28,24},{32,36},... | collective-permute-start | bytes 3145736 | tf_op jit(solution)/shard_map/ppermute | solution.py:30
  64.0 44.3 %collective-permute-start.14 = (bf16[4096,128]{1,0:T(8,128)(2,1)}, bf16[4096,128]{1,0:T(8,128)(2,1)S(1)}, u32[]{:S(2)}, u32[]{:S(2)}) collective-permute-start(bf16[4096,128]{1,0:T(8,128)(2,1)} %collective-permute-done.13.refs_0_), channel_id=1, source_target_pairs={{0,56},{4,12},{8,0},{12,20},{16,8},{20,28},{24,16},{28,36},{32,24}... | collective-permute-start | bytes 3145736 | tf_op jit(solution)/shard_map/ppermute | solution.py:25
  64.1 2.8 %collective-permute-start.21 = (bf16[16,128]{1,0:T(8,128)(2,1)S(1)}, bf16[16,128]{1,0:T(8,128)(2,1)S(1)}, u32[]{:S(2)}, u32[]{:S(2)}) collective-permute-start(bf16[16,128]{1,0:T(8,128)(2,1)S(1)} %fusion.1), channel_id=1, source_target_pairs={{0,1},{1,0},{2,3},{3,2},{4,5},{5,4},{6,7},{7,6},{8,9},{9,8},{10,11... | collective-permute-start | bytes 12296 | tf_op jit(solution)/shard_map/ppermute | solution.py:20
  67.0 4.0 %collective-permute-start.22 = (bf16[16,128]{1,0:T(8,128)(2,1)S(1)}, bf16[16,128]{1,0:T(8,128)(2,1)S(1)}, u32[]{:S(2)}, u32[]{:S(2)}) collective-permute-start(bf16[16,128]{1,0:T(8,128)(2,1)S(1)} %fusion.2), channel_id=1, source_target_pairs={{0,2},{1,3},{2,0},{3,1},{4,6},{5,7},{6,4},{7,5},{8,10},{9,11},{10,... | collective-permute-start | bytes 12296 | tf_op jit(solution)/shard_map/ppermute | solution.py:20
  71.0 12.4 %collective-permute-start.23 = (bf16[16,128]{1,0:T(8,128)(2,1)S(1)}, bf16[16,128]{1,0:T(8,128)(2,1)S(1)}, u32[]{:S(2)}, u32[]{:S(2)}) collective-permute-start(bf16[16,128]{1,0:T(8,128)(2,1)S(1)} %fusion.3), channel_id=1, source_target_pairs={{0,8},{4,12},{8,0},{12,4},{16,24},{20,28},{24,16},{28,20},{32,40},... | collective-permute-start | bytes 12296 | tf_op jit(solution)/shard_map/ppermute | solution.py:20
  83.4 3.4 %collective-permute-start.24 = (bf16[16,128]{1,0:T(8,128)(2,1)S(1)}, bf16[16,128]{1,0:T(8,128)(2,1)S(1)}, u32[]{:S(2)}, u32[]{:S(2)}) collective-permute-start(bf16[16,128]{1,0:T(8,128)(2,1)S(1)} %add.26), channel_id=1, source_target_pairs={{0,16},{4,20},{8,24},{12,28},{16,0},{20,4},{24,8},{28,12},{32,48},... | collective-permute-start | bytes 12296 | tf_op jit(solution)/shard_map/ppermute | solution.py:20
  86.8 6.4 %collective-permute-start.25 = (bf16[16,128]{1,0:T(8,128)(2,1)S(1)}, bf16[16,128]{1,0:T(8,128)(2,1)S(1)}, u32[]{:S(2)}, u32[]{:S(2)}) collective-permute-start(bf16[16,128]{1,0:T(8,128)(2,1)S(1)} %add.27), channel_id=1, source_target_pairs={{0,32},{4,36},{8,40},{12,44},{16,48},{20,52},{24,56},{28,60},{32,0... | collective-permute-start | bytes 12296 | tf_op jit(solution)/shard_map/ppermute | solution.py:20
  93.2 6.6 %collective-permute-start.26 = (bf16[16,128]{1,0:T(8,128)(2,1)S(1)}, bf16[16,128]{1,0:T(8,128)(2,1)S(1)}, u32[]{:S(2)}, u32[]{:S(2)}) collective-permute-start(bf16[16,128]{1,0:T(8,128)(2,1)S(1)} %add.28), channel_id=1, source_target_pairs={{0,4},{4,0},{8,12},{12,8},{16,20},{20,16},{24,28},{28,24},{32,36},... | collective-permute-start | bytes 12296 | tf_op jit(solution)/shard_map/ppermute | solution.py:20
  99.0 9.9 %collective-permute-start.7 = (bf16[1536,128]{1,0:T(8,128)(2,1)S(1)}, bf16[1536,128]{1,0:T(8,128)(2,1)S(1)}, u32[]{:S(2)}, u32[]{:S(2)}) collective-permute-start(bf16[1536,128]{1,0:T(8,128)(2,1)S(1)} %slice.13), channel_id=1, source_target_pairs={{0,56},{4,12},{8,0},{12,20},{16,8},{20,28},{24,16},{28,36},{32,24}... | collective-permute-start | bytes 1179656 | tf_op jit(solution)/shard_map/ppermute | solution.py:25
  99.8 18.4 %collective-permute-start.19 = (bf16[4096,128]{1,0:T(8,128)(2,1)}, bf16[4096,128]{1,0:T(8,128)(2,1)S(1)}, u32[]{:S(2)}, u32[]{:S(2)}) collective-permute-start(bf16[4096,128]{1,0:T(8,128)(2,1)} %collective-permute-done.12.refs_0_), channel_id=1, source_target_pairs={{0,4},{4,0},{8,12},{12,8},{16,20},{20,16},{24,28},{28,24},{32,36},... | collective-permute-start | bytes 3145736 | tf_op jit(solution)/shard_map/ppermute | solution.py:30
  100.4 18.3 %collective-permute-start.17 = (bf16[4096,128]{1,0:T(8,128)(2,1)}, bf16[4096,128]{1,0:T(8,128)(2,1)S(1)}, u32[]{:S(2)}, u32[]{:S(2)}) collective-permute-start(bf16[4096,128]{1,0:T(8,128)(2,1)} %collective-permute-done.13.refs_0_), channel_id=1, source_target_pairs={{0,4},{4,0},{8,12},{12,8},{16,20},{20,16},{24,28},{28,24},{32,36},... | collective-permute-start | bytes 3145736 | tf_op jit(solution)/shard_map/ppermute | solution.py:30
  100.5 7.8 %collective-permute-start.5 = (bf16[512,128]{1,0:T(8,128)(2,1)S(1)}, bf16[512,128]{1,0:T(8,128)(2,1)S(1)}, u32[]{:S(2)}, u32[]{:S(2)}) collective-permute-start(bf16[512,128]{1,0:T(8,128)(2,1)S(1)} %slice.12), channel_id=1, source_target_pairs={{0,56},{4,12},{8,0},{12,20},{16,8},{20,28},{24,16},{28,36},{32,24}... | collective-permute-start | bytes 393224 | tf_op jit(solution)/shard_map/ppermute | solution.py:25
  108.3 20.5 %collective-permute-start.16 = (bf16[4096,128]{1,0:T(8,128)(2,1)S(1)}, bf16[4096,128]{1,0:T(8,128)(2,1)S(1)}, u32[]{:S(2)}, u32[]{:S(2)}) collective-permute-start(bf16[4096,128]{1,0:T(8,128)(2,1)S(1)} %collective-permute-done.4.refs_0_), channel_id=1, source_target_pairs={{0,4},{4,0},{8,12},{12,8},{16,20},{20,16},{24,28},{28,24},{32,36},... | collective-permute-start | bytes 3145736 | tf_op jit(solution)/shard_map/ppermute | solution.py:30
  108.3 21.9 %collective-permute-start.15 = (bf16[4096,128]{1,0:T(8,128)(2,1)S(1)}, bf16[4096,128]{1,0:T(8,128)(2,1)S(1)}, u32[]{:S(2)}, u32[]{:S(2)}) collective-permute-start(bf16[4096,128]{1,0:T(8,128)(2,1)S(1)} %collective-permute-done.14.refs_0_), channel_id=1, source_target_pairs={{0,4},{4,0},{8,12},{12,8},{16,20},{20,16},{24,28},{28,24},{32,36},... | collective-permute-start | bytes 3145736 | tf_op jit(solution)/shard_map/ppermute | solution.py:30
  108.9 9.3 %collective-permute-start.9 = (bf16[2048,128]{1,0:T(8,128)(2,1)S(1)}, bf16[2048,128]{1,0:T(8,128)(2,1)S(1)}, u32[]{:S(2)}, u32[]{:S(2)}) collective-permute-start(bf16[2048,128]{1,0:T(8,128)(2,1)S(1)} %slice.14), channel_id=1, source_target_pairs={{0,56},{4,12},{8,0},{12,20},{16,8},{20,28},{24,16},{28,36},{32,24}... | collective-permute-start | bytes 1572872 | tf_op jit(solution)/shard_map/ppermute | solution.py:25
  118.2 14.3 %collective-permute-start.10 = (bf16[2048,128]{1,0:T(8,128)(2,1)S(1)}, bf16[2048,128]{1,0:T(8,128)(2,1)S(1)}, u32[]{:S(2)}, u32[]{:S(2)}) collective-permute-start(bf16[2048,128]{1,0:T(8,128)(2,1)S(1)} %collective-permute-done.9.refs_0_), channel_id=1, source_target_pairs={{0,4},{4,0},{8,12},{12,8},{16,20},{20,16},{24,28},{28,24},{32,36},... | collective-permute-start | bytes 1572872 | tf_op jit(solution)/shard_map/ppermute | solution.py:30
  118.2 15.3 %collective-permute-start.8 = (bf16[1536,128]{1,0:T(8,128)(2,1)S(1)}, bf16[1536,128]{1,0:T(8,128)(2,1)S(1)}, u32[]{:S(2)}, u32[]{:S(2)}) collective-permute-start(bf16[1536,128]{1,0:T(8,128)(2,1)S(1)} %collective-permute-done.7.refs_1_), channel_id=1, source_target_pairs={{0,4},{4,0},{8,12},{12,8},{16,20},{20,16},{24,28},{28,24},{32,36},... | collective-permute-start | bytes 1179656 | tf_op jit(solution)/shard_map/ppermute | solution.py:30
  118.7 15.6 %collective-permute-start.6 = (bf16[512,128]{1,0:T(8,128)(2,1)S(1)}, bf16[512,128]{1,0:T(8,128)(2,1)S(1)}, u32[]{:S(2)}, u32[]{:S(2)}) collective-permute-start(bf16[512,128]{1,0:T(8,128)(2,1)S(1)} %collective-permute-done.5.refs_1_), channel_id=1, source_target_pairs={{0,4},{4,0},{8,12},{12,8},{16,20},{20,16},{24,28},{28,24},{32,36},... | collective-permute-start | bytes 393224 | tf_op jit(solution)/shard_map/ppermute | solution.py:30
